TPU v7x, 128 devices: a whole 4x4x4 slice. The times are simulated.
128 devices in a mesh: scene: 16 (over y, z), image: 8 (over x, core).
Axes of the slice: x: 4, y: 4, z: 4, core: 2. Of those that a mesh axis runs over, the one named last changes fastest.
Arguments:
- jacobian: bfloat16 [1024, 256, 1152], P(('scene', 'image')), may hold values from -0.1875 to 0.1875
- splat_ids: int32 [1024, 128], P(('scene', 'image')), may hold values from 0 to 16383, as said below
- pix_residual: bfloat16 [1024, 256], P(('scene', 'image')), may hold values from -6 to 6
- live_blocks: int32 [128], replicated, may hold values from 1 to 8, as said below
- proj_jac: bfloat16 [9, 59, 16384], P(None, None, 'scene'), may hold values from -0.75 to 0.75
- damping: float32 [59, 16384], P(None, 'scene'), may hold values from 0.1 to 1
- precond: float32 [59, 16384], P(None, 'scene'), may hold values from 0.3 to 9
Outputs:
- solution: float32 [59, 16384], P(None, 'scene')
- residual: float32 [59, 16384], P(None, 'scene')
Inputs may be any that keep to these rules, and one draw needn't show every extreme that they name: live_blocks[d] counts the blocks in use on device d = scene index * 8 + image index; they are its slots 0 to live_blocks[d] - 1; some device uses all 8 while the device whose index differs from it in the lowest bit uses at most half of them. `splat_ids`: splat s of every block names a Gaussian of scene index s // 8, that is an id from that index times 1024 to the next such multiple.
All inputs are finite; a program needn't handle non-finite values.
Results may differ from a plain program's by a relative error of at most 0.0051.
Values may be sent and summed in bfloat16 or wider, within the bound.
No kernel may reach another device: no remote copies, remote signals or barrier semaphores. Data moves between devices by JAX's collectives and lax.ppermute only.
A program may use at most 64 MiB of HBM per device.

v0:
```python
import jax
import jax.numpy as jnp
from jax import lax
from jax.sharding import Mesh
from jax.sharding import PartitionSpec as P

ITERS = 2
SCENE = ("scene_0", "scene_1")
SCENE_IMAGE = ("scene_0", "scene_1", "image")


def gathered_total(value, axis):
    return lax.all_gather(value, axis).sum(0)


def by_axis(value, axes):
    for axis in axes:
        value = lax.psum(value, axis)
    return value


def project(proj_jac, field):
    return jnp.einsum(
        "kag,ag->kg", proj_jac.astype(jnp.float32), field, precision=lax.Precision.HIGHEST
    ).astype(jnp.bfloat16)


def lift(proj_jac, weights):
    return jnp.einsum(
        "kag,kg->ag", proj_jac.astype(jnp.float32), weights, precision=lax.Precision.HIGHEST
    )


def run_blocks(jac_set, pixel_set, first_pos, last_pos, picker, keeper, initial):

    def advance(position, running):
        jac_block = lax.dynamic_index_in_dim(jac_set, position, 0, keepdims=False)
        if picker is None:
            signal = lax.dynamic_index_in_dim(pixel_set, position, 0, keepdims=False)
        else:
            signal = jnp.dot(
                jac_block, picker(position), preferred_element_type=jnp.float32
            ).astype(jnp.bfloat16)
        returned = jnp.dot(signal, jac_block, preferred_element_type=jnp.float32)
        return keeper(running, position, returned)

    return lax.fori_loop(first_pos, last_pos, advance, initial)


def local(jacobian, splat_ids, pix_residual, live_blocks, proj_jac, damping, precond):
    g_dev = damping.shape[1]
    n_proj = proj_jac.shape[0]
    n_scene = lax.axis_size(SCENE)
    owner_width = splat_ids.shape[1] // n_scene
    scene_pos = lax.axis_index(SCENE)
    device_pos = scene_pos * lax.axis_size("image") + lax.axis_index("image")
    own_live = live_blocks[device_pos]
    block_sets = [(jacobian, splat_ids, pix_residual, 0, own_live)]
    offsets = []
    total_slots = 0
    member = block_sets[0]
    offsets.append(total_slots)
    total_slots += member[0].shape[0]
    ids_all = jnp.concatenate([member[1] for member in block_sets], axis=0)
    routed_ids = lax.all_to_all(
        ids_all.reshape(total_slots, n_scene, owner_width),
        SCENE,
        split_axis=1,
        concat_axis=1,
        tiled=True,
    )
    local_ids = routed_ids - scene_pos * g_dev

    def back_project(source):
        buffer = jnp.zeros((total_slots, n_proj, n_scene, owner_width), jnp.float32)
        for index_set, (jac_set, id_set, pixel_set, first_pos, last_pos) in enumerate(block_sets):
            slot_base = offsets[index_set]

            def keeper(running, position, returned):
                shaped = returned.reshape(n_proj, n_scene, owner_width)
                return lax.dynamic_update_index_in_dim(running, shaped, slot_base + position, 0)

            picker = (
                None
                if source is None
                else lambda position: lax.dynamic_index_in_dim(
                    source, slot_base + position, 0, keepdims=False
                )
            )
            buffer = run_blocks(jac_set, pixel_set, first_pos, last_pos, picker, keeper, buffer)
        arrived = lax.all_to_all(buffer, SCENE, split_axis=2, concat_axis=2, tiled=True)
        arrivals = jnp.moveaxis(arrived, 1, 0).reshape(n_proj, -1)
        partial_sum = (
            jnp.zeros((n_proj, g_dev), jnp.float32).at[:, local_ids.reshape(-1)].add(arrivals)
        )
        return gathered_total(partial_sum, "image")

    def norm_dot(residual, precon_res):
        return by_axis(jnp.sum(residual * precon_res), SCENE)

    residual = -lift(proj_jac, back_project(None))
    solution = jnp.zeros_like(residual)
    precon_res = precond * residual
    direction = precon_res
    rz_now = norm_dot(residual, precon_res)
    for iteration in range(ITERS):
        local_proj = project(proj_jac, direction)
        picked = jnp.moveaxis(jnp.take(local_proj, local_ids, axis=1), 0, 1)
        fetched = lax.all_to_all(picked, SCENE, split_axis=2, concat_axis=2, tiled=True).reshape(
            total_slots, -1
        )
        image = lift(proj_jac, back_project(fetched)) + damping * direction
        alpha = rz_now / by_axis(jnp.sum(direction * image), SCENE)
        solution = solution + alpha * direction
        residual = residual - alpha * image
        precon_res = precond * residual
        rz_next = norm_dot(residual, precon_res)
        direction = precon_res + rz_next / rz_now * direction
        rz_now = rz_next
    return (solution, residual)


def solution(mesh):
    finer = Mesh(mesh.devices.reshape(4, 4, mesh.shape["image"]), ("scene_0", "scene_1", "image"))
    in_specs = (
        P(SCENE_IMAGE, None, None),
        P(SCENE_IMAGE, None),
        P(SCENE_IMAGE, None),
        P(),
        P(None, None, SCENE),
        P(None, SCENE),
        P(None, SCENE),
    )
    out_specs = (P(None, SCENE), P(None, SCENE))
    return jax.shard_map(local, mesh=finer, in_specs=in_specs, out_specs=out_specs, check_vma=False)
```

profile of v0, /device:TPU:1, one launch (start us, length us, event | category | flops | bytes accessed | tf_op | source)
XLA Modules:
  0.0 329.3 jit_solution(16440324529232248904)
XLA Ops:
  2.1 8.6 %all-to-all-start = ((s32[8,16,8]{2,0,1:T(8,128)}), s32[8,16,8]{2,0,1:T(8,128)S(1)}, u32[]{:S(2)}, u32[]{:S(2)}) async-start(s32[8,16,8]{2,0,1:T(8,128)} %copy.48), calls=%async_computation | async-start | bytes 131072 | tf_op jit(solution)/shard_map/all_to_all | solution.py:65
  10.7 6.6 %copy.50 = bf16[8,256,1152]{1,2,0:T(8,128)(2,1)} copy(bf16[8,256,1152]{2,1,0:T(8,128)(2,1)} %param.15) | data formatting | bytes 9437184 | tf_op jit(solution)/shard_map/while | solution.py:47
  18.0 16.5 %while.30 = (s32[]{:T(128)}, f32[8,9,16,8]{2,3,1,0:T(8,128)S(1)}, s32[]{:T(128)}, bf16[8,256]{1,0:T(8,128)(2,1)}, bf16[8,256,1152]{1,2,0:T(8,128)(2,1)}, /*index=5*/s32[]{:T(128)}, s32[]{:T(128)}, s32[]{:T(128)}) while((s32[]{:T(128)}, f32[8,9,16,8]{2,3,1,0:T(8,128)S(1)}, s32[]{:T(128)}, bf16[8,256]{1,0:T(8,128)(2,1)}, ...), condition=%wide.region_1.2_spmd, body=%wide.region_0.1_spmd.sunk | while | flops 589829 | bytes 1858187 | solution.py:47
  36.1 20.1 %all-to-all-start.1 = ((f32[16,1,576]{2,1,0:T(1,128)}), f32[16,1,576]{2,1,0:T(1,128)S(1)}, u32[]{:S(2)}, u32[]{:S(2)}) async-start(f32[16,1,576]{2,1,0:T(1,128)} %reshape.184), calls=%async_computation.1 | async-start | bytes 81920 | tf_op jit(solution)/shard_map/all_to_all | solution.py:91
  56.5 6.2 %all-to-all-done.1 = f32[16,1,576]{2,1,0:T(1,128)S(1)} async-done(((f32[16,1,576]{2,1,0:T(1,128)}), f32[16,1,576]{2,1,0:T(1,128)S(1)}, u32[]{:S(2)}, u32[]{:S(2)}) %all-to-all-start.1) | async-done | bytes 36896 | tf_op jit(solution)/shard_map/all_to_all | solution.py:91
  66.1 6.2 %scatter_custom_fusion = f32[9,1024]{0,1:T(8,128)S(1)} fusion(s32[1024]{0:T(1024)S(1)} %bitcast.196, f32[1024,9]{1,0:T(8,128)S(1)} %copy.53, f32[]{:T(128)} %constant.67.clone.1), kind=kCustom, calls=%fused_computation.61 | custom fusion | flops 9216 | bytes 36868 | tf_op jit(solution)/shard_map/scatter-add | solution.py:94
  72.4 18.1 %all-gather.3 = f32[8,9,1024]{2,1,0:T(8,128)S(1)} all-gather(f32[1,9,1024]{2,1,0:T(8,128)S(1)} %copy.54), channel_id=2, replica_groups=mesh['scene_0'=4,'scene_1'=4,'image'=8] {'image'}, dimensions={0}, use_global_device_ids=true | all-gather | bytes 331776 | tf_op jit(solution)/shard_map/all_gather | solution.py:13
  95.8 3.5 %all-to-all-start.2 = ((bf16[16,2,288]{2,1,0:T(2,128)(2,1)}), bf16[16,2,288]{2,1,0:T(2,128)(2,1)S(1)}, u32[]{:S(2)}, u32[]{:S(2)}) async-start(bf16[16,2,288]{2,1,0:T(2,128)(2,1)} %reshape.186), calls=%async_computation.2 | async-start | bytes 49152 | tf_op jit(solution)/shard_map/all_to_all | solution.py:109
  99.3 6.4 %all-to-all-done.2 = bf16[16,2,288]{2,1,0:T(2,128)(2,1)S(1)} async-done(((bf16[16,2,288]{2,1,0:T(2,128)(2,1)}), bf16[16,2,288]{2,1,0:T(2,128)(2,1)S(1)}, u32[]{:S(2)}, u32[]{:S(2)}) %all-to-all-start.2) | async-done | bytes 18464 | tf_op jit(solution)/shard_map/all_to_all | solution.py:109
  107.5 18.9 %while.31 = (s32[]{:T(128)}, f32[8,9,16,8]{2,3,1,0:T(8,128)S(1)}, s32[]{:T(128)}, bf16[8,256,1152]{1,2,0:T(8,128)(2,1)}, bf16[8,1152]{1,0:T(8,128)(2,1)S(1)}, /*index=5*/s32[]{:T(128)}, s32[]{:T(128)}, s32[]{:T(128)}) while((s32[]{:T(128)}, f32[8,9,16,8]{2,3,1,0:T(8,128)S(1)}, s32[]{:T(128)}, bf16[8,256,1152]{1,2,0:T(8,128)(2,1)}, ...), condition=%wide.region_8.10_spmd, body=%wide.region_7.9_spmd.sunk | while | flops 1179909 | bytes 2456711 | solution.py:47
  127.5 27.1 %all_to_all.30 = f32[16,1,576]{2,1,0:T(1,128)S(1)} all-to-all(f32[16,1,576]{2,1,0:T(1,128)S(1)} %reshape.188), channel_id=1, replica_groups=mesh['scene_0'=4,'scene_1'=4,'image'=8] {'scene_0','scene_1'}, dimensions={0} | all-to-all | bytes 73728 | tf_op jit(solution)/shard_map/all_to_all | solution.py:91
  157.4 6.1 %scatter_custom_fusion.1 = f32[9,1024]{0,1:T(8,128)S(1)} fusion(s32[1024]{0:T(1024)S(1)} %bitcast.197, f32[1024,9]{1,0:T(8,128)S(1)} %copy.62, f32[]{:T(128)} %constant.67.clone.1), kind=kCustom, calls=%fused_computation.59 | custom fusion | flops 9216 | bytes 36868 | tf_op jit(solution)/shard_map/scatter-add | solution.py:94
  163.7 15.7 %all-gather.4 = f32[8,9,1024]{2,1,0:T(8,128)S(1)} all-gather(f32[1,9,1024]{2,1,0:T(8,128)S(1)} %copy.63), channel_id=3, replica_groups=mesh['scene_0'=4,'scene_1'=4,'image'=8] {'image'}, dimensions={0}, use_global_device_ids=true | all-gather | bytes 331776 | tf_op jit(solution)/shard_map/all_gather | solution.py:13
  180.5 7.5 %all-reduce.1 = (f32[]{:T(128)}, f32[]{:T(128)}) all-reduce(f32[]{:T(128)} %get-tuple-element.136, f32[]{:T(128)} %get-tuple-element.135), channel_id=1, replica_groups=mesh['scene_0'=4,'scene_1'=4,'image'=8] {'scene_0'}, use_global_device_ids=true, to_apply=%region_5.6 | all-reduce | flops 2 | bytes 16 | tf_op jit(solution)/shard_map/psum | solution.py:18
  188.0 7.5 %all-reduce = (f32[]{:T(128)}, f32[]{:T(128)}) all-reduce(f32[]{:T(128)} %get-tuple-element.169, f32[]{:T(128)} %get-tuple-element.170), channel_id=1, replica_groups=mesh['scene_0'=4,'scene_1'=4,'image'=8] {'scene_1'}, use_global_device_ids=true, to_apply=%region_6.7 | all-reduce | flops 2 | bytes 16 | tf_op jit(solution)/shard_map/psum | solution.py:18
  198.2 7.6 %psum.60 = f32[]{:T(128)} all-reduce(f32[]{:T(128)} %get-tuple-element.171), channel_id=1, replica_groups=mesh['scene_0'=4,'scene_1'=4,'image'=8] {'scene_0'}, use_global_device_ids=true, to_apply=%region_15.17 | all-reduce | flops 1 | bytes 8 | tf_op jit(solution)/shard_map/psum | solution.py:18
  205.8 7.2 %psum.61 = f32[]{:T(128)} all-reduce(f32[]{:T(128)} %psum.60), channel_id=1, replica_groups=mesh['scene_0'=4,'scene_1'=4,'image'=8] {'scene_1'}, use_global_device_ids=true, to_apply=%region_16.18 | all-reduce | flops 1 | bytes 8 | tf_op jit(solution)/shard_map/psum | solution.py:18
  222.8 6.4 %all-to-all-done.4 = bf16[16,2,288]{2,1,0:T(2,128)(2,1)S(1)} async-done(((bf16[16,2,288]{2,1,0:T(2,128)(2,1)}), bf16[16,2,288]{2,1,0:T(2,128)(2,1)S(1)}, u32[]{:S(2)}, u32[]{:S(2)}) %all-to-all-start.4) | async-done | bytes 18464 | tf_op jit(solution)/shard_map/all_to_all | solution.py:109
  231.0 18.9 %while.32 = (s32[]{:T(128)}, f32[8,9,16,8]{2,3,1,0:T(8,128)S(1)}, s32[]{:T(128)}, bf16[8,256,1152]{1,2,0:T(8,128)(2,1)}, bf16[8,1152]{1,0:T(8,128)(2,1)S(1)}, /*index=5*/s32[]{:T(128)}, s32[]{:T(128)}, s32[]{:T(128)}) while((s32[]{:T(128)}, f32[8,9,16,8]{2,3,1,0:T(8,128)S(1)}, s32[]{:T(128)}, bf16[8,256,1152]{1,2,0:T(8,128)(2,1)}, ...), condition=%wide.region_18.20_spmd, body=%wide.region_17.19_spmd.sunk | while | flops 1179909 | bytes 2456711 | solution.py:47
  251.0 26.9 %all_to_all.31 = f32[16,1,576]{2,1,0:T(1,128)S(1)} all-to-all(f32[16,1,576]{2,1,0:T(1,128)S(1)} %reshape.192), channel_id=1, replica_groups=mesh['scene_0'=4,'scene_1'=4,'image'=8] {'scene_0','scene_1'}, dimensions={0} | all-to-all | bytes 73728 | tf_op jit(solution)/shard_map/all_to_all | solution.py:91
  280.7 6.1 %scatter_custom_fusion.2 = f32[9,1024]{0,1:T(8,128)S(1)} fusion(s32[1024]{0:T(1024)S(1)} %bitcast.198, f32[1024,9]{1,0:T(8,128)S(1)} %copy.71, f32[]{:T(128)} %constant.67.clone.1), kind=kCustom, calls=%fused_computation.57 | custom fusion | flops 9216 | bytes 36868 | tf_op jit(solution)/shard_map/scatter-add | solution.py:94
  287.0 24.1 %all-gather.5 = f32[8,9,1024]{2,1,0:T(8,128)S(1)} all-gather(f32[1,9,1024]{2,1,0:T(8,128)S(1)} %copy.72), channel_id=4, replica_groups=mesh['scene_0'=4,'scene_1'=4,'image'=8] {'image'}, dimensions={0}, use_global_device_ids=true | all-gather | bytes 331776 | tf_op jit(solution)/shard_map/all_gather | solution.py:13
  312.1 7.5 %psum.62 = f32[]{:T(128)} all-reduce(f32[]{:T(128)} %multiply_reduce_fusion), channel_id=1, replica_groups=mesh['scene_0'=4,'scene_1'=4,'image'=8] {'scene_0'}, use_global_device_ids=true, to_apply=%region_22.24 | all-reduce | flops 1 | bytes 8 | tf_op jit(solution)/shard_map/psum | solution.py:18
  319.5 7.5 %psum.63 = f32[]{:T(128)} all-reduce(f32[]{:T(128)} %psum.62), channel_id=1, replica_groups=mesh['scene_0'=4,'scene_1'=4,'image'=8] {'scene_1'}, use_global_device_ids=true, to_apply=%region_23.25 | all-reduce | flops 1 | bytes 8 | tf_op jit(solution)/shard_map/psum | solution.py:18
  (160 shorter events, 81.2 us)
Async XLA Ops:
  2.1 34.1 %all-to-all-start = ((s32[8,16,8]{2,0,1:T(8,128)}), s32[8,16,8]{2,0,1:T(8,128)S(1)}, u32[]{:S(2)}, u32[]{:S(2)}) async-start(s32[8,16,8]{2,0,1:T(8,128)} %copy.48), calls=%async_computation | async-start | bytes 131072 | tf_op jit(solution)/shard_map/all_to_all | solution.py:65
  10.7 6.7 %copy-start.7 = (s32[128]{0:T(128)S(1)}, s32[128]{0:T(128)}, u32[]{:S(2)}) copy-start(s32[128]{0:T(128)} %param.18) | copy-start | bytes 1540
  36.1 26.6 %all-to-all-start.1 = ((f32[16,1,576]{2,1,0:T(1,128)}), f32[16,1,576]{2,1,0:T(1,128)S(1)}, u32[]{:S(2)}, u32[]{:S(2)}) async-start(f32[16,1,576]{2,1,0:T(1,128)} %reshape.184), calls=%async_computation.1 | async-start | bytes 81920 | tf_op jit(solution)/shard_map/all_to_all | solution.py:91
  56.3 38.3 %copy-start.5 = (pred[8,16,8]{2,0,1:T(8,128)(4,1)}, pred[8,16,8]{2,0,1:T(8,128)(4,1)S(1)}, u32[]{:S(2)}) copy-start(pred[8,16,8]{2,0,1:T(8,128)(4,1)S(1)} %get-tuple-element.174) | copy-start | bytes 3076
  64.6 25.9 %copy-start = (bf16[9,59,1024]{2,1,0:T(8,128)(2,1)S(1)}, bf16[9,59,1024]{2,1,0:T(8,128)(2,1)}, u32[]{:S(2)}) copy-start(bf16[9,59,1024]{2,1,0:T(8,128)(2,1)} %param.19) | copy-start | bytes 3262468
  65.8 25.0 %copy-start.2 = (f32[59,1024]{1,0:T(8,128)S(1)}, f32[59,1024]{1,0:T(8,128)}, u32[]{:S(2)}) copy-start(f32[59,1024]{1,0:T(8,128)} %param.21) | copy-start | bytes 724996
  95.8 9.9 %all-to-all-start.2 = ((bf16[16,2,288]{2,1,0:T(2,128)(2,1)}), bf16[16,2,288]{2,1,0:T(2,128)(2,1)S(1)}, u32[]{:S(2)}, u32[]{:S(2)}) async-start(bf16[16,2,288]{2,1,0:T(2,128)(2,1)} %reshape.186), calls=%async_computation.2 | async-start | bytes 49152 | tf_op jit(solution)/shard_map/all_to_all | solution.py:109
  157.2 22.6 %copy-start.1 = (f32[59,1024]{1,0:T(8,128)S(1)}, f32[59,1024]{1,0:T(8,128)}, u32[]{:S(2)}) copy-start(f32[59,1024]{1,0:T(8,128)} %param.20) | copy-start | bytes 724996
  157.4 39.4 %copy-start.3 = (f32[59,1024]{1,0:T(8,128)S(1)}, f32[59,1024]{1,0:T(8,128)}, u32[]{:S(2)}) copy-start(f32[59,1024]{1,0:T(8,128)} %param.21) | copy-start | bytes 724996
  214.3 3.8 %copy-start.6 = (pred[8,16,8]{2,0,1:T(8,128)(4,1)S(1)}, pred[8,16,8]{2,0,1:T(8,128)(4,1)}, u32[]{:S(2)}) copy-start(pred[8,16,8]{2,0,1:T(8,128)(4,1)} %copy-done.5) | copy-start | bytes 3076
  219.3 9.9 %all-to-all-start.4 = ((bf16[16,2,288]{2,1,0:T(2,128)(2,1)}), bf16[16,2,288]{2,1,0:T(2,128)(2,1)S(1)}, u32[]{:S(2)}, u32[]{:S(2)}) async-start(bf16[16,2,288]{2,1,0:T(2,128)(2,1)} %reshape.190), calls=%async_computation.4 | async-start | bytes 49152 | tf_op jit(solution)/shard_map/all_to_all | solution.py:109
  280.6 47.7 %copy-start.4 = (f32[59,1024]{1,0:T(8,128)S(1)}, f32[59,1024]{1,0:T(8,128)}, u32[]{:S(2)}) copy-start(f32[59,1024]{1,0:T(8,128)} %get-tuple-element.173) | copy-start | bytes 724996
where the time goes:
time: 336 us; the launch traced here: 329 us
  blocking collectives  157 us (47%)
  local copies, waits for them, and re-layouts  46.9 us (14%)
  starting transfers between devices  35.7 us (11%)
  matrix products  29.3 us (9%)
  other arithmetic  26.6 us (8%)
  waiting for transfers between devices  19 us (6%)
  loops' own time  10.1 us (3%)
  between operations  5.13 us (2%)
    all_gather x3, blocking collectives, gathered_total(): return lax.all_gather(value, axis).sum(0)  57.9 us
    all_to_all x2, blocking collectives, back_project(): lax.all_to_all(buffer, SCENE, split_axis=2, concat_axis=2, tiled=True)  54 us
    psum x6, blocking collectives, by_axis(): value = lax.psum(value, axis)  44.7 us
    all_to_all x1, starting transfers between devices, back_project(): lax.all_to_all(buffer, SCENE, split_axis=2, concat_axis=2, tiled=True)  20.1 us
    dot_general x12, matrix products, advance(): returned = jnp.dot(signal, jac_block, preferred_element_type=jnp.float32)  19.4 us
    scatter-add x3, other arithmetic, back_project(): jnp.zeros((n_proj, g_dev), jnp.float32).at[:, local_ids.reshape(-1)]  18.4 us
    dynamic_slice x12, local copies, waits for them, and re-layouts, advance(): jac_block = lax.dynamic_index_in_dim(jac_set, position, 0, keepdims=False)  13.3 us
    all_to_all x2, waiting for transfers between devices, local(): lax.all_to_all(picked, SCENE, split_axis=2, concat_axis=2, tiled=True)  12.8 us
  transfers between devices with their start and end apart: 4, of which 3 were waited for; matrix products, arithmetic and copies ran while one was open for 7% of the time, Pallas kernels for 0%

commit v1 on v0

v1 whole, which is shorter than its diff:
```python
import jax
import jax.numpy as jnp
from jax import lax
from jax.experimental import pallas as pl
from jax.experimental.pallas import tpu as pltpu
from jax.sharding import Mesh
from jax.sharding import PartitionSpec as P

F32 = jnp.float32
BF16 = jnp.bfloat16
LANES = 128
ROWS = 16
VMEM = pl.BlockSpec(memory_space=pltpu.VMEM)
SMEM = pl.BlockSpec(memory_space=pltpu.SMEM)
ANY = pl.BlockSpec(memory_space=pl.ANY)
NT = (((1,), (1,)), ((), ()))


def call(kernel, out, in_specs, scratch=(), flops=1 << 20):
    return pl.pallas_call(
        kernel,
        out_shape=out,
        in_specs=in_specs,
        out_specs=jax.tree.map(lambda _: VMEM, out),
        scratch_shapes=scratch,
        compiler_params=pltpu.CompilerParams(vmem_limit_bytes=24 << 20),
        cost_estimate=pl.CostEstimate(flops=flops, bytes_accessed=1 << 20, transcendentals=0),
    )


def f32(*shape):
    return jax.ShapeDtypeStruct(shape, F32)


def j_copies(jac, jbuf, sem):
    return [pltpu.make_async_copy(jac.at[b], jbuf.at[b], sem.at[b]) for b in range(jac.shape[0])]


def pack_return(acc, ids, scalars, stage, out):
    n_blk = acc.shape[0]
    n_proj = acc.shape[1] // LANES
    stage[...] = jnp.zeros_like(stage)
    for k in range(n_proj):
        stage[pl.ds(k, n_blk, stride=ROWS), :] = acc[:, k * LANES : (k + 1) * LANES]
    stage[pl.ds(n_proj, n_blk, stride=ROWS), :] = ids.astype(F32)
    for i, value in enumerate(scalars):
        stage[n_proj + 1 + i : n_proj + 2 + i, :] = jnp.full((1, LANES), value, F32)
    turned = stage[...].T.reshape(out.shape[0], *out.shape[2:])
    for x in range(out.shape[1]):
        out[:, x] = turned


def rhs_kernel(live, jac, pix, ids, out, jbuf, stage, sem):
    copies = j_copies(jac, jbuf, sem)
    for copy in copies:
        copy.start()
    n_blk, n_pix = pix.shape
    row = lax.broadcasted_iota(jnp.int32, (n_blk, n_pix), 0)
    values = jnp.where(row < live[0], pix[...].astype(F32), 0.0)
    acc = jnp.zeros((n_blk, jac.shape[2]), F32)
    for b, copy in enumerate(copies):
        copy.wait()
        signal = jnp.where(row == b, values, 0.0).astype(BF16)
        acc += jnp.dot(signal, jbuf[b], preferred_element_type=F32)
    pack_return(acc, ids[...], (), stage, out)


def block_pass(picks, live, copies, jbuf, n_pix):
    n_blk = picks.shape[0]
    row = lax.broadcasted_iota(jnp.int32, (n_blk, n_pix), 0)
    chosen = picks.astype(BF16)
    acc = jnp.zeros(picks.shape, F32)
    for b, copy in enumerate(copies):
        copy.wait()
        image = lax.dot_general(chosen, jbuf[b], NT, preferred_element_type=F32)
        keep = (row == b) & (row < live)
        signal = jnp.where(keep, image, 0.0).astype(BF16)
        acc += jnp.dot(signal, jbuf[b], preferred_element_type=F32)
    return acc


def unpack_picks(recv, turned, n_blk, n_proj):
    turned[...] = recv[...].reshape(LANES, LANES).T
    return jnp.concatenate(
        [turned[pl.ds(k, n_blk, stride=ROWS), :] for k in range(n_proj)], axis=1
    )


def total_of(row, copies):
    return jnp.sum(row) * (1.0 / copies)


def first_kernel(live, jac, ids, recv, out, picks_out, jbuf, turned, stage, sem):
    copies = j_copies(jac, jbuf, sem)
    for copy in copies:
        copy.start()
    n_blk = ids.shape[0]
    n_proj = jac.shape[2] // LANES
    picks = unpack_picks(recv, turned, n_blk, n_proj)
    picks_out[...] = picks
    acc = block_pass(picks, live[0], copies, jbuf, jac.shape[1])
    pack_return(acc, ids[...], (), stage, out)


def second_kernel(
    live, jac, ids, recv, picks_in, res, dirn, image, precond, damping,
    out, res_out, dir_out, alpha_out, jbuf, turned, stage, sem,
):
    copies = j_copies(jac, jbuf, sem)
    for copy in copies:
        copy.start()
    n_blk = ids.shape[0]
    n_proj = jac.shape[2] // LANES
    fresh = unpack_picks(recv, turned, n_blk, n_proj)
    per = recv.shape[1]
    rz = total_of(turned[n_proj + 1 : n_proj + 2, :], per)
    curve = total_of(turned[n_proj + 2 : n_proj + 3, :], per)
    square = total_of(turned[n_proj + 3 : n_proj + 4, :], per)
    alpha = jnp.full((1, LANES), rz, F32) / jnp.full((1, LANES), curve, F32)
    after = rz - 2.0 * alpha * curve + alpha * alpha * square
    beta = after / jnp.full((1, LANES), rz, F32)
    alpha_out[...] = jnp.broadcast_to(alpha, alpha_out.shape)
    pieces = []
    for k in range(n_proj):
        cols = slice(k * LANES, (k + 1) * LANES)
        pieces.append((1.0 + beta) * picks_in[:, cols] - alpha * fresh[:, cols])
    picks = jnp.concatenate(pieces, axis=1)
    n_par, width = res.shape
    damped = jnp.zeros((n_par, LANES), F32)
    rz_next = jnp.zeros((n_par, LANES), F32)
    for h in range(width // LANES):
        cols = slice(h * LANES, (h + 1) * LANES)
        new_res = res[:, cols] - alpha * image[:, cols]
        precon = precond[:, cols] * new_res
        new_dir = precon + beta * dirn[:, cols]
        res_out[:, cols] = new_res
        dir_out[:, cols] = new_dir
        damped += damping[:, cols] * new_dir * new_dir
        rz_next += new_res * precon
    acc = block_pass(picks, live[0], copies, jbuf, jac.shape[1])
    scalars = (jnp.sum(picks * acc), jnp.sum(damped), jnp.sum(rz_next))
    pack_return(acc, ids[...], scalars, stage, out)


def sum_kernel(own_x, recv, out, ids_out, turned, left, right):
    n_x = recv.shape[1]
    n_blk = LANES // ROWS
    n_proj = 9
    sub = lax.broadcasted_iota(jnp.int32, (n_blk, LANES), 0)
    deep = lax.broadcasted_iota(jnp.int32, (LANES, LANES), 0)
    half = n_proj * 8
    for x in range(n_x):
        turned[x] = recv[:, x].reshape(LANES, LANES).T
        for b in range(n_blk):
            at = (x * n_blk + b) * LANES
            cols = slice(at, at + LANES)
            base = b * ROWS
            ids = turned[x, base + n_proj : base + n_proj + 1, :].astype(jnp.int32)
            high = jnp.broadcast_to(ids >> 7, (8, LANES)) == sub
            low = jnp.broadcast_to(ids & 127, (LANES, LANES)) == deep
            spread = jnp.concatenate(
                [
                    jnp.where(
                        high,
                        jnp.broadcast_to(turned[x, base + k : base + k + 1, :], (8, LANES)),
                        0.0,
                    )
                    for k in range(n_proj)
                ],
                axis=0,
            )
            coarse = spread.astype(BF16)
            left[0:half, cols] = coarse
            left[80 : 80 + half, cols] = (spread - coarse.astype(F32)).astype(BF16)
            right[:, cols] = jnp.where(low, 1.0, 0.0).astype(BF16)
    summed = lax.dot_general(left[...], right[...], NT, preferred_element_type=F32)
    out[0:half, :] = summed[0:half] + summed[80 : 80 + half]
    per = recv.shape[2]
    mixed = jnp.zeros((1, LANES), F32)
    for x in range(n_x):
        mixed += turned[x, n_proj + 1 : n_proj + 2, :]
    out[half : half + 1, :] = jnp.full((1, LANES), total_of(mixed, per), F32)
    for i in (1, 2):
        line = turned[0, n_proj + 1 + i : n_proj + 2 + i, :]
        out[half + i : half + i + 1, :] = jnp.full((1, LANES), total_of(line, per), F32)
    out[half + 3 : half + 8, :] = jnp.zeros((5, LANES), F32)
    ids_out[...] = turned[own_x[0], pl.ds(n_proj, n_blk, stride=ROWS), :].astype(jnp.int32)


def lifted(proj, weights, h):
    cols = slice(h * LANES, (h + 1) * LANES)
    n_proj, n_par, _ = proj.shape
    acc = jnp.zeros((n_par, LANES), F32)
    for k in range(n_proj):
        line = weights[k * 8 + h : k * 8 + h + 1, :]
        acc += proj[k, :, cols].astype(F32) * jnp.broadcast_to(line, (n_par, LANES))
    return acc


def projected(proj, field, h, table):
    cols = slice(h * LANES, (h + 1) * LANES)
    for k in range(proj.shape[0]):
        table[k : k + 1, cols] = jnp.sum(
            proj[k, :, cols].astype(F32) * field, axis=0, keepdims=True
        )


def lane_pick(table, low):
    return jnp.take_along_axis(table, low, axis=1, mode="promise_in_bounds")


def send_picks(table, ids, scalars, stage, out):
    n_blk = ids.shape[0]
    n_chunk = table.shape[1] // LANES
    stage[...] = jnp.zeros_like(stage)
    index = ids[...]
    low = index & 127
    high = index >> 7
    for b in range(n_blk):
        low_b = jnp.broadcast_to(low[b : b + 1, :], (8, LANES))
        high_b = jnp.broadcast_to(high[b : b + 1, :], (8, LANES))
        got = jnp.zeros((8, LANES), F32)
        for h in range(n_chunk):
            piece = lane_pick(table[0:8, h * LANES : (h + 1) * LANES], low_b)
            got = jnp.where(high_b == h, piece, got)
        stage[b * ROWS : b * ROWS + 8, :] = got
    got = jnp.zeros((n_blk, LANES), F32)
    for h in range(n_chunk):
        line = jnp.broadcast_to(table[8:9, h * LANES : (h + 1) * LANES], (n_blk, LANES))
        got = jnp.where(high == h, lane_pick(line, low), got)
    stage[pl.ds(8, n_blk, stride=ROWS), :] = got
    for i, value in enumerate(scalars):
        stage[10 + i : 11 + i, :] = jnp.full((1, LANES), value, F32)
    out[...] = stage[...].T.reshape(out.shape)


def start_kernel(own, partner, proj, precond, ids, out, res_out, dir_out, weights, table, stage):
    weights[...] = own[...] + partner[...]
    n_par, width = precond.shape
    for h in range(width // LANES):
        cols = slice(h * LANES, (h + 1) * LANES)
        res = -lifted(proj, weights, h)
        dirn = precond[:, cols] * res
        res_out[:, cols] = res
        dir_out[:, cols] = dirn
        projected(proj, dirn, h, table)
    send_picks(table, ids, (), stage, out)


def step_kernel(
    own, partner, proj, precond, damping, ids, res, dirn, out, image_out, weights, table, stage
):
    weights[...] = own[...] + partner[...]
    n_par, width = precond.shape
    rz = jnp.zeros((n_par, LANES), F32)
    curve = jnp.zeros((n_par, LANES), F32)
    square = jnp.zeros((n_par, LANES), F32)
    for h in range(width // LANES):
        cols = slice(h * LANES, (h + 1) * LANES)
        image = lifted(proj, weights, h) + damping[:, cols] * dirn[:, cols]
        image_out[:, cols] = image
        scaled = precond[:, cols] * image
        projected(proj, scaled, h, table)
        rz += res[:, cols] * dirn[:, cols]
        curve += dirn[:, cols] * image
        square += scaled * image
    send_picks(table, ids, (jnp.sum(rz), jnp.sum(curve), jnp.sum(square)), stage, out)


def last_kernel(
    own, partner, proj, damping, alpha_in, first_dir, res, dirn, sol_out, res_out, weights
):
    weights[...] = own[...] + partner[...]
    rows = proj.shape[0] * 8
    curve = weights[rows : rows + 1, :] + own[rows + 1 : rows + 2, :]
    alpha = own[rows + 2 : rows + 3, :] / curve
    alpha_first = alpha_in[0:1, :]
    for h in range(damping.shape[1] // LANES):
        cols = slice(h * LANES, (h + 1) * LANES)
        image = lifted(proj, weights, h) + damping[:, cols] * dirn[:, cols]
        sol_out[:, cols] = alpha_first * first_dir[:, cols] + alpha * dirn[:, cols]
        res_out[:, cols] = res[:, cols] - alpha * image


def local(jacobian, splat_ids, pix_residual, live_blocks, proj_jac, damping, precond):
    n_blk, n_pix, n_col = jacobian.shape
    n_par, g_dev = damping.shape
    n_scene, n_x, n_core = lax.axis_size("scene"), lax.axis_size("x"), lax.axis_size("core")
    position = (lax.axis_index("scene") * n_x + lax.axis_index("x")) * n_core + lax.axis_index(
        "core"
    )
    live = lax.dynamic_slice(live_blocks, (position,), (1,))
    own_x = lax.axis_index("x").astype(jnp.int32).reshape(1)
    ids = splat_ids & (g_dev - 1)

    per = LANES // n_scene
    msg = f32(n_scene, per, LANES)
    wide = f32(n_scene, n_x, per, LANES)
    sums = f32(80, LANES)
    state = f32(n_par, g_dev)
    square = pltpu.VMEM((LANES, LANES), F32)
    jbuf = pltpu.VMEM((n_blk, n_pix, n_col), BF16)
    sems = pltpu.SemaphoreType.DMA((n_blk,))
    weights = pltpu.VMEM((80, LANES), F32)
    table = pltpu.VMEM((16, g_dev), F32)

    def to_owners(message):
        flat = message.reshape(n_scene * n_x, per, LANES)
        got = lax.all_to_all(flat, ("scene", "x"), 0, 0, tiled=True)
        own, index = call(
            sum_kernel,
            (sums, jax.ShapeDtypeStruct((n_blk, LANES), jnp.int32)),
            [SMEM, VMEM],
            [
                pltpu.VMEM((n_x, LANES, LANES), F32),
                pltpu.VMEM((160, n_x * n_blk * LANES), BF16),
                pltpu.VMEM((LANES, n_x * n_blk * LANES), BF16),
            ],
        )(own_x, got.reshape(n_scene, n_x, per, LANES))
        partner = lax.ppermute(own, "core", [(0, 1), (1, 0)])
        return own, partner, index

    def to_blocks(message):
        return lax.all_to_all(message, "scene", 0, 0, tiled=True)

    message = call(rhs_kernel, wide, [SMEM, ANY, VMEM, VMEM], [jbuf, square, sems])(
        live, jacobian, pix_residual, ids
    )
    own, partner, index = to_owners(message)
    message, res, first_dir = call(
        start_kernel, (msg, state, state), [VMEM] * 5, [weights, table, square]
    )(own, partner, proj_jac, precond, index)
    arrived = to_blocks(message)
    message, picks = call(
        first_kernel,
        (wide, f32(n_blk, n_col)),
        [SMEM, ANY, VMEM, VMEM],
        [jbuf, square, square, sems],
    )(live, jacobian, ids, arrived)
    own, partner, index = to_owners(message)
    message, image = call(step_kernel, (msg, state), [VMEM] * 8, [weights, table, square])(
        own, partner, proj_jac, precond, damping, index, res, first_dir
    )
    arrived = to_blocks(message)
    message, res, second_dir, alpha = call(
        second_kernel,
        (wide, state, state, f32(8, LANES)),
        [SMEM, ANY] + [VMEM] * 8,
        [jbuf, square, square, sems],
    )(live, jacobian, ids, arrived, picks, res, first_dir, image, precond, damping)
    own, partner, index = to_owners(message)
    return call(last_kernel, (state, state), [VMEM] * 8, [weights])(
        own, partner, proj_jac, damping, alpha, first_dir, res, second_dir
    )


def solution(mesh):
    scene = mesh.shape["scene"]
    finer = Mesh(mesh.devices.reshape(scene, -1, 2), ("scene", "x", "core"))
    everywhere = ("scene", "x", "core")
    in_specs = (
        P(everywhere, None, None),
        P(everywhere, None),
        P(everywhere, None),
        P(),
        P(None, None, "scene"),
        P(None, "scene"),
        P(None, "scene"),
    )
    out_specs = (P(None, "scene"), P(None, "scene"))
    return jax.shard_map(local, mesh=finer, in_specs=in_specs, out_specs=out_specs, check_vma=False)
```

time: 336 us -> 110 us (0.33); the launches traced: 329 us -> 109 us
  blocking collectives: 157 us -> 68.7 us
  local copies, waits for them, and re-layouts: 46.9 us -> 5.55 us
  matrix products: 29.3 us -> 0 us
  starting transfers between devices: 35.7 us -> 7.94 us
  other arithmetic: 26.6 us -> 0.69 us
  Pallas kernels: 0 us -> 23.3 us
  waiting for transfers between devices: 19 us -> 2.61 us
  loops' own time: 10.1 us -> 0 us
  between operations: 5.13 us -> 0.71 us
    all_gather x3 -> x0, blocking collectives: 57.9 us -> none  [gathered_total(): return lax.all_gather(value, axis).sum(0)]
    psum x6 -> x0, blocking collectives: 44.7 us -> none  [by_axis(): value = lax.psum(value, axis)]
    all_to_all x4 -> x0, starting transfers between devices: 35.7 us -> none  [the longest x1 20.1 us: back_project(): lax.all_to_all(buffer, SCENE, split_axis=2, concat_axis=2, tiled=True)]
    dot_general x20 -> x0, matrix products: 29.3 us -> none  [the longest x12 19.4 us: advance(): returned = jnp.dot(signal, jac_block, preferred_element_type=jnp.float32)]
    pallas_call x0 -> x9, Pallas kernels: none -> 23.3 us  [the longest x1 6.85 us: local(): call(second_kernel, (wide, state, state, f32(8, LANES)), [SMEM, ANY] + [V...]
    all_to_all x4 -> x0, waiting for transfers between devices: 19 us -> none  [the longest x2 12.8 us: local(): lax.all_to_all(picked, SCENE, split_axis=2, concat_axis=2, tiled=True)]
    scatter-add x3 -> x0, other arithmetic: 18.4 us -> none  [back_project(): jnp.zeros((n_proj, g_dev), jnp.float32).at[:, local_ids.reshape(-1)]]
    all_to_all x2 -> x5, blocking collectives: 54 us -> 68.7 us  [the longest x3 50.1 us: to_owners(): got = lax.all_to_all(flat, ('scene', 'x'), 0, 0, tiled=True)]
  transfers between devices with their start and end apart: 4 -> 3, of which waited for: 3 -> 3; matrix products, arithmetic and copies ran while one was open for 7% -> 0% of each run, Pallas kernels for 0% -> 0%
where the time goes in v1:
time: 110 us; the launch traced here: 109 us
  blocking collectives  68.7 us (62%)
  Pallas kernels  23.3 us (21%)
  starting transfers between devices  7.94 us (7%)
  local copies, waits for them, and re-layouts  5.55 us (5%)
  waiting for transfers between devices  2.61 us (2%)
    all_to_all x3, blocking collectives, to_owners(): got = lax.all_to_all(flat, ('scene', 'x'), 0, 0, tiled=True)  50.1 us
    all_to_all x2, blocking collectives, to_blocks(): return lax.all_to_all(message, 'scene', 0, 0, tiled=True)  18.6 us
    ppermute x3, starting transfers between devices, to_owners(): partner = lax.ppermute(own, 'core', [(0, 1), (1, 0)])  7.94 us
    pallas_call x1, Pallas kernels, local(): call(second_kernel, (wide, state, state, f32(8, LANES)), [SMEM, ANY] + [V...  6.85 us
    pallas_call x1, Pallas kernels, local(): call(first_kernel, (wide, f32(n_blk, n_col)), [SMEM, ANY, VMEM, VMEM], [j...  6.48 us
    unnamed x14, local copies, waits for them, and re-layouts  4.31 us
    pallas_call x3, Pallas kernels, to_owners(): call(sum_kernel, (sums, jax.ShapeDtypeStruct((n_blk, LANES), jnp.int32)),...  3.64 us
    pallas_call x1, Pallas kernels, local(): call(rhs_kernel, wide, [SMEM, ANY, VMEM, VMEM], [jbuf, square, sems])  3.45 us
  transfers between devices with their start and end apart: 3, of which 3 were waited for; matrix products, arithmetic and copies ran while one was open for 0% of the time, Pallas kernels for 0%

profile of v1, /device:TPU:1, one launch (start us, length us, event | category | flops | bytes accessed | tf_op | source)
XLA Modules:
  0.0 109.5 jit_solution(1437224678916893222)
XLA Ops:
  0.6 0.7 broadcast_and_fusion.ids
  1.3 1.2 %dynamic_slice.3.live = s32[1]{0:T(128)} dynamic-slice(s32[128]{0:T(128)} %param.10, s32[]{:T(128)S(6)} %select_n.3), dynamic_slice_sizes={1} | dynamic-slice | bytes 12 | tf_op jit(solution)/shard_map/dynamic_slice | solution.py:292
  2.6 2.3 %copy-done = bf16[8,256,1152]{2,1,0:T(8,128)(2,1)S(1)} copy-done((bf16[8,256,1152]{2,1,0:T(8,128)(2,1)S(1)}, bf16[8,256,1152]{2,1,0:T(8,128)(2,1)}, u32[]{:S(2)}) %copy-start) | copy-done | bytes 4718616
  5.6 3.5 %shard_map.86 = f32[16,4,8,128]{3,2,1,0:T(8,128)S(1)} custom-call(s32[1]{0:T(128)} %dynamic_slice.3.live, bf16[8,256,1152]{2,1,0:T(8,128)(2,1)S(1)} %copy-done, bf16[8,256]{1,0:T(8,128)(2,1)S(1)} %copy-done.6, s32[8,128]{1,0:T(8,128)S(1)} %broadcast_and_fusion.ids), custom_call_target="tpu_custom_call" | custom-call | flops 1048576 | bytes 1048576 | tf_op jit(solution)/shard_map/pallas_call | solution.py:326
  9.1 21.4 %all_to_all.25 = f32[64,8,128]{2,1,0:T(8,128)S(1)} all-to-all(f32[64,8,128]{2,1,0:T(8,128)S(1)} %bitcast.7), channel_id=1, replica_groups=mesh['scene'=16,'x'=4,'core'=2] {'scene','x'}, dimensions={0} | all-to-all | bytes 524288 | tf_op jit(solution)/shard_map/all_to_all | solution.py:309
  30.4 1.1 shard_map.87
  31.5 2.1 %collective-permute-start = (f32[80,128]{1,0:T(8,128)S(1)}, f32[80,128]{1,0:T(8,128)S(1)}, u32[]{:S(2)}, u32[]{:S(2)}) collective-permute-start(f32[80,128]{1,0:T(8,128)S(1)} %get-tuple-element.18.own), channel_id=1, source_target_pairs={{0,1},{1,0},{2,3},{3,2},{4,5},{5,4},{6,7},{7,6},{8,9},{9,8},{10,11... | collective-permute-start | bytes 122888 | tf_op jit(solution)/shard_map/ppermute | solution.py:320
  33.7 0.9 collective-permute-done.partner
  34.5 1.3 %copy-done.2 = bf16[9,59,1024]{2,1,0:T(8,128)(2,1)S(1)} copy-done((bf16[9,59,1024]{2,1,0:T(8,128)(2,1)S(1)}, bf16[9,59,1024]{2,1,0:T(8,128)(2,1)}, u32[]{:S(2)}) %copy-start.2) | copy-done | bytes 1087512
  35.8 0.8 shard_map.88
  36.6 9.3 %all_to_all.26.recv = f32[16,8,128]{2,1,0:T(8,128)S(1)} all-to-all(f32[16,8,128]{2,1,0:T(8,128)S(1)} %get-tuple-element.20), channel_id=1, replica_groups=mesh['scene'=16,'x'=4,'core'=2] {'scene'}, dimensions={0} | all-to-all | bytes 131072 | tf_op jit(solution)/shard_map/all_to_all | solution.py:324
  45.9 6.5 %shard_map.89 = (f32[16,4,8,128]{3,2,1,0:T(8,128)S(1)}, f32[8,1152]{1,0:T(8,128)S(1)}) custom-call(s32[1]{0:T(128)} %dynamic_slice.3.live, bf16[8,256,1152]{2,1,0:T(8,128)(2,1)S(1)} %copy-done.1, s32[8,128]{1,0:T(8,128)S(1)} %broadcast_and_fusion.ids, f32[16,8,128]{2,1,0:T(8,128)S(1)} %all_to_all.26.recv), custom_call_target="tpu_custom_call" | custom-call | flops 1048576 | bytes 1048576 | tf_op jit(solution)/shard_map/pallas_call | solution.py:334
  52.4 14.4 %all_to_all.27 = f32[64,8,128]{2,1,0:T(8,128)S(1)} all-to-all(f32[64,8,128]{2,1,0:T(8,128)S(1)} %bitcast.12), channel_id=1, replica_groups=mesh['scene'=16,'x'=4,'core'=2] {'scene','x'}, dimensions={0} | all-to-all | bytes 524288 | tf_op jit(solution)/shard_map/all_to_all | solution.py:309
  66.8 1.1 shard_map.90
  67.8 2.9 %collective-permute-start.1 = (f32[80,128]{1,0:T(8,128)S(1)}, f32[80,128]{1,0:T(8,128)S(1)}, u32[]{:S(2)}, u32[]{:S(2)}) collective-permute-start(f32[80,128]{1,0:T(8,128)S(1)} %get-tuple-element.22.own), channel_id=1, source_target_pairs={{0,1},{1,0},{2,3},{3,2},{4,5},{5,4},{6,7},{7,6},{8,9},{9,8},{10,11... | collective-permute-start | bytes 122888 | tf_op jit(solution)/shard_map/ppermute | solution.py:320
  70.8 0.9 collective-permute-done.1.partner
  71.6 1.0 shard_map.91
  72.6 9.3 %all_to_all.28.recv = f32[16,8,128]{2,1,0:T(8,128)S(1)} all-to-all(f32[16,8,128]{2,1,0:T(8,128)S(1)} %get-tuple-element.26), channel_id=1, replica_groups=mesh['scene'=16,'x'=4,'core'=2] {'scene'}, dimensions={0} | all-to-all | bytes 131072 | tf_op jit(solution)/shard_map/all_to_all | solution.py:324
  81.9 6.8 %shard_map.92 = (f32[16,4,8,128]{3,2,1,0:T(8,128)S(1)}, f32[59,1024]{1,0:T(8,128)S(1)}, f32[59,1024]{1,0:T(8,128)S(1)}, f32[8,128]{1,0:T(8,128)S(1)}) custom-call(s32[1]{0:T(128)} %dynamic_slice.3.live, bf16[8,256,1152]{2,1,0:T(8,128)(2,1)S(1)} %copy-done.1, s32[8,128]{1,0:T(8,128)S(1)} %broadcast_and_fusion.ids, f32[16,8,128]{2,1,0:T(8,128)S(1)} %all_to_all.28.recv, ...), custom_call_target="tpu_custom_call" | custom-call | flops 1048576 | bytes 1048576 | tf_op jit(solution)/shard_map/pallas_call | solution.py:345
  88.8 14.4 %all_to_all.29 = f32[64,8,128]{2,1,0:T(8,128)S(1)} all-to-all(f32[64,8,128]{2,1,0:T(8,128)S(1)} %bitcast.11), channel_id=1, replica_groups=mesh['scene'=16,'x'=4,'core'=2] {'scene','x'}, dimensions={0} | all-to-all | bytes 524288 | tf_op jit(solution)/shard_map/all_to_all | solution.py:309
  103.1 1.5 %shard_map.93 = (f32[80,128]{1,0:T(8,128)S(1)}, s32[8,128]{1,0:T(8,128)}) custom-call(s32[1]{0:T(128)} %bitcast.own_x, f32[16,4,8,128]{3,2,1,0:T(8,128)S(1)} %bitcast.8), custom_call_target="tpu_custom_call" | custom-call | flops 1048576 | bytes 1048576 | tf_op jit(solution)/shard_map/pallas_call | solution.py:310
  104.6 2.9 %collective-permute-start.2 = (f32[80,128]{1,0:T(8,128)S(1)}, f32[80,128]{1,0:T(8,128)S(1)}, u32[]{:S(2)}, u32[]{:S(2)}) collective-permute-start(f32[80,128]{1,0:T(8,128)S(1)} %get-tuple-element.30.own), channel_id=1, source_target_pairs={{0,1},{1,0},{2,3},{3,2},{4,5},{5,4},{6,7},{7,6},{8,9},{9,8},{10,11... | collective-permute-start | bytes 122888 | tf_op jit(solution)/shard_map/ppermute | solution.py:320
  107.5 0.9 collective-permute-done.2.partner
  108.3 1.1 %shard_map.94 = (f32[59,1024]{1,0:T(8,128)}, f32[59,1024]{1,0:T(8,128)}) custom-call(f32[80,128]{1,0:T(8,128)S(1)} %get-tuple-element.30.own, f32[80,128]{1,0:T(8,128)S(1)} %collective-permute-done.2.partner, bf16[9,59,1024]{2,1,0:T(8,128)(2,1)S(1)} %copy-done.3, f32[59,1024]{1,0:T(8,128)S(1)} %copy-done.4, f32[8,128]{1,0:T(8,128)S(1)} %get-tuple-element.31.alpha_in, ...), custom_call_target="tpu_custom_call" | custom-call | flops 1048576 | bytes 1048576 | tf_op jit(solution)/shard_map/pallas_call | solution.py:352
  (12 shorter events, 0.7 us)
Async XLA Ops:
  2.6 2.3 %copy-start = (bf16[8,256,1152]{2,1,0:T(8,128)(2,1)S(1)}, bf16[8,256,1152]{2,1,0:T(8,128)(2,1)}, u32[]{:S(2)}) copy-start(bf16[8,256,1152]{2,1,0:T(8,128)(2,1)} %jac.5) | copy-start | bytes 14155780
  4.9 0.7 copy-start.6
  5.6 28.9 %copy-start.5 = (f32[59,1024]{1,0:T(8,128)S(1)}, f32[59,1024]{1,0:T(8,128)}, u32[]{:S(2)}) copy-start(f32[59,1024]{1,0:T(8,128)} %precond.5) | copy-start | bytes 724996
  5.6 40.3 %copy-start.1 = (bf16[8,256,1152]{2,1,0:T(8,128)(2,1)S(1)}, bf16[8,256,1152]{2,1,0:T(8,128)(2,1)}, u32[]{:S(2)}) copy-start(bf16[8,256,1152]{2,1,0:T(8,128)(2,1)} %jac.5) | copy-start | bytes 14155780
  9.1 62.6 %copy-start.4 = (f32[59,1024]{1,0:T(8,128)S(1)}, f32[59,1024]{1,0:T(8,128)}, u32[]{:S(2)}) copy-start(f32[59,1024]{1,0:T(8,128)} %damping.5) | copy-start | bytes 724996
  31.5 3.0 %collective-permute-start = (f32[80,128]{1,0:T(8,128)S(1)}, f32[80,128]{1,0:T(8,128)S(1)}, u32[]{:S(2)}, u32[]{:S(2)}) collective-permute-start(f32[80,128]{1,0:T(8,128)S(1)} %get-tuple-element.18.own), channel_id=1, source_target_pairs={{0,1},{1,0},{2,3},{3,2},{4,5},{5,4},{6,7},{7,6},{8,9},{9,8},{10,11... | collective-permute-start | bytes 122888 | tf_op jit(solution)/shard_map/ppermute | solution.py:320
  34.5 1.3 %copy-start.2 = (bf16[9,59,1024]{2,1,0:T(8,128)(2,1)S(1)}, bf16[9,59,1024]{2,1,0:T(8,128)(2,1)}, u32[]{:S(2)}) copy-start(bf16[9,59,1024]{2,1,0:T(8,128)(2,1)} %proj.5) | copy-start | bytes 3262468
  35.8 35.8 %copy-start.3 = (bf16[9,59,1024]{2,1,0:T(8,128)(2,1)S(1)}, bf16[9,59,1024]{2,1,0:T(8,128)(2,1)}, u32[]{:S(2)}) copy-start(bf16[9,59,1024]{2,1,0:T(8,128)(2,1)} %proj.5) | copy-start | bytes 3262468
  67.8 3.8 %collective-permute-start.1 = (f32[80,128]{1,0:T(8,128)S(1)}, f32[80,128]{1,0:T(8,128)S(1)}, u32[]{:S(2)}, u32[]{:S(2)}) collective-permute-start(f32[80,128]{1,0:T(8,128)S(1)} %get-tuple-element.22.own), channel_id=1, source_target_pairs={{0,1},{1,0},{2,3},{3,2},{4,5},{5,4},{6,7},{7,6},{8,9},{9,8},{10,11... | collective-permute-start | bytes 122888 | tf_op jit(solution)/shard_map/ppermute | solution.py:320
  104.6 3.7 %collective-permute-start.2 = (f32[80,128]{1,0:T(8,128)S(1)}, f32[80,128]{1,0:T(8,128)S(1)}, u32[]{:S(2)}, u32[]{:S(2)}) collective-permute-start(f32[80,128]{1,0:T(8,128)S(1)} %get-tuple-element.30.own), channel_id=1, source_target_pairs={{0,1},{1,0},{2,3},{3,2},{4,5},{5,4},{6,7},{7,6},{8,9},{9,8},{10,11... | collective-permute-start | bytes 122888 | tf_op jit(solution)/shard_map/ppermute | solution.py:320

commit v2 on v1

--- a/solution.py
+++ b/solution.py
@@ -11,8 +11,7 @@
 LANES = 128
 ROWS = 16
 VMEM = pl.BlockSpec(memory_space=pltpu.VMEM)
-SMEM = pl.BlockSpec(memory_space=pltpu.SMEM)
-ANY = pl.BlockSpec(memory_space=pl.ANY)
+HBM = pl.BlockSpec(memory_space=pltpu.HBM)
 NT = (((1,), (1,)), ((), ()))
 
 
@@ -28,12 +27,12 @@
     )
 
 
+def in_hbm(array):
+    return pltpu.with_memory_space_constraint(array, pltpu.HBM)
+
+
 def f32(*shape):
     return jax.ShapeDtypeStruct(shape, F32)
-
-
-def j_copies(jac, jbuf, sem):
-    return [pltpu.make_async_copy(jac.at[b], jbuf.at[b], sem.at[b]) for b in range(jac.shape[0])]
 
 
 def pack_return(acc, ids, scalars, stage, out):
@@ -50,32 +49,47 @@
         out[:, x] = turned
 
 
-def rhs_kernel(live, jac, pix, ids, out, jbuf, stage, sem):
-    copies = j_copies(jac, jbuf, sem)
-    for copy in copies:
+def rhs_kernel(live, jac, pix, ids, out, jbuf, aux, pixels, lives, index, stage, sem, small):
+    n_blk = jac.shape[0]
+    minor = [
+        pltpu.make_async_copy(pix, pixels, small.at[0]),
+        pltpu.make_async_copy(live, lives, small.at[1]),
+        pltpu.make_async_copy(ids, index, small.at[2]),
+    ]
+    copies = [pltpu.make_async_copy(jac.at[b], jbuf.at[b], sem.at[b]) for b in range(n_blk)]
+    for copy in minor + copies:
         copy.start()
-    n_blk, n_pix = pix.shape
-    row = lax.broadcasted_iota(jnp.int32, (n_blk, n_pix), 0)
-    values = jnp.where(row < live[0], pix[...].astype(F32), 0.0)
+    for copy in minor:
+        copy.wait()
+    n_x, n_core = lax.axis_size("x"), lax.axis_size("core")
+    position = (lax.axis_index("scene") * n_x + lax.axis_index("x")) * n_core
+    position = position + lax.axis_index("core")
+    lane = lax.broadcasted_iota(jnp.int32, lives.shape, 1)
+    own = jnp.sum(jnp.where(lane == position, lives[...], 0), axis=1, keepdims=True)
+    local_ids = index[...] & (LANES * 8 - 1)
+    aux[0:n_blk, :] = local_ids
+    aux[n_blk : 2 * n_blk, :] = jnp.broadcast_to(own, (n_blk, LANES))
+    row = lax.broadcasted_iota(jnp.int32, pix.shape, 0)
+    keep = row < jnp.broadcast_to(own, pix.shape)
+    values = jnp.where(keep, pixels[...].astype(F32), 0.0)
     acc = jnp.zeros((n_blk, jac.shape[2]), F32)
     for b, copy in enumerate(copies):
         copy.wait()
         signal = jnp.where(row == b, values, 0.0).astype(BF16)
         acc += jnp.dot(signal, jbuf[b], preferred_element_type=F32)
-    pack_return(acc, ids[...], (), stage, out)
-
-
-def block_pass(picks, live, copies, jbuf, n_pix):
-    n_blk = picks.shape[0]
+    pack_return(acc, local_ids, (), stage, out)
+
+
+def block_pass(picks, aux, jac):
+    n_blk, n_pix = jac.shape[:2]
     row = lax.broadcasted_iota(jnp.int32, (n_blk, n_pix), 0)
+    live = row < aux[n_blk : n_blk + 1, 0:1]
     chosen = picks.astype(BF16)
     acc = jnp.zeros(picks.shape, F32)
-    for b, copy in enumerate(copies):
-        copy.wait()
-        image = lax.dot_general(chosen, jbuf[b], NT, preferred_element_type=F32)
-        keep = (row == b) & (row < live)
-        signal = jnp.where(keep, image, 0.0).astype(BF16)
-        acc += jnp.dot(signal, jbuf[b], preferred_element_type=F32)
+    for b in range(n_blk):
+        image = lax.dot_general(chosen, jac[b], NT, preferred_element_type=F32)
+        signal = jnp.where((row == b) & live, image, 0.0).astype(BF16)
+        acc += jnp.dot(signal, jac[b], preferred_element_type=F32)
     return acc
 
 
@@ -90,26 +104,20 @@
     return jnp.sum(row) * (1.0 / copies)
 
 
-def first_kernel(live, jac, ids, recv, out, picks_out, jbuf, turned, stage, sem):
-    copies = j_copies(jac, jbuf, sem)
-    for copy in copies:
-        copy.start()
-    n_blk = ids.shape[0]
+def first_kernel(jac, aux, recv, out, picks_out, turned, stage):
+    n_blk = jac.shape[0]
     n_proj = jac.shape[2] // LANES
     picks = unpack_picks(recv, turned, n_blk, n_proj)
     picks_out[...] = picks
-    acc = block_pass(picks, live[0], copies, jbuf, jac.shape[1])
-    pack_return(acc, ids[...], (), stage, out)
+    acc = block_pass(picks, aux, jac)
+    pack_return(acc, aux[0:n_blk, :], (), stage, out)
 
 
 def second_kernel(
-    live, jac, ids, recv, picks_in, res, dirn, image, precond, damping,
-    out, res_out, dir_out, alpha_out, jbuf, turned, stage, sem,
+    jac, aux, recv, picks_in, res, dirn, image, precond, damping,
+    out, res_out, dir_out, alpha_out, turned, stage,
 ):
-    copies = j_copies(jac, jbuf, sem)
-    for copy in copies:
-        copy.start()
-    n_blk = ids.shape[0]
+    n_blk = jac.shape[0]
     n_proj = jac.shape[2] // LANES
     fresh = unpack_picks(recv, turned, n_blk, n_proj)
     per = recv.shape[1]
@@ -137,12 +145,12 @@
         dir_out[:, cols] = new_dir
         damped += damping[:, cols] * new_dir * new_dir
         rz_next += new_res * precon
-    acc = block_pass(picks, live[0], copies, jbuf, jac.shape[1])
+    acc = block_pass(picks, aux, jac)
     scalars = (jnp.sum(picks * acc), jnp.sum(damped), jnp.sum(rz_next))
-    pack_return(acc, ids[...], scalars, stage, out)
-
-
-def sum_kernel(own_x, recv, out, ids_out, turned, left, right):
+    pack_return(acc, aux[0:n_blk, :], scalars, stage, out)
+
+
+def sum_kernel(recv, out, ids_out, turned, left, right):
     n_x = recv.shape[1]
     n_blk = LANES // ROWS
     n_proj = 9
@@ -184,7 +192,7 @@
         line = turned[0, n_proj + 1 + i : n_proj + 2 + i, :]
         out[half + i : half + i + 1, :] = jnp.full((1, LANES), total_of(line, per), F32)
     out[half + 3 : half + 8, :] = jnp.zeros((5, LANES), F32)
-    ids_out[...] = turned[own_x[0], pl.ds(n_proj, n_blk, stride=ROWS), :].astype(jnp.int32)
+    ids_out[...] = turned[lax.axis_index("x"), pl.ds(n_proj, n_blk, stride=ROWS), :].astype(jnp.int32)
 
 
 def lifted(proj, weights, h):
@@ -285,22 +293,14 @@
 def local(jacobian, splat_ids, pix_residual, live_blocks, proj_jac, damping, precond):
     n_blk, n_pix, n_col = jacobian.shape
     n_par, g_dev = damping.shape
-    n_scene, n_x, n_core = lax.axis_size("scene"), lax.axis_size("x"), lax.axis_size("core")
-    position = (lax.axis_index("scene") * n_x + lax.axis_index("x")) * n_core + lax.axis_index(
-        "core"
-    )
-    live = lax.dynamic_slice(live_blocks, (position,), (1,))
-    own_x = lax.axis_index("x").astype(jnp.int32).reshape(1)
-    ids = splat_ids & (g_dev - 1)
-
+    n_scene, n_x = lax.axis_size("scene"), lax.axis_size("x")
     per = LANES // n_scene
     msg = f32(n_scene, per, LANES)
     wide = f32(n_scene, n_x, per, LANES)
     sums = f32(80, LANES)
     state = f32(n_par, g_dev)
     square = pltpu.VMEM((LANES, LANES), F32)
-    jbuf = pltpu.VMEM((n_blk, n_pix, n_col), BF16)
-    sems = pltpu.SemaphoreType.DMA((n_blk,))
+    whole = jax.ShapeDtypeStruct
     weights = pltpu.VMEM((80, LANES), F32)
     table = pltpu.VMEM((16, g_dev), F32)
 
@@ -310,22 +310,32 @@
         own, index = call(
             sum_kernel,
             (sums, jax.ShapeDtypeStruct((n_blk, LANES), jnp.int32)),
-            [SMEM, VMEM],
+            [VMEM],
             [
                 pltpu.VMEM((n_x, LANES, LANES), F32),
                 pltpu.VMEM((160, n_x * n_blk * LANES), BF16),
                 pltpu.VMEM((LANES, n_x * n_blk * LANES), BF16),
             ],
-        )(own_x, got.reshape(n_scene, n_x, per, LANES))
+        )(got.reshape(n_scene, n_x, per, LANES))
         partner = lax.ppermute(own, "core", [(0, 1), (1, 0)])
         return own, partner, index
 
     def to_blocks(message):
         return lax.all_to_all(message, "scene", 0, 0, tiled=True)
 
-    message = call(rhs_kernel, wide, [SMEM, ANY, VMEM, VMEM], [jbuf, square, sems])(
-        live, jacobian, pix_residual, ids
-    )
+    message, jac, aux = call(
+        rhs_kernel,
+        (wide, whole(jacobian.shape, BF16), whole((2 * n_blk, LANES), jnp.int32)),
+        [HBM] * 4,
+        [
+            pltpu.VMEM((n_blk, n_pix), BF16),
+            pltpu.VMEM((1, live_blocks.shape[0]), jnp.int32),
+            pltpu.VMEM((n_blk, LANES), jnp.int32),
+            square,
+            pltpu.SemaphoreType.DMA((n_blk,)),
+            pltpu.SemaphoreType.DMA((3,)),
+        ],
+    )(*map(in_hbm, (live_blocks.reshape(1, -1), jacobian, pix_residual, splat_ids)))
     own, partner, index = to_owners(message)
     message, res, first_dir = call(
         start_kernel, (msg, state, state), [VMEM] * 5, [weights, table, square]
@@ -334,9 +344,9 @@
     message, picks = call(
         first_kernel,
         (wide, f32(n_blk, n_col)),
-        [SMEM, ANY, VMEM, VMEM],
-        [jbuf, square, square, sems],
-    )(live, jacobian, ids, arrived)
+        [VMEM] * 3,
+        [square, square],
+    )(jac, aux, arrived)
     own, partner, index = to_owners(message)
     message, image = call(step_kernel, (msg, state), [VMEM] * 8, [weights, table, square])(
         own, partner, proj_jac, precond, damping, index, res, first_dir
@@ -345,9 +355,9 @@
     message, res, second_dir, alpha = call(
         second_kernel,
         (wide, state, state, f32(8, LANES)),
-        [SMEM, ANY] + [VMEM] * 8,
-        [jbuf, square, square, sems],
-    )(live, jacobian, ids, arrived, picks, res, first_dir, image, precond, damping)
+        [VMEM] * 9,
+        [square, square],
+    )(jac, aux, arrived, picks, res, first_dir, image, precond, damping)
     own, partner, index = to_owners(message)
     return call(last_kernel, (state, state), [VMEM] * 8, [weights])(
         own, partner, proj_jac, damping, alpha, first_dir, res, second_dir

time: 110 us -> 98.3 us (0.89)
  local copies, waits for them, and re-layouts: 5.55 us -> 0.01 us
  Pallas kernels: 23.3 us -> 18 us
    pallas_call x3, Pallas kernels: 16.8 us -> 11.5 us  [the longest x1 3.98 us: local(): call(second_kernel, (wide, state, state, f32(8, LANES)), [VMEM] * 9, [squ...]
    unnamed x14 -> x6, local copies, waits for them, and re-layouts: 4.31 us -> 0.01 us
    dynamic_slice x1 -> x0, local copies, waits for them, and re-layouts: 1.24 us -> none  [local(): live = lax.dynamic_slice(live_blocks, (position,), (1,))]
where the time goes in v2:
time: 98.3 us; the launch traced here: 98 us
  blocking collectives  68.7 us (70%)
  Pallas kernels  18 us (18%)
  starting transfers between devices  7.95 us (8%)
  waiting for transfers between devices  2.61 us (3%)
    all_to_all x3, blocking collectives, to_owners(): got = lax.all_to_all(flat, ('scene', 'x'), 0, 0, tiled=True)  50.1 us
    all_to_all x2, blocking collectives, to_blocks(): return lax.all_to_all(message, 'scene', 0, 0, tiled=True)  18.6 us
    ppermute x3, starting transfers between devices, to_owners(): partner = lax.ppermute(own, 'core', [(0, 1), (1, 0)])  7.95 us
    pallas_call x1, Pallas kernels, local(): call(second_kernel, (wide, state, state, f32(8, LANES)), [VMEM] * 9, [squ...  3.98 us
    pallas_call x1, Pallas kernels, local(): call(rhs_kernel, (wide, whole(jacobian.shape, BF16), whole((2 * n_blk, LA...  3.86 us
    pallas_call x1, Pallas kernels, local(): call(first_kernel, (wide, f32(n_blk, n_col)), [VMEM] * 3, [square, square])  3.64 us
    pallas_call x3, Pallas kernels, to_owners(): call(sum_kernel, (sums, jax.ShapeDtypeStruct((n_blk, LANES), jnp.int32)),...  3.64 us
    ppermute x3, waiting for transfers between devices, to_owners(): partner = lax.ppermute(own, 'core', [(0, 1), (1, 0)])  2.61 us
  transfers between devices with their start and end apart: 3, of which 3 were waited for; matrix products, arithmetic and copies ran while one was open for 0% of the time, Pallas kernels for 0%

profile of v2, /device:TPU:1, one launch (start us, length us, event | category | flops | bytes accessed | tf_op | source)
XLA Modules:
  0.0 98.0 jit_solution(5182296786641778159)
XLA Ops:
  0.6 0.0 copy-start.2
  0.6 0.0 copy-start
  0.7 3.9 %shard_map.86 = (f32[16,4,8,128]{3,2,1,0:T(8,128)S(1)}, bf16[8,256,1152]{2,1,0:T(8,128)(2,1)S(1)}, s32[16,128]{1,0:T(8,128)S(1)}) custom-call(s32[1,128]{1,0:T(1,128)} %bitcast.13, bf16[8,256,1152]{2,1,0:T(8,128)(2,1)} %jac.1, bf16[8,256]{1,0:T(8,128)(2,1)} %pix.1, s32[8,128]{1,0:T(8,128)} %ids.1), custom_call_target="tpu_custom_call" | custom-call | flops 1048576 | bytes 1048576 | tf_op jit(solution)/shard_map/pallas_call | solution.py:326
  4.5 0.0 copy-start.1
  4.5 21.4 %all_to_all.25 = f32[64,8,128]{2,1,0:T(8,128)S(1)} all-to-all(f32[64,8,128]{2,1,0:T(8,128)S(1)} %bitcast.11), channel_id=1, replica_groups=mesh['scene'=16,'x'=4,'core'=2] {'scene','x'}, dimensions={0} | all-to-all | bytes 524288 | tf_op jit(solution)/shard_map/all_to_all | solution.py:309
  25.9 1.1 %shard_map.87 = (f32[80,128]{1,0:T(8,128)S(1)}, s32[8,128]{1,0:T(8,128)S(1)}) custom-call(f32[16,4,8,128]{3,2,1,0:T(8,128)S(1)} %bitcast.7), custom_call_target="tpu_custom_call" | custom-call | flops 1048576 | bytes 1048576 | tf_op jit(solution)/shard_map/pallas_call | solution.py:310
  27.0 2.1 %collective-permute-start = (f32[80,128]{1,0:T(8,128)S(1)}, f32[80,128]{1,0:T(8,128)S(1)}, u32[]{:S(2)}, u32[]{:S(2)}) collective-permute-start(f32[80,128]{1,0:T(8,128)S(1)} %get-tuple-element.24.own), channel_id=1, source_target_pairs={{0,1},{1,0},{2,3},{3,2},{4,5},{5,4},{6,7},{7,6},{8,9},{9,8},{10,11... | collective-permute-start | bytes 122888 | tf_op jit(solution)/shard_map/ppermute | solution.py:320
  29.1 0.9 collective-permute-done.partner
  30.0 0.8 shard_map.88
  30.8 9.3 %all_to_all.26.recv = f32[16,8,128]{2,1,0:T(8,128)S(1)} all-to-all(f32[16,8,128]{2,1,0:T(8,128)S(1)} %get-tuple-element.26), channel_id=1, replica_groups=mesh['scene'=16,'x'=4,'core'=2] {'scene'}, dimensions={0} | all-to-all | bytes 131072 | tf_op jit(solution)/shard_map/all_to_all | solution.py:324
  40.1 3.6 %shard_map.89 = (f32[16,4,8,128]{3,2,1,0:T(8,128)S(1)}, f32[8,1152]{1,0:T(8,128)S(1)}) custom-call(bf16[8,256,1152]{2,1,0:T(8,128)(2,1)S(1)} %get-tuple-element.21.jac, s32[16,128]{1,0:T(8,128)S(1)} %get-tuple-element.22.aux, f32[16,8,128]{2,1,0:T(8,128)S(1)} %all_to_all.26.recv), custom_call_target="tpu_custom_call" | custom-call | flops 1048576 | bytes 1048576 | tf_op jit(solution)/shard_map/pallas_call | solution.py:344
  43.7 14.4 %all_to_all.27 = f32[64,8,128]{2,1,0:T(8,128)S(1)} all-to-all(f32[64,8,128]{2,1,0:T(8,128)S(1)} %bitcast.12), channel_id=1, replica_groups=mesh['scene'=16,'x'=4,'core'=2] {'scene','x'}, dimensions={0} | all-to-all | bytes 524288 | tf_op jit(solution)/shard_map/all_to_all | solution.py:309
  58.1 1.1 %shard_map.90 = (f32[80,128]{1,0:T(8,128)S(1)}, s32[8,128]{1,0:T(8,128)S(1)}) custom-call(f32[16,4,8,128]{3,2,1,0:T(8,128)S(1)} %bitcast.8), custom_call_target="tpu_custom_call" | custom-call | flops 1048576 | bytes 1048576 | tf_op jit(solution)/shard_map/pallas_call | solution.py:310
  59.2 2.9 %collective-permute-start.1 = (f32[80,128]{1,0:T(8,128)S(1)}, f32[80,128]{1,0:T(8,128)S(1)}, u32[]{:S(2)}, u32[]{:S(2)}) collective-permute-start(f32[80,128]{1,0:T(8,128)S(1)} %get-tuple-element.28.own), channel_id=1, source_target_pairs={{0,1},{1,0},{2,3},{3,2},{4,5},{5,4},{6,7},{7,6},{8,9},{9,8},{10,11... | collective-permute-start | bytes 122888 | tf_op jit(solution)/shard_map/ppermute | solution.py:320
  62.1 0.9 collective-permute-done.1.partner
  63.0 0.0 copy-done.1
  63.0 1.0 shard_map.91
  63.9 9.3 %all_to_all.28.recv = f32[16,8,128]{2,1,0:T(8,128)S(1)} all-to-all(f32[16,8,128]{2,1,0:T(8,128)S(1)} %get-tuple-element.32), channel_id=1, replica_groups=mesh['scene'=16,'x'=4,'core'=2] {'scene'}, dimensions={0} | all-to-all | bytes 131072 | tf_op jit(solution)/shard_map/all_to_all | solution.py:324
  73.2 4.0 %shard_map.92 = (f32[16,4,8,128]{3,2,1,0:T(8,128)S(1)}, f32[59,1024]{1,0:T(8,128)S(1)}, f32[59,1024]{1,0:T(8,128)S(1)}, f32[8,128]{1,0:T(8,128)S(1)}) custom-call(bf16[8,256,1152]{2,1,0:T(8,128)(2,1)S(1)} %get-tuple-element.21.jac, s32[16,128]{1,0:T(8,128)S(1)} %get-tuple-element.22.aux, f32[16,8,128]{2,1,0:T(8,128)S(1)} %all_to_all.28.recv, ...), custom_call_target="tpu_custom_call" | custom-call | flops 1048576 | bytes 1048576 | tf_op jit(solution)/shard_map/pallas_call | solution.py:355
  77.2 14.4 %all_to_all.29 = f32[64,8,128]{2,1,0:T(8,128)S(1)} all-to-all(f32[64,8,128]{2,1,0:T(8,128)S(1)} %bitcast.10), channel_id=1, replica_groups=mesh['scene'=16,'x'=4,'core'=2] {'scene','x'}, dimensions={0} | all-to-all | bytes 524288 | tf_op jit(solution)/shard_map/all_to_all | solution.py:309
  91.6 1.5 %shard_map.93 = (f32[80,128]{1,0:T(8,128)S(1)}, s32[8,128]{1,0:T(8,128)}) custom-call(f32[16,4,8,128]{3,2,1,0:T(8,128)S(1)} %bitcast.9), custom_call_target="tpu_custom_call" | custom-call | flops 1048576 | bytes 1048576 | tf_op jit(solution)/shard_map/pallas_call | solution.py:310
  93.1 2.9 %collective-permute-start.2 = (f32[80,128]{1,0:T(8,128)S(1)}, f32[80,128]{1,0:T(8,128)S(1)}, u32[]{:S(2)}, u32[]{:S(2)}) collective-permute-start(f32[80,128]{1,0:T(8,128)S(1)} %get-tuple-element.36.own), channel_id=1, source_target_pairs={{0,1},{1,0},{2,3},{3,2},{4,5},{5,4},{6,7},{7,6},{8,9},{9,8},{10,11... | collective-permute-start | bytes 122888 | tf_op jit(solution)/shard_map/ppermute | solution.py:320
  96.0 0.9 collective-permute-done.2.partner
  96.8 1.2 %shard_map.94 = (f32[59,1024]{1,0:T(8,128)}, f32[59,1024]{1,0:T(8,128)}) custom-call(f32[80,128]{1,0:T(8,128)S(1)} %get-tuple-element.36.own, f32[80,128]{1,0:T(8,128)S(1)} %collective-permute-done.2.partner, bf16[9,59,1024]{2,1,0:T(8,128)(2,1)S(1)} %copy-done, f32[59,1024]{1,0:T(8,128)S(1)} %copy-done.1, f32[8,128]{1,0:T(8,128)S(1)} %get-tuple-element.37.alpha_in, ...), custom_call_target="tpu_custom_call" | custom-call | flops 1048576 | bytes 1048576 | tf_op jit(solution)/shard_map/pallas_call | solution.py:362
  (2 shorter events, 0.0 us)
Async XLA Ops:
  0.6 29.4 %copy-start.2 = (f32[59,1024]{1,0:T(8,128)S(1)}, f32[59,1024]{1,0:T(8,128)}, u32[]{:S(2)}) copy-start(f32[59,1024]{1,0:T(8,128)} %precond.5) | copy-start | bytes 724996
  0.6 29.4 %copy-start = (bf16[9,59,1024]{2,1,0:T(8,128)(2,1)S(1)}, bf16[9,59,1024]{2,1,0:T(8,128)(2,1)}, u32[]{:S(2)}) copy-start(bf16[9,59,1024]{2,1,0:T(8,128)(2,1)} %proj.5) | copy-start | bytes 3262468
  4.5 58.5 %copy-start.1 = (f32[59,1024]{1,0:T(8,128)S(1)}, f32[59,1024]{1,0:T(8,128)}, u32[]{:S(2)}) copy-start(f32[59,1024]{1,0:T(8,128)} %damping.5) | copy-start | bytes 724996
  27.0 3.0 %collective-permute-start = (f32[80,128]{1,0:T(8,128)S(1)}, f32[80,128]{1,0:T(8,128)S(1)}, u32[]{:S(2)}, u32[]{:S(2)}) collective-permute-start(f32[80,128]{1,0:T(8,128)S(1)} %get-tuple-element.24.own), channel_id=1, source_target_pairs={{0,1},{1,0},{2,3},{3,2},{4,5},{5,4},{6,7},{7,6},{8,9},{9,8},{10,11... | collective-permute-start | bytes 122888 | tf_op jit(solution)/shard_map/ppermute | solution.py:320
  59.2 3.8 %collective-permute-start.1 = (f32[80,128]{1,0:T(8,128)S(1)}, f32[80,128]{1,0:T(8,128)S(1)}, u32[]{:S(2)}, u32[]{:S(2)}) collective-permute-start(f32[80,128]{1,0:T(8,128)S(1)} %get-tuple-element.28.own), channel_id=1, source_target_pairs={{0,1},{1,0},{2,3},{3,2},{4,5},{5,4},{6,7},{7,6},{8,9},{9,8},{10,11... | collective-permute-start | bytes 122888 | tf_op jit(solution)/shard_map/ppermute | solution.py:320
  93.1 3.7 %collective-permute-start.2 = (f32[80,128]{1,0:T(8,128)S(1)}, f32[80,128]{1,0:T(8,128)S(1)}, u32[]{:S(2)}, u32[]{:S(2)}) collective-permute-start(f32[80,128]{1,0:T(8,128)S(1)} %get-tuple-element.36.own), channel_id=1, source_target_pairs={{0,1},{1,0},{2,3},{3,2},{4,5},{5,4},{6,7},{7,6},{8,9},{9,8},{10,11... | collective-permute-start | bytes 122888 | tf_op jit(solution)/shard_map/ppermute | solution.py:320

commit v3 on v2

--- a/solution.py
+++ b/solution.py
@@ -49,8 +49,18 @@
         out[:, x] = turned
 
 
-def rhs_kernel(live, jac, pix, ids, out, jbuf, aux, pixels, lives, index, stage, sem, small):
+def rhs_kernel(
+    live, jac, pix, ids, proj, damping, precond,
+    out, jbuf, aux, proj_out, damping_out, precond_out,
+    pixels, lives, index, stage, sem, small, late,
+):
     n_blk = jac.shape[0]
+    later = [
+        pltpu.make_async_copy(source, target, late.at[i])
+        for i, (source, target) in enumerate(
+            ((proj, proj_out), (precond, precond_out), (damping, damping_out))
+        )
+    ]
     minor = [
         pltpu.make_async_copy(pix, pixels, small.at[0]),
         pltpu.make_async_copy(live, lives, small.at[1]),
@@ -75,9 +85,14 @@
     acc = jnp.zeros((n_blk, jac.shape[2]), F32)
     for b, copy in enumerate(copies):
         copy.wait()
+        if b == n_blk - 2:
+            for extra in later:
+                extra.start()
         signal = jnp.where(row == b, values, 0.0).astype(BF16)
         acc += jnp.dot(signal, jbuf[b], preferred_element_type=F32)
     pack_return(acc, local_ids, (), stage, out)
+    for extra in later:
+        extra.wait()
 
 
 def block_pass(picks, aux, jac):
@@ -85,12 +100,12 @@
     row = lax.broadcasted_iota(jnp.int32, (n_blk, n_pix), 0)
     live = row < aux[n_blk : n_blk + 1, 0:1]
     chosen = picks.astype(BF16)
-    acc = jnp.zeros(picks.shape, F32)
+    signals = []
     for b in range(n_blk):
         image = lax.dot_general(chosen, jac[b], NT, preferred_element_type=F32)
-        signal = jnp.where((row == b) & live, image, 0.0).astype(BF16)
-        acc += jnp.dot(signal, jac[b], preferred_element_type=F32)
-    return acc
+        signals.append(jnp.where((row == b) & live, image, 0.0).astype(BF16))
+    stacked = jac[...].reshape(n_blk * n_pix, jac.shape[2])
+    return jnp.dot(jnp.concatenate(signals, axis=1), stacked, preferred_element_type=F32)
 
 
 def unpack_picks(recv, turned, n_blk, n_proj):
@@ -150,7 +165,8 @@
     pack_return(acc, aux[0:n_blk, :], scalars, stage, out)
 
 
-def sum_kernel(recv, out, ids_out, turned, left, right):
+def sum_kernel(recv, out, *rest):
+    *ids_outs, turned, left, right = rest
     n_x = recv.shape[1]
     n_blk = LANES // ROWS
     n_proj = 9
@@ -192,7 +208,8 @@
         line = turned[0, n_proj + 1 + i : n_proj + 2 + i, :]
         out[half + i : half + i + 1, :] = jnp.full((1, LANES), total_of(line, per), F32)
     out[half + 3 : half + 8, :] = jnp.zeros((5, LANES), F32)
-    ids_out[...] = turned[lax.axis_index("x"), pl.ds(n_proj, n_blk, stride=ROWS), :].astype(jnp.int32)
+    for ids_out in ids_outs:
+        ids_out[...] = turned[lax.axis_index("x"), pl.ds(n_proj, n_blk, stride=ROWS), :].astype(jnp.int32)
 
 
 def lifted(proj, weights, h):
@@ -304,12 +321,12 @@
     weights = pltpu.VMEM((80, LANES), F32)
     table = pltpu.VMEM((16, g_dev), F32)
 
-    def to_owners(message):
+    def to_owners(message, indices):
         flat = message.reshape(n_scene * n_x, per, LANES)
         got = lax.all_to_all(flat, ("scene", "x"), 0, 0, tiled=True)
-        own, index = call(
+        own, *index = call(
             sum_kernel,
-            (sums, jax.ShapeDtypeStruct((n_blk, LANES), jnp.int32)),
+            (sums,) + (whole((n_blk, LANES), jnp.int32),) * indices,
             [VMEM],
             [
                 pltpu.VMEM((n_x, LANES, LANES), F32),
@@ -318,15 +335,16 @@
             ],
         )(got.reshape(n_scene, n_x, per, LANES))
         partner = lax.ppermute(own, "core", [(0, 1), (1, 0)])
-        return own, partner, index
+        return own, partner, *index
 
     def to_blocks(message):
         return lax.all_to_all(message, "scene", 0, 0, tiled=True)
 
-    message, jac, aux = call(
+    message, jac, aux, proj, damping, precond = call(
         rhs_kernel,
-        (wide, whole(jacobian.shape, BF16), whole((2 * n_blk, LANES), jnp.int32)),
-        [HBM] * 4,
+        (wide, whole(jacobian.shape, BF16), whole((2 * n_blk, LANES), jnp.int32))
+        + (whole(proj_jac.shape, BF16), state, state),
+        [HBM] * 7,
         [
             pltpu.VMEM((n_blk, n_pix), BF16),
             pltpu.VMEM((1, live_blocks.shape[0]), jnp.int32),
@@ -334,12 +352,16 @@
             square,
             pltpu.SemaphoreType.DMA((n_blk,)),
             pltpu.SemaphoreType.DMA((3,)),
+            pltpu.SemaphoreType.DMA((3,)),
         ],
-    )(*map(in_hbm, (live_blocks.reshape(1, -1), jacobian, pix_residual, splat_ids)))
-    own, partner, index = to_owners(message)
+    )(
+        *map(in_hbm, (live_blocks.reshape(1, -1), jacobian, pix_residual, splat_ids)),
+        *map(in_hbm, (proj_jac, damping, precond)),
+    )
+    own, partner, index = to_owners(message, 1)
     message, res, first_dir = call(
         start_kernel, (msg, state, state), [VMEM] * 5, [weights, table, square]
-    )(own, partner, proj_jac, precond, index)
+    )(own, partner, proj, precond, index)
     arrived = to_blocks(message)
     message, picks = call(
         first_kernel,
@@ -347,9 +369,9 @@
         [VMEM] * 3,
         [square, square],
     )(jac, aux, arrived)
-    own, partner, index = to_owners(message)
+    own, partner = to_owners(message, 0)
     message, image = call(step_kernel, (msg, state), [VMEM] * 8, [weights, table, square])(
-        own, partner, proj_jac, precond, damping, index, res, first_dir
+        own, partner, proj, precond, damping, index, res, first_dir
     )
     arrived = to_blocks(message)
     message, res, second_dir, alpha = call(
@@ -358,9 +380,9 @@
         [VMEM] * 9,
         [square, square],
     )(jac, aux, arrived, picks, res, first_dir, image, precond, damping)
-    own, partner, index = to_owners(message)
+    own, partner = to_owners(message, 0)
     return call(last_kernel, (state, state), [VMEM] * 8, [weights])(
-        own, partner, proj_jac, damping, alpha, first_dir, res, second_dir
+        own, partner, proj, damping, alpha, first_dir, res, second_dir
     )
 
 

time: 98.3 us -> 95.4 us (0.970)
  Pallas kernels: 18 us -> 15.2 us
    pallas_call x1, Pallas kernels: 3.98 us -> 2.41 us  [local(): call(second_kernel, (wide, state, state, f32(8, LANES)), [VMEM] * 9, [squ...]
    pallas_call x1, Pallas kernels: 3.64 us -> 2.09 us  [local(): call(first_kernel, (wide, f32(n_blk, n_col)), [VMEM] * 3, [square, square])]
where the time goes in v3:
time: 95.4 us; the launch traced here: 95.1 us
  blocking collectives  68.5 us (72%)
  Pallas kernels  15.2 us (16%)
  starting transfers between devices  8.02 us (8%)
  waiting for transfers between devices  2.61 us (3%)
    all_to_all x3, blocking collectives, to_owners(): got = lax.all_to_all(flat, ('scene', 'x'), 0, 0, tiled=True)  50 us
    all_to_all x2, blocking collectives, to_blocks(): return lax.all_to_all(message, 'scene', 0, 0, tiled=True)  18.6 us
    ppermute x3, starting transfers between devices, to_owners(): partner = lax.ppermute(own, 'core', [(0, 1), (1, 0)])  8.02 us
    pallas_call x1, Pallas kernels, local(): call(rhs_kernel, (wide, whole(jacobian.shape, BF16), whole((2 * n_blk, LA...  4.68 us
    pallas_call x3, Pallas kernels, to_owners(): call(sum_kernel, (sums,) + (whole((n_blk, LANES), jnp.int32),) * indices,...  3.14 us
    ppermute x3, waiting for transfers between devices, to_owners(): partner = lax.ppermute(own, 'core', [(0, 1), (1, 0)])  2.61 us
    pallas_call x1, Pallas kernels, local(): call(second_kernel, (wide, state, state, f32(8, LANES)), [VMEM] * 9, [squ...  2.41 us
    pallas_call x1, Pallas kernels, local(): call(first_kernel, (wide, f32(n_blk, n_col)), [VMEM] * 3, [square, square])  2.09 us
  transfers between devices with their start and end apart: 3, of which 3 were waited for; matrix products, arithmetic and copies ran while one was open for 0% of the time, Pallas kernels for 0%

profile of v3, /device:TPU:1, one launch (start us, length us, event | category | flops | bytes accessed | tf_op | source)
XLA Modules:
  0.0 95.1 jit_solution(18181645567458800151)
XLA Ops:
  0.6 4.7 %shard_map.86 = (f32[16,4,8,128]{3,2,1,0:T(8,128)S(1)}, bf16[8,256,1152]{2,1,0:T(8,128)(2,1)S(1)}, s32[16,128]{1,0:T(8,128)S(1)}, bf16[9,59,1024]{2,1,0:T(8,128)...) custom-call(s32[1,128]{1,0:T(1,128)} %bitcast.13, bf16[8,256,1152]{2,1,0:T(8,128)(2,1)} %jac.1, ...), custom_call_target="tpu_custom_call" | custom-call | flops 1048576 | bytes 1048576 | tf_op jit(solution)/shard_map/pallas_call | solution.py:343
  5.3 21.2 %all_to_all.25 = f32[64,8,128]{2,1,0:T(8,128)S(1)} all-to-all(f32[64,8,128]{2,1,0:T(8,128)S(1)} %bitcast.11), channel_id=1, replica_groups=mesh['scene'=16,'x'=4,'core'=2] {'scene','x'}, dimensions={0} | all-to-all | bytes 524288 | tf_op jit(solution)/shard_map/all_to_all | solution.py:326
  26.6 1.1 %shard_map.87 = (f32[80,128]{1,0:T(8,128)S(1)}, s32[8,128]{1,0:T(8,128)S(1)}) custom-call(f32[16,4,8,128]{3,2,1,0:T(8,128)S(1)} %bitcast.7), custom_call_target="tpu_custom_call" | custom-call | flops 1048576 | bytes 1048576 | tf_op jit(solution)/shard_map/pallas_call | solution.py:327
  27.6 2.1 %collective-permute-start = (f32[80,128]{1,0:T(8,128)S(1)}, f32[80,128]{1,0:T(8,128)S(1)}, u32[]{:S(2)}, u32[]{:S(2)}) collective-permute-start(f32[80,128]{1,0:T(8,128)S(1)} %get-tuple-element.24.own), channel_id=1, source_target_pairs={{0,1},{1,0},{2,3},{3,2},{4,5},{5,4},{6,7},{7,6},{8,9},{9,8},{10,11... | collective-permute-start | bytes 122888 | tf_op jit(solution)/shard_map/ppermute | solution.py:337
  29.8 0.9 collective-permute-done.partner
  30.7 0.8 shard_map.88
  31.5 9.3 %all_to_all.26.recv = f32[16,8,128]{2,1,0:T(8,128)S(1)} all-to-all(f32[16,8,128]{2,1,0:T(8,128)S(1)} %get-tuple-element.28), channel_id=1, replica_groups=mesh['scene'=16,'x'=4,'core'=2] {'scene'}, dimensions={0} | all-to-all | bytes 131072 | tf_op jit(solution)/shard_map/all_to_all | solution.py:341
  40.7 2.1 %shard_map.89 = (f32[16,4,8,128]{3,2,1,0:T(8,128)S(1)}, f32[8,1152]{1,0:T(8,128)S(1)}) custom-call(bf16[8,256,1152]{2,1,0:T(8,128)(2,1)S(1)} %get-tuple-element.21.jac, s32[16,128]{1,0:T(8,128)S(1)} %get-tuple-element.22.aux, f32[16,8,128]{2,1,0:T(8,128)S(1)} %all_to_all.26.recv), custom_call_target="tpu_custom_call" | custom-call | flops 1048576 | bytes 1048576 | tf_op jit(solution)/shard_map/pallas_call | solution.py:366
  42.8 14.4 %all_to_all.27 = f32[64,8,128]{2,1,0:T(8,128)S(1)} all-to-all(f32[64,8,128]{2,1,0:T(8,128)S(1)} %bitcast.12), channel_id=1, replica_groups=mesh['scene'=16,'x'=4,'core'=2] {'scene','x'}, dimensions={0} | all-to-all | bytes 524288 | tf_op jit(solution)/shard_map/all_to_all | solution.py:326
  57.2 1.0 %shard_map.90.own = f32[80,128]{1,0:T(8,128)S(1)} custom-call(f32[16,4,8,128]{3,2,1,0:T(8,128)S(1)} %bitcast.8), custom_call_target="tpu_custom_call" | custom-call | flops 1048576 | bytes 1048576 | tf_op jit(solution)/shard_map/pallas_call | solution.py:327
  58.3 2.9 %collective-permute-start.1 = (f32[80,128]{1,0:T(8,128)S(1)}, f32[80,128]{1,0:T(8,128)S(1)}, u32[]{:S(2)}, u32[]{:S(2)}) collective-permute-start(f32[80,128]{1,0:T(8,128)S(1)} %shard_map.90.own), channel_id=1, source_target_pairs={{0,1},{1,0},{2,3},{3,2},{4,5},{5,4},{6,7},{7,6},{8,9},{9,8},{10,11... | collective-permute-start | bytes 122888 | tf_op jit(solution)/shard_map/ppermute | solution.py:337
  61.2 0.9 collective-permute-done.1.partner
  62.1 1.0 %shard_map.91 = (f32[16,8,128]{2,1,0:T(8,128)S(1)}, f32[59,1024]{1,0:T(8,128)S(1)}) custom-call(f32[80,128]{1,0:T(8,128)S(1)} %shard_map.90.own, f32[80,128]{1,0:T(8,128)S(1)} %collective-permute-done.1.partner, bf16[9,59,1024]{2,1,0:T(8,128)(2,1)S(1)} %get-tuple-element.25.proj, f32[59,1024]{1,0:T(8,128)S(1)} %get-tuple-element.26.precond, ...), custom_call_target="tpu_custom_call" | custom-call | flops 1048576 | bytes 1048576 | tf_op jit(solution)/shard_map/pallas_call | solution.py:373
  63.0 9.3 %all_to_all.28.recv = f32[16,8,128]{2,1,0:T(8,128)S(1)} all-to-all(f32[16,8,128]{2,1,0:T(8,128)S(1)} %get-tuple-element.33), channel_id=1, replica_groups=mesh['scene'=16,'x'=4,'core'=2] {'scene'}, dimensions={0} | all-to-all | bytes 131072 | tf_op jit(solution)/shard_map/all_to_all | solution.py:341
  72.3 2.4 %shard_map.92 = (f32[16,4,8,128]{3,2,1,0:T(8,128)S(1)}, f32[59,1024]{1,0:T(8,128)S(1)}, f32[59,1024]{1,0:T(8,128)S(1)}, f32[8,128]{1,0:T(8,128)S(1)}) custom-call(bf16[8,256,1152]{2,1,0:T(8,128)(2,1)S(1)} %get-tuple-element.21.jac, s32[16,128]{1,0:T(8,128)S(1)} %get-tuple-element.22.aux, f32[16,8,128]{2,1,0:T(8,128)S(1)} %all_to_all.28.recv, ...), custom_call_target="tpu_custom_call" | custom-call | flops 1048576 | bytes 1048576 | tf_op jit(solution)/shard_map/pallas_call | solution.py:377
  74.7 14.4 %all_to_all.29 = f32[64,8,128]{2,1,0:T(8,128)S(1)} all-to-all(f32[64,8,128]{2,1,0:T(8,128)S(1)} %bitcast.10), channel_id=1, replica_groups=mesh['scene'=16,'x'=4,'core'=2] {'scene','x'}, dimensions={0} | all-to-all | bytes 524288 | tf_op jit(solution)/shard_map/all_to_all | solution.py:326
  89.1 1.0 %shard_map.93.own = f32[80,128]{1,0:T(8,128)S(1)} custom-call(f32[16,4,8,128]{3,2,1,0:T(8,128)S(1)} %bitcast.9), custom_call_target="tpu_custom_call" | custom-call | flops 1048576 | bytes 1048576 | tf_op jit(solution)/shard_map/pallas_call | solution.py:327
  90.1 2.9 %collective-permute-start.2 = (f32[80,128]{1,0:T(8,128)S(1)}, f32[80,128]{1,0:T(8,128)S(1)}, u32[]{:S(2)}, u32[]{:S(2)}) collective-permute-start(f32[80,128]{1,0:T(8,128)S(1)} %shard_map.93.own), channel_id=1, source_target_pairs={{0,1},{1,0},{2,3},{3,2},{4,5},{5,4},{6,7},{7,6},{8,9},{9,8},{10,11... | collective-permute-start | bytes 122888 | tf_op jit(solution)/shard_map/ppermute | solution.py:337
  93.1 0.9 collective-permute-done.2.partner
  94.0 1.2 %shard_map.94 = (f32[59,1024]{1,0:T(8,128)}, f32[59,1024]{1,0:T(8,128)}) custom-call(f32[80,128]{1,0:T(8,128)S(1)} %shard_map.93.own, f32[80,128]{1,0:T(8,128)S(1)} %collective-permute-done.2.partner, bf16[9,59,1024]{2,1,0:T(8,128)(2,1)S(1)} %get-tuple-element.25.proj, f32[59,1024]{1,0:T(8,128)S(1)} %get-tuple-element.30.damping, ...), custom_call_target="tpu_custom_call" | custom-call | flops 1048576 | bytes 1048576 | tf_op jit(solution)/shard_map/pallas_call | solution.py:384
Async XLA Ops:
  27.6 3.0 %collective-permute-start = (f32[80,128]{1,0:T(8,128)S(1)}, f32[80,128]{1,0:T(8,128)S(1)}, u32[]{:S(2)}, u32[]{:S(2)}) collective-permute-start(f32[80,128]{1,0:T(8,128)S(1)} %get-tuple-element.24.own), channel_id=1, source_target_pairs={{0,1},{1,0},{2,3},{3,2},{4,5},{5,4},{6,7},{7,6},{8,9},{9,8},{10,11... | collective-permute-start | bytes 122888 | tf_op jit(solution)/shard_map/ppermute | solution.py:337
  58.3 3.8 %collective-permute-start.1 = (f32[80,128]{1,0:T(8,128)S(1)}, f32[80,128]{1,0:T(8,128)S(1)}, u32[]{:S(2)}, u32[]{:S(2)}) collective-permute-start(f32[80,128]{1,0:T(8,128)S(1)} %shard_map.90.own), channel_id=1, source_target_pairs={{0,1},{1,0},{2,3},{3,2},{4,5},{5,4},{6,7},{7,6},{8,9},{9,8},{10,11... | collective-permute-start | bytes 122888 | tf_op jit(solution)/shard_map/ppermute | solution.py:337
  90.1 3.8 %collective-permute-start.2 = (f32[80,128]{1,0:T(8,128)S(1)}, f32[80,128]{1,0:T(8,128)S(1)}, u32[]{:S(2)}, u32[]{:S(2)}) collective-permute-start(f32[80,128]{1,0:T(8,128)S(1)} %shard_map.93.own), channel_id=1, source_target_pairs={{0,1},{1,0},{2,3},{3,2},{4,5},{5,4},{6,7},{7,6},{8,9},{9,8},{10,11... | collective-permute-start | bytes 122888 | tf_op jit(solution)/shard_map/ppermute | solution.py:337

commit v4 on v2

--- a/solution.py
+++ b/solution.py
@@ -85,12 +85,12 @@
     row = lax.broadcasted_iota(jnp.int32, (n_blk, n_pix), 0)
     live = row < aux[n_blk : n_blk + 1, 0:1]
     chosen = picks.astype(BF16)
-    acc = jnp.zeros(picks.shape, F32)
+    signals = []
     for b in range(n_blk):
         image = lax.dot_general(chosen, jac[b], NT, preferred_element_type=F32)
-        signal = jnp.where((row == b) & live, image, 0.0).astype(BF16)
-        acc += jnp.dot(signal, jac[b], preferred_element_type=F32)
-    return acc
+        signals.append(jnp.where((row == b) & live, image, 0.0).astype(BF16))
+    stacked = jac[...].reshape(n_blk * n_pix, jac.shape[2])
+    return jnp.dot(jnp.concatenate(signals, axis=1), stacked, preferred_element_type=F32)
 
 
 def unpack_picks(recv, turned, n_blk, n_proj):
@@ -150,7 +150,8 @@
     pack_return(acc, aux[0:n_blk, :], scalars, stage, out)
 
 
-def sum_kernel(recv, out, ids_out, turned, left, right):
+def sum_kernel(recv, out, *rest):
+    *ids_outs, turned, left, right = rest
     n_x = recv.shape[1]
     n_blk = LANES // ROWS
     n_proj = 9
@@ -192,7 +193,8 @@
         line = turned[0, n_proj + 1 + i : n_proj + 2 + i, :]
         out[half + i : half + i + 1, :] = jnp.full((1, LANES), total_of(line, per), F32)
     out[half + 3 : half + 8, :] = jnp.zeros((5, LANES), F32)
-    ids_out[...] = turned[lax.axis_index("x"), pl.ds(n_proj, n_blk, stride=ROWS), :].astype(jnp.int32)
+    for ids_out in ids_outs:
+        ids_out[...] = turned[lax.axis_index("x"), pl.ds(n_proj, n_blk, stride=ROWS), :].astype(jnp.int32)
 
 
 def lifted(proj, weights, h):
@@ -304,21 +306,22 @@
     weights = pltpu.VMEM((80, LANES), F32)
     table = pltpu.VMEM((16, g_dev), F32)
 
-    def to_owners(message):
+    def to_owners(message, indices):
         flat = message.reshape(n_scene * n_x, per, LANES)
         got = lax.all_to_all(flat, ("scene", "x"), 0, 0, tiled=True)
-        own, index = call(
+        own, *index = call(
             sum_kernel,
-            (sums, jax.ShapeDtypeStruct((n_blk, LANES), jnp.int32)),
+            (sums,) + (whole((n_blk, LANES), jnp.int32),) * indices,
             [VMEM],
             [
                 pltpu.VMEM((n_x, LANES, LANES), F32),
                 pltpu.VMEM((160, n_x * n_blk * LANES), BF16),
                 pltpu.VMEM((LANES, n_x * n_blk * LANES), BF16),
             ],
+            2147483648,
         )(got.reshape(n_scene, n_x, per, LANES))
         partner = lax.ppermute(own, "core", [(0, 1), (1, 0)])
-        return own, partner, index
+        return own, partner, *index
 
     def to_blocks(message):
         return lax.all_to_all(message, "scene", 0, 0, tiled=True)
@@ -336,7 +339,7 @@
             pltpu.SemaphoreType.DMA((3,)),
         ],
     )(*map(in_hbm, (live_blocks.reshape(1, -1), jacobian, pix_residual, splat_ids)))
-    own, partner, index = to_owners(message)
+    own, partner, index = to_owners(message, 1)
     message, res, first_dir = call(
         start_kernel, (msg, state, state), [VMEM] * 5, [weights, table, square]
     )(own, partner, proj_jac, precond, index)
@@ -347,7 +350,7 @@
         [VMEM] * 3,
         [square, square],
     )(jac, aux, arrived)
-    own, partner, index = to_owners(message)
+    own, partner = to_owners(message, 0)
     message, image = call(step_kernel, (msg, state), [VMEM] * 8, [weights, table, square])(
         own, partner, proj_jac, precond, damping, index, res, first_dir
     )
@@ -358,7 +361,7 @@
         [VMEM] * 9,
         [square, square],
     )(jac, aux, arrived, picks, res, first_dir, image, precond, damping)
-    own, partner, index = to_owners(message)
+    own, partner = to_owners(message, 0)
     return call(last_kernel, (state, state), [VMEM] * 8, [weights])(
         own, partner, proj_jac, damping, alpha, first_dir, res, second_dir
     )

time: 98.3 us -> 94.8 us (0.964)
  Pallas kernels: 18 us -> 14.3 us
    pallas_call x1, Pallas kernels: 3.98 us -> 2.42 us  [local(): call(second_kernel, (wide, state, state, f32(8, LANES)), [VMEM] * 9, [squ...]
    pallas_call x1, Pallas kernels: 3.64 us -> 2.09 us  [local(): call(first_kernel, (wide, f32(n_blk, n_col)), [VMEM] * 3, [square, square])]
where the time goes in v4:
time: 94.8 us; the launch traced here: 94.5 us
  blocking collectives  68.8 us (73%)
  Pallas kernels  14.3 us (15%)
  starting transfers between devices  8.03 us (8%)
  waiting for transfers between devices  2.61 us (3%)
    all_to_all x3, blocking collectives, to_owners(): got = lax.all_to_all(flat, ('scene', 'x'), 0, 0, tiled=True)  50.2 us
    all_to_all x2, blocking collectives, to_blocks(): return lax.all_to_all(message, 'scene', 0, 0, tiled=True)  18.6 us
    ppermute x3, starting transfers between devices, to_owners(): partner = lax.ppermute(own, 'core', [(0, 1), (1, 0)])  8.03 us
    pallas_call x1, Pallas kernels, local(): call(rhs_kernel, (wide, whole(jacobian.shape, BF16), whole((2 * n_blk, LA...  3.77 us
    pallas_call x3, Pallas kernels, to_owners(): call(sum_kernel, (sums,) + (whole((n_blk, LANES), jnp.int32),) * indices,...  3.15 us
    ppermute x3, waiting for transfers between devices, to_owners(): partner = lax.ppermute(own, 'core', [(0, 1), (1, 0)])  2.61 us
    pallas_call x1, Pallas kernels, local(): call(second_kernel, (wide, state, state, f32(8, LANES)), [VMEM] * 9, [squ...  2.42 us
    pallas_call x1, Pallas kernels, local(): call(first_kernel, (wide, f32(n_blk, n_col)), [VMEM] * 3, [square, square])  2.09 us
  transfers between devices with their start and end apart: 3, of which 3 were waited for; matrix products, arithmetic and copies ran while one was open for 0% of the time, Pallas kernels for 0%

profile of v4, /device:TPU:1, one launch (start us, length us, event | category | flops | bytes accessed | tf_op | source)
XLA Modules:
  0.0 94.5 jit_solution(8434425951431943408)
XLA Ops:
  0.6 3.8 %shard_map.86 = (f32[16,4,8,128]{3,2,1,0:T(8,128)S(1)}, bf16[8,256,1152]{2,1,0:T(8,128)(2,1)S(1)}, s32[16,128]{1,0:T(8,128)S(1)}) custom-call(s32[1,128]{1,0:T(1,128)} %bitcast.13, bf16[8,256,1152]{2,1,0:T(8,128)(2,1)} %jac.1, bf16[8,256]{1,0:T(8,128)(2,1)} %pix.1, s32[8,128]{1,0:T(8,128)} %ids.1), custom_call_target="tpu_custom_call" | custom-call | flops 1048576 | bytes 1048576 | tf_op jit(solution)/shard_map/pallas_call | solution.py:329
  4.4 0.0 copy-start
  4.4 0.0 copy-start.2
  4.4 21.4 %all_to_all.25 = f32[64,8,128]{2,1,0:T(8,128)S(1)} all-to-all(f32[64,8,128]{2,1,0:T(8,128)S(1)} %bitcast.8), channel_id=1, replica_groups=mesh['scene'=16,'x'=4,'core'=2] {'scene','x'}, dimensions={0} | all-to-all | bytes 524288 | tf_op jit(solution)/shard_map/all_to_all | solution.py:311
  25.8 1.1 %shard_map.87 = (f32[80,128]{1,0:T(8,128)S(1)}, s32[8,128]{1,0:T(8,128)S(1)}) custom-call(f32[16,4,8,128]{3,2,1,0:T(8,128)S(1)} %bitcast.9), custom_call_target="tpu_custom_call" | custom-call | flops 2147483648 | bytes 1048576 | tf_op jit(solution)/shard_map/pallas_call | solution.py:312
  26.9 2.1 %collective-permute-start = (f32[80,128]{1,0:T(8,128)S(1)}, f32[80,128]{1,0:T(8,128)S(1)}, u32[]{:S(2)}, u32[]{:S(2)}) collective-permute-start(f32[80,128]{1,0:T(8,128)S(1)} %get-tuple-element.21.own), channel_id=1, source_target_pairs={{0,1},{1,0},{2,3},{3,2},{4,5},{5,4},{6,7},{7,6},{8,9},{9,8},{10,11... | collective-permute-start | bytes 122888 | tf_op jit(solution)/shard_map/ppermute | solution.py:323
  29.0 0.9 collective-permute-done.partner
  29.9 0.0 copy-done
  29.9 0.8 shard_map.88
  30.7 9.3 %all_to_all.26.recv = f32[16,8,128]{2,1,0:T(8,128)S(1)} all-to-all(f32[16,8,128]{2,1,0:T(8,128)S(1)} %get-tuple-element.23), channel_id=1, replica_groups=mesh['scene'=16,'x'=4,'core'=2] {'scene'}, dimensions={0} | all-to-all | bytes 131072 | tf_op jit(solution)/shard_map/all_to_all | solution.py:327
  40.0 2.1 %shard_map.89 = (f32[16,4,8,128]{3,2,1,0:T(8,128)S(1)}, f32[8,1152]{1,0:T(8,128)S(1)}) custom-call(bf16[8,256,1152]{2,1,0:T(8,128)(2,1)S(1)} %get-tuple-element.18.jac, s32[16,128]{1,0:T(8,128)S(1)} %get-tuple-element.19.aux, f32[16,8,128]{2,1,0:T(8,128)S(1)} %all_to_all.26.recv), custom_call_target="tpu_custom_call" | custom-call | flops 1048576 | bytes 1048576 | tf_op jit(solution)/shard_map/pallas_call | solution.py:347
  42.1 0.0 copy-start.1
  42.1 14.5 %all_to_all.27 = f32[64,8,128]{2,1,0:T(8,128)S(1)} all-to-all(f32[64,8,128]{2,1,0:T(8,128)S(1)} %bitcast.10), channel_id=1, replica_groups=mesh['scene'=16,'x'=4,'core'=2] {'scene','x'}, dimensions={0} | all-to-all | bytes 524288 | tf_op jit(solution)/shard_map/all_to_all | solution.py:311
  56.6 1.0 %shard_map.90.own = f32[80,128]{1,0:T(8,128)S(1)} custom-call(f32[16,4,8,128]{3,2,1,0:T(8,128)S(1)} %bitcast.11), custom_call_target="tpu_custom_call" | custom-call | flops 2147483648 | bytes 1048576 | tf_op jit(solution)/shard_map/pallas_call | solution.py:312
  57.6 2.9 %collective-permute-start.1 = (f32[80,128]{1,0:T(8,128)S(1)}, f32[80,128]{1,0:T(8,128)S(1)}, u32[]{:S(2)}, u32[]{:S(2)}) collective-permute-start(f32[80,128]{1,0:T(8,128)S(1)} %shard_map.90.own), channel_id=1, source_target_pairs={{0,1},{1,0},{2,3},{3,2},{4,5},{5,4},{6,7},{7,6},{8,9},{9,8},{10,11... | collective-permute-start | bytes 122888 | tf_op jit(solution)/shard_map/ppermute | solution.py:323
  60.6 0.9 collective-permute-done.1.partner
  61.5 1.0 %shard_map.91 = (f32[16,8,128]{2,1,0:T(8,128)S(1)}, f32[59,1024]{1,0:T(8,128)S(1)}) custom-call(f32[80,128]{1,0:T(8,128)S(1)} %shard_map.90.own, f32[80,128]{1,0:T(8,128)S(1)} %collective-permute-done.1.partner, bf16[9,59,1024]{2,1,0:T(8,128)(2,1)S(1)} %copy-done, f32[59,1024]{1,0:T(8,128)S(1)} %copy-done.2, f32[59,1024]{1,0:T(8,128)S(1)} %copy-done.1, ...), custom_call_target="tpu_custom_call" | custom-call | flops 1048576 | bytes 1048576 | tf_op jit(solution)/shard_map/pallas_call | solution.py:354
  62.4 9.3 %all_to_all.28.recv = f32[16,8,128]{2,1,0:T(8,128)S(1)} all-to-all(f32[16,8,128]{2,1,0:T(8,128)S(1)} %get-tuple-element.27), channel_id=1, replica_groups=mesh['scene'=16,'x'=4,'core'=2] {'scene'}, dimensions={0} | all-to-all | bytes 131072 | tf_op jit(solution)/shard_map/all_to_all | solution.py:327
  71.7 2.4 %shard_map.92 = (f32[16,4,8,128]{3,2,1,0:T(8,128)S(1)}, f32[59,1024]{1,0:T(8,128)S(1)}, f32[59,1024]{1,0:T(8,128)S(1)}, f32[8,128]{1,0:T(8,128)S(1)}) custom-call(bf16[8,256,1152]{2,1,0:T(8,128)(2,1)S(1)} %get-tuple-element.18.jac, s32[16,128]{1,0:T(8,128)S(1)} %get-tuple-element.19.aux, f32[16,8,128]{2,1,0:T(8,128)S(1)} %all_to_all.28.recv, ...), custom_call_target="tpu_custom_call" | custom-call | flops 1048576 | bytes 1048576 | tf_op jit(solution)/shard_map/pallas_call | solution.py:358
  74.1 14.4 %all_to_all.29 = f32[64,8,128]{2,1,0:T(8,128)S(1)} all-to-all(f32[64,8,128]{2,1,0:T(8,128)S(1)} %bitcast.7), channel_id=1, replica_groups=mesh['scene'=16,'x'=4,'core'=2] {'scene','x'}, dimensions={0} | all-to-all | bytes 524288 | tf_op jit(solution)/shard_map/all_to_all | solution.py:311
  88.5 1.0 %shard_map.93.own = f32[80,128]{1,0:T(8,128)S(1)} custom-call(f32[16,4,8,128]{3,2,1,0:T(8,128)S(1)} %bitcast.12), custom_call_target="tpu_custom_call" | custom-call | flops 2147483648 | bytes 1048576 | tf_op jit(solution)/shard_map/pallas_call | solution.py:312
  89.5 2.9 %collective-permute-start.2 = (f32[80,128]{1,0:T(8,128)S(1)}, f32[80,128]{1,0:T(8,128)S(1)}, u32[]{:S(2)}, u32[]{:S(2)}) collective-permute-start(f32[80,128]{1,0:T(8,128)S(1)} %shard_map.93.own), channel_id=1, source_target_pairs={{0,1},{1,0},{2,3},{3,2},{4,5},{5,4},{6,7},{7,6},{8,9},{9,8},{10,11... | collective-permute-start | bytes 122888 | tf_op jit(solution)/shard_map/ppermute | solution.py:323
  92.5 0.9 collective-permute-done.2.partner
  93.4 1.1 %shard_map.94 = (f32[59,1024]{1,0:T(8,128)}, f32[59,1024]{1,0:T(8,128)}) custom-call(f32[80,128]{1,0:T(8,128)S(1)} %shard_map.93.own, f32[80,128]{1,0:T(8,128)S(1)} %collective-permute-done.2.partner, bf16[9,59,1024]{2,1,0:T(8,128)(2,1)S(1)} %copy-done, f32[59,1024]{1,0:T(8,128)S(1)} %copy-done.1, f32[8,128]{1,0:T(8,128)S(1)} %get-tuple-element.31.alpha_in, ...), custom_call_target="tpu_custom_call" | custom-call | flops 1048576 | bytes 1048576 | tf_op jit(solution)/shard_map/pallas_call | solution.py:365
  (2 shorter events, 0.0 us)
Async XLA Ops:
  4.4 25.5 %copy-start = (bf16[9,59,1024]{2,1,0:T(8,128)(2,1)S(1)}, bf16[9,59,1024]{2,1,0:T(8,128)(2,1)}, u32[]{:S(2)}) copy-start(bf16[9,59,1024]{2,1,0:T(8,128)(2,1)} %proj.5) | copy-start | bytes 3262468
  4.4 25.5 %copy-start.2 = (f32[59,1024]{1,0:T(8,128)S(1)}, f32[59,1024]{1,0:T(8,128)}, u32[]{:S(2)}) copy-start(f32[59,1024]{1,0:T(8,128)} %precond.5) | copy-start | bytes 724996
  26.9 3.0 %collective-permute-start = (f32[80,128]{1,0:T(8,128)S(1)}, f32[80,128]{1,0:T(8,128)S(1)}, u32[]{:S(2)}, u32[]{:S(2)}) collective-permute-start(f32[80,128]{1,0:T(8,128)S(1)} %get-tuple-element.21.own), channel_id=1, source_target_pairs={{0,1},{1,0},{2,3},{3,2},{4,5},{5,4},{6,7},{7,6},{8,9},{9,8},{10,11... | collective-permute-start | bytes 122888 | tf_op jit(solution)/shard_map/ppermute | solution.py:323
  42.1 19.4 %copy-start.1 = (f32[59,1024]{1,0:T(8,128)S(1)}, f32[59,1024]{1,0:T(8,128)}, u32[]{:S(2)}) copy-start(f32[59,1024]{1,0:T(8,128)} %damping.5) | copy-start | bytes 724996
  57.6 3.8 %collective-permute-start.1 = (f32[80,128]{1,0:T(8,128)S(1)}, f32[80,128]{1,0:T(8,128)S(1)}, u32[]{:S(2)}, u32[]{:S(2)}) collective-permute-start(f32[80,128]{1,0:T(8,128)S(1)} %shard_map.90.own), channel_id=1, source_target_pairs={{0,1},{1,0},{2,3},{3,2},{4,5},{5,4},{6,7},{7,6},{8,9},{9,8},{10,11... | collective-permute-start | bytes 122888 | tf_op jit(solution)/shard_map/ppermute | solution.py:323
  89.5 3.8 %collective-permute-start.2 = (f32[80,128]{1,0:T(8,128)S(1)}, f32[80,128]{1,0:T(8,128)S(1)}, u32[]{:S(2)}, u32[]{:S(2)}) collective-permute-start(f32[80,128]{1,0:T(8,128)S(1)} %shard_map.93.own), channel_id=1, source_target_pairs={{0,1},{1,0},{2,3},{3,2},{4,5},{5,4},{6,7},{7,6},{8,9},{9,8},{10,11... | collective-permute-start | bytes 122888 | tf_op jit(solution)/shard_map/ppermute | solution.py:323

commit v5 on v4

--- a/solution.py
+++ b/solution.py
@@ -1,3 +1,5 @@
+import functools
+
 import jax
 import jax.numpy as jnp
 from jax import lax
@@ -15,12 +17,12 @@
 NT = (((1,), (1,)), ((), ()))
 
 
-def call(kernel, out, in_specs, scratch=(), flops=1 << 20):
+def call(kernel, out, in_specs, scratch=(), flops=1 << 20, out_space=VMEM):
     return pl.pallas_call(
         kernel,
         out_shape=out,
         in_specs=in_specs,
-        out_specs=jax.tree.map(lambda _: VMEM, out),
+        out_specs=jax.tree.map(lambda _: out_space, out),
         scratch_shapes=scratch,
         compiler_params=pltpu.CompilerParams(vmem_limit_bytes=24 << 20),
         cost_estimate=pl.CostEstimate(flops=flops, bytes_accessed=1 << 20, transcendentals=0),
@@ -72,15 +74,19 @@
     row = lax.broadcasted_iota(jnp.int32, pix.shape, 0)
     keep = row < jnp.broadcast_to(own, pix.shape)
     values = jnp.where(keep, pixels[...].astype(F32), 0.0)
-    acc = jnp.zeros((n_blk, jac.shape[2]), F32)
-    for b, copy in enumerate(copies):
-        copy.wait()
-        signal = jnp.where(row == b, values, 0.0).astype(BF16)
-        acc += jnp.dot(signal, jbuf[b], preferred_element_type=F32)
+    n_pix, n_col = jac.shape[1:]
+    acc = jnp.zeros((n_blk, n_col), F32)
+    cut = n_blk * 3 // 4
+    for first, last in ((0, cut), (cut, n_blk)):
+        signals = [jnp.where(row == b, values, 0.0).astype(BF16) for b in range(first, last)]
+        for copy in copies[first:last]:
+            copy.wait()
+        stacked = jbuf[first:last].reshape((last - first) * n_pix, n_col)
+        acc += jnp.dot(jnp.concatenate(signals, axis=1), stacked, preferred_element_type=F32)
     pack_return(acc, local_ids, (), stage, out)
 
 
-def block_pass(picks, aux, jac):
+def block_pass(picks, aux, jac, beside=None):
     n_blk, n_pix = jac.shape[:2]
     row = lax.broadcasted_iota(jnp.int32, (n_blk, n_pix), 0)
     live = row < aux[n_blk : n_blk + 1, 0:1]
@@ -88,6 +94,8 @@
     signals = []
     for b in range(n_blk):
         image = lax.dot_general(chosen, jac[b], NT, preferred_element_type=F32)
+        if beside is not None:
+            beside(b)
         signals.append(jnp.where((row == b) & live, image, 0.0).astype(BF16))
     stacked = jac[...].reshape(n_blk * n_pix, jac.shape[2])
     return jnp.dot(jnp.concatenate(signals, axis=1), stacked, preferred_element_type=F32)
@@ -134,54 +142,57 @@
         pieces.append((1.0 + beta) * picks_in[:, cols] - alpha * fresh[:, cols])
     picks = jnp.concatenate(pieces, axis=1)
     n_par, width = res.shape
-    damped = jnp.zeros((n_par, LANES), F32)
-    rz_next = jnp.zeros((n_par, LANES), F32)
-    for h in range(width // LANES):
+    sums = [jnp.zeros((n_par, LANES), F32)] * 2
+
+    def update(h):
         cols = slice(h * LANES, (h + 1) * LANES)
         new_res = res[:, cols] - alpha * image[:, cols]
         precon = precond[:, cols] * new_res
         new_dir = precon + beta * dirn[:, cols]
         res_out[:, cols] = new_res
         dir_out[:, cols] = new_dir
-        damped += damping[:, cols] * new_dir * new_dir
-        rz_next += new_res * precon
-    acc = block_pass(picks, aux, jac)
-    scalars = (jnp.sum(picks * acc), jnp.sum(damped), jnp.sum(rz_next))
+        sums[0] += damping[:, cols] * new_dir * new_dir
+        sums[1] += new_res * precon
+
+    acc = block_pass(picks, aux, jac, update)
+    scalars = (jnp.sum(picks * acc), jnp.sum(sums[0]), jnp.sum(sums[1]))
     pack_return(acc, aux[0:n_blk, :], scalars, stage, out)
 
 
-def sum_kernel(recv, out, *rest):
-    *ids_outs, turned, left, right = rest
+def sum_kernel(first, recv, *rest):
+    if first:
+        out, ids_out, right, turned, fine, left = rest
+    else:
+        right, out, turned, fine, left = rest
     n_x = recv.shape[1]
     n_blk = LANES // ROWS
     n_proj = 9
     sub = lax.broadcasted_iota(jnp.int32, (n_blk, LANES), 0)
     deep = lax.broadcasted_iota(jnp.int32, (LANES, LANES), 0)
     half = n_proj * 8
+
+    def spread(table, x, base, high):
+        lines = [
+            jnp.broadcast_to(table[x, base + k : base + k + 1, :], (8, LANES))
+            for k in range(n_proj)
+        ]
+        return jnp.concatenate([jnp.where(high, line, 0.0) for line in lines], axis=0)
+
     for x in range(n_x):
-        turned[x] = recv[:, x].reshape(LANES, LANES).T
+        values = recv[:, x].reshape(LANES, LANES).T
+        turned[x] = values
+        fine[x] = values - values.astype(BF16).astype(F32)
         for b in range(n_blk):
             at = (x * n_blk + b) * LANES
             cols = slice(at, at + LANES)
             base = b * ROWS
             ids = turned[x, base + n_proj : base + n_proj + 1, :].astype(jnp.int32)
             high = jnp.broadcast_to(ids >> 7, (8, LANES)) == sub
-            low = jnp.broadcast_to(ids & 127, (LANES, LANES)) == deep
-            spread = jnp.concatenate(
-                [
-                    jnp.where(
-                        high,
-                        jnp.broadcast_to(turned[x, base + k : base + k + 1, :], (8, LANES)),
-                        0.0,
-                    )
-                    for k in range(n_proj)
-                ],
-                axis=0,
-            )
-            coarse = spread.astype(BF16)
-            left[0:half, cols] = coarse
-            left[80 : 80 + half, cols] = (spread - coarse.astype(F32)).astype(BF16)
-            right[:, cols] = jnp.where(low, 1.0, 0.0).astype(BF16)
+            left[0:half, cols] = spread(turned, x, base, high).astype(BF16)
+            left[80 : 80 + half, cols] = spread(fine, x, base, high).astype(BF16)
+            if first:
+                low = jnp.broadcast_to(ids & 127, (LANES, LANES)) == deep
+                right[:, cols] = jnp.where(low, 1.0, 0.0).astype(BF16)
     summed = lax.dot_general(left[...], right[...], NT, preferred_element_type=F32)
     out[0:half, :] = summed[0:half] + summed[80 : 80 + half]
     per = recv.shape[2]
@@ -193,7 +204,7 @@
         line = turned[0, n_proj + 1 + i : n_proj + 2 + i, :]
         out[half + i : half + i + 1, :] = jnp.full((1, LANES), total_of(line, per), F32)
     out[half + 3 : half + 8, :] = jnp.zeros((5, LANES), F32)
-    for ids_out in ids_outs:
+    if first:
         ids_out[...] = turned[lax.axis_index("x"), pl.ds(n_proj, n_blk, stride=ROWS), :].astype(jnp.int32)
 
 
@@ -278,18 +289,34 @@
 
 
 def last_kernel(
-    own, partner, proj, damping, alpha_in, first_dir, res, dirn, sol_out, res_out, weights
+    own, partner, proj, damping, alpha_in, first_dir, res, dirn,
+    sol_hbm, res_hbm, weights, sol_out, res_out, sem,
 ):
     weights[...] = own[...] + partner[...]
     rows = proj.shape[0] * 8
     curve = weights[rows : rows + 1, :] + own[rows + 1 : rows + 2, :]
     alpha = own[rows + 2 : rows + 3, :] / curve
     alpha_first = alpha_in[0:1, :]
-    for h in range(damping.shape[1] // LANES):
+    chunks = damping.shape[1] // LANES
+    copies = []
+
+    def send(end):
+        cols = pl.ds((end - 2) * LANES, 2 * LANES)
+        for here, there in ((sol_out, sol_hbm), (res_out, res_hbm)):
+            copy = pltpu.make_async_copy(here.at[:, cols], there.at[:, cols], sem.at[len(copies)])
+            copy.start()
+            copies.append(copy)
+
+    for h in range(chunks):
         cols = slice(h * LANES, (h + 1) * LANES)
         image = lifted(proj, weights, h) + damping[:, cols] * dirn[:, cols]
         sol_out[:, cols] = alpha_first * first_dir[:, cols] + alpha * dirn[:, cols]
         res_out[:, cols] = res[:, cols] - alpha * image
+        if h >= 2 and h % 2 == 0:
+            send(h)
+    send(chunks)
+    for copy in copies:
+        copy.wait()
 
 
 def local(jacobian, splat_ids, pix_residual, live_blocks, proj_jac, damping, precond):
@@ -306,22 +333,25 @@
     weights = pltpu.VMEM((80, LANES), F32)
     table = pltpu.VMEM((16, g_dev), F32)
 
-    def to_owners(message, indices):
+    def to_owners(message, right):
         flat = message.reshape(n_scene * n_x, per, LANES)
         got = lax.all_to_all(flat, ("scene", "x"), 0, 0, tiled=True)
-        own, *index = call(
-            sum_kernel,
-            (sums,) + (whole((n_blk, LANES), jnp.int32),) * indices,
-            [VMEM],
+        first = right is None
+        wide_k = n_x * n_blk * LANES
+        extra = (whole((n_blk, LANES), jnp.int32), whole((LANES, wide_k), BF16))
+        own, *kept = call(
+            functools.partial(sum_kernel, first),
+            (sums,) + (extra if first else ()),
+            [VMEM] * (1 if first else 2),
             [
                 pltpu.VMEM((n_x, LANES, LANES), F32),
-                pltpu.VMEM((160, n_x * n_blk * LANES), BF16),
-                pltpu.VMEM((LANES, n_x * n_blk * LANES), BF16),
+                pltpu.VMEM((n_x, LANES, LANES), F32),
+                pltpu.VMEM((160, wide_k), BF16),
             ],
-            2147483648,
-        )(got.reshape(n_scene, n_x, per, LANES))
+            1 << 31,
+        )(got.reshape(n_scene, n_x, per, LANES), *(() if first else (right,)))
         partner = lax.ppermute(own, "core", [(0, 1), (1, 0)])
-        return own, partner, *index
+        return own, partner, *kept
 
     def to_blocks(message):
         return lax.all_to_all(message, "scene", 0, 0, tiled=True)
@@ -339,7 +369,7 @@
             pltpu.SemaphoreType.DMA((3,)),
         ],
     )(*map(in_hbm, (live_blocks.reshape(1, -1), jacobian, pix_residual, splat_ids)))
-    own, partner, index = to_owners(message, 1)
+    own, partner, index, right = to_owners(message, None)
     message, res, first_dir = call(
         start_kernel, (msg, state, state), [VMEM] * 5, [weights, table, square]
     )(own, partner, proj_jac, precond, index)
@@ -350,7 +380,7 @@
         [VMEM] * 3,
         [square, square],
     )(jac, aux, arrived)
-    own, partner = to_owners(message, 0)
+    own, partner = to_owners(message, right)
     message, image = call(step_kernel, (msg, state), [VMEM] * 8, [weights, table, square])(
         own, partner, proj_jac, precond, damping, index, res, first_dir
     )
@@ -361,8 +391,15 @@
         [VMEM] * 9,
         [square, square],
     )(jac, aux, arrived, picks, res, first_dir, image, precond, damping)
-    own, partner = to_owners(message, 0)
-    return call(last_kernel, (state, state), [VMEM] * 8, [weights])(
+    own, partner = to_owners(message, right)
+    held = pltpu.VMEM((n_par, g_dev), F32)
+    return call(
+        last_kernel,
+        (state, state),
+        [VMEM] * 8,
+        [weights, held, held, pltpu.SemaphoreType.DMA((2 * (g_dev // (2 * LANES)),))],
+        out_space=HBM,
+    )(
         own, partner, proj_jac, damping, alpha, first_dir, res, second_dir
     )
 

time: 94.8 us -> 93.5 us (0.986)
  Pallas kernels: 14.3 us -> 13 us
where the time goes in v5:
time: 93.5 us; the launch traced here: 93.1 us
  blocking collectives  68.8 us (74%)
  Pallas kernels  13 us (14%)
  starting transfers between devices  8.03 us (9%)
  waiting for transfers between devices  2.61 us (3%)
    all_to_all x3, blocking collectives, to_owners(): got = lax.all_to_all(flat, ('scene', 'x'), 0, 0, tiled=True)  50.2 us
    all_to_all x2, blocking collectives, to_blocks(): return lax.all_to_all(message, 'scene', 0, 0, tiled=True)  18.6 us
    ppermute x3, starting transfers between devices, to_owners(): partner = lax.ppermute(own, 'core', [(0, 1), (1, 0)])  8.03 us
    pallas_call x1, Pallas kernels, local(): call(rhs_kernel, (wide, whole(jacobian.shape, BF16), whole((2 * n_blk, LA...  3.27 us
    ppermute x3, waiting for transfers between devices, to_owners(): partner = lax.ppermute(own, 'core', [(0, 1), (1, 0)])  2.61 us
    pallas_call x1, Pallas kernels, local(): call(second_kernel, (wide, state, state, f32(8, LANES)), [VMEM] * 9, [squ...  2.41 us
    pallas_call x3, Pallas kernels, to_owners(): call(functools.partial(sum_kernel, first), (sums,) + (extra if first else...  2.35 us
    pallas_call x1, Pallas kernels, local(): call(first_kernel, (wide, f32(n_blk, n_col)), [VMEM] * 3, [square, square])  2.09 us
  transfers between devices with their start and end apart: 3, of which 3 were waited for; matrix products, arithmetic and copies ran while one was open for 0% of the time, Pallas kernels for 0%

profile of v5, /device:TPU:1, one launch (start us, length us, event | category | flops | bytes accessed | tf_op | source)
XLA Modules:
  0.0 93.1 jit_solution(6385724282417172015)
XLA Ops:
  0.6 3.3 %shard_map.86 = (f32[16,4,8,128]{3,2,1,0:T(8,128)S(1)}, bf16[8,256,1152]{2,1,0:T(8,128)(2,1)S(1)}, s32[16,128]{1,0:T(8,128)S(1)}) custom-call(s32[1,128]{1,0:T(1,128)} %bitcast.13, bf16[8,256,1152]{2,1,0:T(8,128)(2,1)} %jac.1, bf16[8,256]{1,0:T(8,128)(2,1)} %pix.1, s32[8,128]{1,0:T(8,128)} %ids.1), custom_call_target="tpu_custom_call" | custom-call | flops 1048576 | bytes 1048576 | tf_op jit(solution)/shard_map/pallas_call | solution.py:359
  3.9 0.0 copy-start
  3.9 0.0 copy-start.2
  3.9 21.4 %all_to_all.25 = f32[64,8,128]{2,1,0:T(8,128)S(1)} all-to-all(f32[64,8,128]{2,1,0:T(8,128)S(1)} %bitcast.9), channel_id=1, replica_groups=mesh['scene'=16,'x'=4,'core'=2] {'scene','x'}, dimensions={0} | all-to-all | bytes 524288 | tf_op jit(solution)/shard_map/all_to_all | solution.py:338
  25.3 1.0 %shard_map.87 = (f32[80,128]{1,0:T(8,128)S(1)}, s32[8,128]{1,0:T(8,128)S(1)}, bf16[128,4096]{1,0:T(8,128)(2,1)S(1)}) custom-call(f32[16,4,8,128]{3,2,1,0:T(8,128)S(1)} %bitcast.8), custom_call_target="tpu_custom_call" | custom-call | flops 2147483648 | bytes 1048576 | tf_op jit(solution)/shard_map/pallas_call | solution.py:342
  26.3 2.1 %collective-permute-start = (f32[80,128]{1,0:T(8,128)S(1)}, f32[80,128]{1,0:T(8,128)S(1)}, u32[]{:S(2)}, u32[]{:S(2)}) collective-permute-start(f32[80,128]{1,0:T(8,128)S(1)} %get-tuple-element.22.own), channel_id=1, source_target_pairs={{0,1},{1,0},{2,3},{3,2},{4,5},{5,4},{6,7},{7,6},{8,9},{9,8},{10,11... | collective-permute-start | bytes 122888 | tf_op jit(solution)/shard_map/ppermute | solution.py:353
  28.5 0.9 collective-permute-done.partner
  29.4 0.8 shard_map.88
  30.2 9.3 %all_to_all.26.recv = f32[16,8,128]{2,1,0:T(8,128)S(1)} all-to-all(f32[16,8,128]{2,1,0:T(8,128)S(1)} %get-tuple-element.24), channel_id=1, replica_groups=mesh['scene'=16,'x'=4,'core'=2] {'scene'}, dimensions={0} | all-to-all | bytes 131072 | tf_op jit(solution)/shard_map/all_to_all | solution.py:357
  39.4 2.1 %shard_map.89 = (f32[16,4,8,128]{3,2,1,0:T(8,128)S(1)}, f32[8,1152]{1,0:T(8,128)S(1)}) custom-call(bf16[8,256,1152]{2,1,0:T(8,128)(2,1)S(1)} %get-tuple-element.19.jac, s32[16,128]{1,0:T(8,128)S(1)} %get-tuple-element.20.aux, f32[16,8,128]{2,1,0:T(8,128)S(1)} %all_to_all.26.recv), custom_call_target="tpu_custom_call" | custom-call | flops 1048576 | bytes 1048576 | tf_op jit(solution)/shard_map/pallas_call | solution.py:377
  41.5 0.0 copy-start.1
  41.6 14.5 %all_to_all.27 = f32[64,8,128]{2,1,0:T(8,128)S(1)} all-to-all(f32[64,8,128]{2,1,0:T(8,128)S(1)} %bitcast.10), channel_id=1, replica_groups=mesh['scene'=16,'x'=4,'core'=2] {'scene','x'}, dimensions={0} | all-to-all | bytes 524288 | tf_op jit(solution)/shard_map/all_to_all | solution.py:338
  56.0 0.7 shard_map.90.own
  56.7 2.9 %collective-permute-start.1 = (f32[80,128]{1,0:T(8,128)S(1)}, f32[80,128]{1,0:T(8,128)S(1)}, u32[]{:S(2)}, u32[]{:S(2)}) collective-permute-start(f32[80,128]{1,0:T(8,128)S(1)} %shard_map.90.own), channel_id=1, source_target_pairs={{0,1},{1,0},{2,3},{3,2},{4,5},{5,4},{6,7},{7,6},{8,9},{9,8},{10,11... | collective-permute-start | bytes 122888 | tf_op jit(solution)/shard_map/ppermute | solution.py:353
  59.7 0.9 collective-permute-done.1.partner
  60.5 0.0 copy-done.1
  60.5 1.0 %shard_map.91 = (f32[16,8,128]{2,1,0:T(8,128)S(1)}, f32[59,1024]{1,0:T(8,128)S(1)}) custom-call(f32[80,128]{1,0:T(8,128)S(1)} %shard_map.90.own, f32[80,128]{1,0:T(8,128)S(1)} %collective-permute-done.1.partner, bf16[9,59,1024]{2,1,0:T(8,128)(2,1)S(1)} %copy-done, f32[59,1024]{1,0:T(8,128)S(1)} %copy-done.2, f32[59,1024]{1,0:T(8,128)S(1)} %copy-done.1, ...), custom_call_target="tpu_custom_call" | custom-call | flops 1048576 | bytes 1048576 | tf_op jit(solution)/shard_map/pallas_call | solution.py:384
  61.5 9.3 %all_to_all.28.recv = f32[16,8,128]{2,1,0:T(8,128)S(1)} all-to-all(f32[16,8,128]{2,1,0:T(8,128)S(1)} %get-tuple-element.29), channel_id=1, replica_groups=mesh['scene'=16,'x'=4,'core'=2] {'scene'}, dimensions={0} | all-to-all | bytes 131072 | tf_op jit(solution)/shard_map/all_to_all | solution.py:357
  70.8 2.4 %shard_map.92 = (f32[16,4,8,128]{3,2,1,0:T(8,128)S(1)}, f32[59,1024]{1,0:T(8,128)S(1)}, f32[59,1024]{1,0:T(8,128)S(1)}, f32[8,128]{1,0:T(8,128)S(1)}) custom-call(bf16[8,256,1152]{2,1,0:T(8,128)(2,1)S(1)} %get-tuple-element.19.jac, s32[16,128]{1,0:T(8,128)S(1)} %get-tuple-element.20.aux, f32[16,8,128]{2,1,0:T(8,128)S(1)} %all_to_all.28.recv, ...), custom_call_target="tpu_custom_call" | custom-call | flops 1048576 | bytes 1048576 | tf_op jit(solution)/shard_map/pallas_call | solution.py:388
  73.2 14.4 %all_to_all.29 = f32[64,8,128]{2,1,0:T(8,128)S(1)} all-to-all(f32[64,8,128]{2,1,0:T(8,128)S(1)} %bitcast.7), channel_id=1, replica_groups=mesh['scene'=16,'x'=4,'core'=2] {'scene','x'}, dimensions={0} | all-to-all | bytes 524288 | tf_op jit(solution)/shard_map/all_to_all | solution.py:338
  87.6 0.7 shard_map.93.own
  88.2 2.9 %collective-permute-start.2 = (f32[80,128]{1,0:T(8,128)S(1)}, f32[80,128]{1,0:T(8,128)S(1)}, u32[]{:S(2)}, u32[]{:S(2)}) collective-permute-start(f32[80,128]{1,0:T(8,128)S(1)} %shard_map.93.own), channel_id=1, source_target_pairs={{0,1},{1,0},{2,3},{3,2},{4,5},{5,4},{6,7},{7,6},{8,9},{9,8},{10,11... | collective-permute-start | bytes 122888 | tf_op jit(solution)/shard_map/ppermute | solution.py:353
  91.2 0.9 collective-permute-done.2.partner
  92.0 1.1 %shard_map.94 = (f32[59,1024]{1,0:T(8,128)}, f32[59,1024]{1,0:T(8,128)}) custom-call(f32[80,128]{1,0:T(8,128)S(1)} %shard_map.93.own, f32[80,128]{1,0:T(8,128)S(1)} %collective-permute-done.2.partner, bf16[9,59,1024]{2,1,0:T(8,128)(2,1)S(1)} %copy-done, f32[59,1024]{1,0:T(8,128)S(1)} %copy-done.1, f32[8,128]{1,0:T(8,128)S(1)} %get-tuple-element.33.alpha_in, ...), custom_call_target="tpu_custom_call" | custom-call | flops 1048576 | bytes 1048576 | tf_op jit(solution)/shard_map/pallas_call | solution.py:396
  (2 shorter events, 0.0 us)
Async XLA Ops:
  3.9 25.4 %copy-start = (bf16[9,59,1024]{2,1,0:T(8,128)(2,1)S(1)}, bf16[9,59,1024]{2,1,0:T(8,128)(2,1)}, u32[]{:S(2)}) copy-start(bf16[9,59,1024]{2,1,0:T(8,128)(2,1)} %proj.5) | copy-start | bytes 3262468
  3.9 25.4 %copy-start.2 = (f32[59,1024]{1,0:T(8,128)S(1)}, f32[59,1024]{1,0:T(8,128)}, u32[]{:S(2)}) copy-start(f32[59,1024]{1,0:T(8,128)} %precond.5) | copy-start | bytes 724996
  26.3 3.0 %collective-permute-start = (f32[80,128]{1,0:T(8,128)S(1)}, f32[80,128]{1,0:T(8,128)S(1)}, u32[]{:S(2)}, u32[]{:S(2)}) collective-permute-start(f32[80,128]{1,0:T(8,128)S(1)} %get-tuple-element.22.own), channel_id=1, source_target_pairs={{0,1},{1,0},{2,3},{3,2},{4,5},{5,4},{6,7},{7,6},{8,9},{9,8},{10,11... | collective-permute-start | bytes 122888 | tf_op jit(solution)/shard_map/ppermute | solution.py:353
  41.5 19.0 %copy-start.1 = (f32[59,1024]{1,0:T(8,128)S(1)}, f32[59,1024]{1,0:T(8,128)}, u32[]{:S(2)}) copy-start(f32[59,1024]{1,0:T(8,128)} %damping.5) | copy-start | bytes 724996
  56.7 3.8 %collective-permute-start.1 = (f32[80,128]{1,0:T(8,128)S(1)}, f32[80,128]{1,0:T(8,128)S(1)}, u32[]{:S(2)}, u32[]{:S(2)}) collective-permute-start(f32[80,128]{1,0:T(8,128)S(1)} %shard_map.90.own), channel_id=1, source_target_pairs={{0,1},{1,0},{2,3},{3,2},{4,5},{5,4},{6,7},{7,6},{8,9},{9,8},{10,11... | collective-permute-start | bytes 122888 | tf_op jit(solution)/shard_map/ppermute | solution.py:353
  88.2 3.8 %collective-permute-start.2 = (f32[80,128]{1,0:T(8,128)S(1)}, f32[80,128]{1,0:T(8,128)S(1)}, u32[]{:S(2)}, u32[]{:S(2)}) collective-permute-start(f32[80,128]{1,0:T(8,128)S(1)} %shard_map.93.own), channel_id=1, source_target_pairs={{0,1},{1,0},{2,3},{3,2},{4,5},{5,4},{6,7},{7,6},{8,9},{9,8},{10,11... | collective-permute-start | bytes 122888 | tf_op jit(solution)/shard_map/ppermute | solution.py:353

commit v6 on v5

--- a/solution.py
+++ b/solution.py
@@ -86,14 +86,33 @@
     pack_return(acc, local_ids, (), stage, out)
 
 
-def block_pass(picks, aux, jac, beside=None):
+def lane_image(jac, b, line, ones):
+    pieces = []
+    for top in range(0, jac.shape[1], 64):
+        folded = jnp.zeros((64, LANES), F32)
+        for at in range(0, jac.shape[2], LANES):
+            tile = jac[b, top : top + 64, at : at + LANES].astype(F32)
+            folded += tile * line[:, at : at + LANES]
+        high = folded.astype(BF16)
+        pieces.append(jnp.concatenate([high, (folded - high.astype(F32)).astype(BF16)], axis=1))
+    return lax.dot_general(
+        ones, jnp.concatenate(pieces, axis=0), NT, preferred_element_type=F32
+    )
+
+
+def block_pass(picks, aux, jac, by_lanes, beside=None):
     n_blk, n_pix = jac.shape[:2]
     row = lax.broadcasted_iota(jnp.int32, (n_blk, n_pix), 0)
     live = row < aux[n_blk : n_blk + 1, 0:1]
     chosen = picks.astype(BF16)
+    rounded = chosen.astype(F32)
+    ones = jnp.ones((n_blk, 2 * LANES), BF16)
     signals = []
     for b in range(n_blk):
-        image = lax.dot_general(chosen, jac[b], NT, preferred_element_type=F32)
+        if (b * by_lanes) // n_blk != ((b + 1) * by_lanes) // n_blk:
+            image = lane_image(jac, b, rounded[b : b + 1, :], ones)
+        else:
+            image = lax.dot_general(chosen, jac[b], NT, preferred_element_type=F32)
         if beside is not None:
             beside(b)
         signals.append(jnp.where((row == b) & live, image, 0.0).astype(BF16))
@@ -117,7 +136,7 @@
     n_proj = jac.shape[2] // LANES
     picks = unpack_picks(recv, turned, n_blk, n_proj)
     picks_out[...] = picks
-    acc = block_pass(picks, aux, jac)
+    acc = block_pass(picks, aux, jac, 5)
     pack_return(acc, aux[0:n_blk, :], (), stage, out)
 
 
@@ -154,7 +173,7 @@
         sums[0] += damping[:, cols] * new_dir * new_dir
         sums[1] += new_res * precon
 
-    acc = block_pass(picks, aux, jac, update)
+    acc = block_pass(picks, aux, jac, 5, update)
     scalars = (jnp.sum(picks * acc), jnp.sum(sums[0]), jnp.sum(sums[1]))
     pack_return(acc, aux[0:n_blk, :], scalars, stage, out)
 

time: 93.5 us -> 92.6 us (level)
  no operation moved by 1% of the time
where the time goes in v6:
time: 92.6 us; the launch traced here: 92.3 us
  blocking collectives  68.8 us (74%)
  Pallas kernels  12.1 us (13%)
  starting transfers between devices  8.02 us (9%)
  waiting for transfers between devices  2.61 us (3%)
    all_to_all x3, blocking collectives, to_owners(): got = lax.all_to_all(flat, ('scene', 'x'), 0, 0, tiled=True)  50.2 us
    all_to_all x2, blocking collectives, to_blocks(): return lax.all_to_all(message, 'scene', 0, 0, tiled=True)  18.6 us
    ppermute x3, starting transfers between devices, to_owners(): partner = lax.ppermute(own, 'core', [(0, 1), (1, 0)])  8.02 us
    pallas_call x1, Pallas kernels, local(): call(rhs_kernel, (wide, whole(jacobian.shape, BF16), whole((2 * n_blk, LA...  3.27 us
    ppermute x3, waiting for transfers between devices, to_owners(): partner = lax.ppermute(own, 'core', [(0, 1), (1, 0)])  2.61 us
    pallas_call x3, Pallas kernels, to_owners(): call(functools.partial(sum_kernel, first), (sums,) + (extra if first else...  2.35 us
    pallas_call x1, Pallas kernels, local(): call(second_kernel, (wide, state, state, f32(8, LANES)), [VMEM] * 9, [squ...  2.01 us
  transfers between devices with their start and end apart: 3, of which 3 were waited for; matrix products, arithmetic and copies ran while one was open for 0% of the time, Pallas kernels for 0%

profile of v6, /device:TPU:1, one launch (start us, length us, event | category | flops | bytes accessed | tf_op | source)
XLA Modules:
  0.0 92.3 jit_solution(15888465706730320072)
XLA Ops:
  0.6 3.3 %shard_map.86 = (f32[16,4,8,128]{3,2,1,0:T(8,128)S(1)}, bf16[8,256,1152]{2,1,0:T(8,128)(2,1)S(1)}, s32[16,128]{1,0:T(8,128)S(1)}) custom-call(s32[1,128]{1,0:T(1,128)} %bitcast.13, bf16[8,256,1152]{2,1,0:T(8,128)(2,1)} %jac.1, bf16[8,256]{1,0:T(8,128)(2,1)} %pix.1, s32[8,128]{1,0:T(8,128)} %ids.1), custom_call_target="tpu_custom_call" | custom-call | flops 1048576 | bytes 1048576 | tf_op jit(solution)/shard_map/pallas_call | solution.py:378
  3.9 0.0 copy-start
  3.9 0.0 copy-start.2
  3.9 21.4 %all_to_all.25 = f32[64,8,128]{2,1,0:T(8,128)S(1)} all-to-all(f32[64,8,128]{2,1,0:T(8,128)S(1)} %bitcast.9), channel_id=1, replica_groups=mesh['scene'=16,'x'=4,'core'=2] {'scene','x'}, dimensions={0} | all-to-all | bytes 524288 | tf_op jit(solution)/shard_map/all_to_all | solution.py:357
  25.3 1.0 %shard_map.87 = (f32[80,128]{1,0:T(8,128)S(1)}, s32[8,128]{1,0:T(8,128)S(1)}, bf16[128,4096]{1,0:T(8,128)(2,1)S(1)}) custom-call(f32[16,4,8,128]{3,2,1,0:T(8,128)S(1)} %bitcast.8), custom_call_target="tpu_custom_call" | custom-call | flops 2147483648 | bytes 1048576 | tf_op jit(solution)/shard_map/pallas_call | solution.py:361
  26.3 2.1 %collective-permute-start = (f32[80,128]{1,0:T(8,128)S(1)}, f32[80,128]{1,0:T(8,128)S(1)}, u32[]{:S(2)}, u32[]{:S(2)}) collective-permute-start(f32[80,128]{1,0:T(8,128)S(1)} %get-tuple-element.22.own), channel_id=1, source_target_pairs={{0,1},{1,0},{2,3},{3,2},{4,5},{5,4},{6,7},{7,6},{8,9},{9,8},{10,11... | collective-permute-start | bytes 122888 | tf_op jit(solution)/shard_map/ppermute | solution.py:372
  28.5 0.9 collective-permute-done.partner
  29.4 0.0 copy-done
  29.4 0.8 shard_map.88
  30.2 9.3 %all_to_all.26.recv = f32[16,8,128]{2,1,0:T(8,128)S(1)} all-to-all(f32[16,8,128]{2,1,0:T(8,128)S(1)} %get-tuple-element.24), channel_id=1, replica_groups=mesh['scene'=16,'x'=4,'core'=2] {'scene'}, dimensions={0} | all-to-all | bytes 131072 | tf_op jit(solution)/shard_map/all_to_all | solution.py:376
  39.4 1.7 %shard_map.89 = (f32[16,4,8,128]{3,2,1,0:T(8,128)S(1)}, f32[8,1152]{1,0:T(8,128)S(1)}) custom-call(bf16[8,256,1152]{2,1,0:T(8,128)(2,1)S(1)} %get-tuple-element.19.jac, s32[16,128]{1,0:T(8,128)S(1)} %get-tuple-element.20.aux, f32[16,8,128]{2,1,0:T(8,128)S(1)} %all_to_all.26.recv), custom_call_target="tpu_custom_call" | custom-call | flops 1048576 | bytes 1048576 | tf_op jit(solution)/shard_map/pallas_call | solution.py:396
  41.1 0.0 copy-start.1
  41.1 14.5 %all_to_all.27 = f32[64,8,128]{2,1,0:T(8,128)S(1)} all-to-all(f32[64,8,128]{2,1,0:T(8,128)S(1)} %bitcast.10), channel_id=1, replica_groups=mesh['scene'=16,'x'=4,'core'=2] {'scene','x'}, dimensions={0} | all-to-all | bytes 524288 | tf_op jit(solution)/shard_map/all_to_all | solution.py:357
  55.6 0.7 shard_map.90.own
  56.3 2.9 %collective-permute-start.1 = (f32[80,128]{1,0:T(8,128)S(1)}, f32[80,128]{1,0:T(8,128)S(1)}, u32[]{:S(2)}, u32[]{:S(2)}) collective-permute-start(f32[80,128]{1,0:T(8,128)S(1)} %shard_map.90.own), channel_id=1, source_target_pairs={{0,1},{1,0},{2,3},{3,2},{4,5},{5,4},{6,7},{7,6},{8,9},{9,8},{10,11... | collective-permute-start | bytes 122888 | tf_op jit(solution)/shard_map/ppermute | solution.py:372
  59.2 0.9 collective-permute-done.1.partner
  60.1 1.0 %shard_map.91 = (f32[16,8,128]{2,1,0:T(8,128)S(1)}, f32[59,1024]{1,0:T(8,128)S(1)}) custom-call(f32[80,128]{1,0:T(8,128)S(1)} %shard_map.90.own, f32[80,128]{1,0:T(8,128)S(1)} %collective-permute-done.1.partner, bf16[9,59,1024]{2,1,0:T(8,128)(2,1)S(1)} %copy-done, f32[59,1024]{1,0:T(8,128)S(1)} %copy-done.2, f32[59,1024]{1,0:T(8,128)S(1)} %copy-done.1, ...), custom_call_target="tpu_custom_call" | custom-call | flops 1048576 | bytes 1048576 | tf_op jit(solution)/shard_map/pallas_call | solution.py:403
  61.1 9.3 %all_to_all.28.recv = f32[16,8,128]{2,1,0:T(8,128)S(1)} all-to-all(f32[16,8,128]{2,1,0:T(8,128)S(1)} %get-tuple-element.29), channel_id=1, replica_groups=mesh['scene'=16,'x'=4,'core'=2] {'scene'}, dimensions={0} | all-to-all | bytes 131072 | tf_op jit(solution)/shard_map/all_to_all | solution.py:376
  70.4 2.0 %shard_map.92 = (f32[16,4,8,128]{3,2,1,0:T(8,128)S(1)}, f32[59,1024]{1,0:T(8,128)S(1)}, f32[59,1024]{1,0:T(8,128)S(1)}, f32[8,128]{1,0:T(8,128)S(1)}) custom-call(bf16[8,256,1152]{2,1,0:T(8,128)(2,1)S(1)} %get-tuple-element.19.jac, s32[16,128]{1,0:T(8,128)S(1)} %get-tuple-element.20.aux, f32[16,8,128]{2,1,0:T(8,128)S(1)} %all_to_all.28.recv, ...), custom_call_target="tpu_custom_call" | custom-call | flops 1048576 | bytes 1048576 | tf_op jit(solution)/shard_map/pallas_call | solution.py:407
  72.4 14.4 %all_to_all.29 = f32[64,8,128]{2,1,0:T(8,128)S(1)} all-to-all(f32[64,8,128]{2,1,0:T(8,128)S(1)} %bitcast.7), channel_id=1, replica_groups=mesh['scene'=16,'x'=4,'core'=2] {'scene','x'}, dimensions={0} | all-to-all | bytes 524288 | tf_op jit(solution)/shard_map/all_to_all | solution.py:357
  86.7 0.7 shard_map.93.own
  87.4 2.9 %collective-permute-start.2 = (f32[80,128]{1,0:T(8,128)S(1)}, f32[80,128]{1,0:T(8,128)S(1)}, u32[]{:S(2)}, u32[]{:S(2)}) collective-permute-start(f32[80,128]{1,0:T(8,128)S(1)} %shard_map.93.own), channel_id=1, source_target_pairs={{0,1},{1,0},{2,3},{3,2},{4,5},{5,4},{6,7},{7,6},{8,9},{9,8},{10,11... | collective-permute-start | bytes 122888 | tf_op jit(solution)/shard_map/ppermute | solution.py:372
  90.3 0.9 collective-permute-done.2.partner
  91.2 1.1 %shard_map.94 = (f32[59,1024]{1,0:T(8,128)}, f32[59,1024]{1,0:T(8,128)}) custom-call(f32[80,128]{1,0:T(8,128)S(1)} %shard_map.93.own, f32[80,128]{1,0:T(8,128)S(1)} %collective-permute-done.2.partner, bf16[9,59,1024]{2,1,0:T(8,128)(2,1)S(1)} %copy-done, f32[59,1024]{1,0:T(8,128)S(1)} %copy-done.1, f32[8,128]{1,0:T(8,128)S(1)} %get-tuple-element.33.alpha_in, ...), custom_call_target="tpu_custom_call" | custom-call | flops 1048576 | bytes 1048576 | tf_op jit(solution)/shard_map/pallas_call | solution.py:415
  (2 shorter events, 0.0 us)
Async XLA Ops:
  3.9 25.4 %copy-start = (bf16[9,59,1024]{2,1,0:T(8,128)(2,1)S(1)}, bf16[9,59,1024]{2,1,0:T(8,128)(2,1)}, u32[]{:S(2)}) copy-start(bf16[9,59,1024]{2,1,0:T(8,128)(2,1)} %proj.5) | copy-start | bytes 3262468
  3.9 25.4 %copy-start.2 = (f32[59,1024]{1,0:T(8,128)S(1)}, f32[59,1024]{1,0:T(8,128)}, u32[]{:S(2)}) copy-start(f32[59,1024]{1,0:T(8,128)} %precond.5) | copy-start | bytes 724996
  26.3 3.0 %collective-permute-start = (f32[80,128]{1,0:T(8,128)S(1)}, f32[80,128]{1,0:T(8,128)S(1)}, u32[]{:S(2)}, u32[]{:S(2)}) collective-permute-start(f32[80,128]{1,0:T(8,128)S(1)} %get-tuple-element.22.own), channel_id=1, source_target_pairs={{0,1},{1,0},{2,3},{3,2},{4,5},{5,4},{6,7},{7,6},{8,9},{9,8},{10,11... | collective-permute-start | bytes 122888 | tf_op jit(solution)/shard_map/ppermute | solution.py:372
  41.1 19.0 %copy-start.1 = (f32[59,1024]{1,0:T(8,128)S(1)}, f32[59,1024]{1,0:T(8,128)}, u32[]{:S(2)}) copy-start(f32[59,1024]{1,0:T(8,128)} %damping.5) | copy-start | bytes 724996
  56.3 3.8 %collective-permute-start.1 = (f32[80,128]{1,0:T(8,128)S(1)}, f32[80,128]{1,0:T(8,128)S(1)}, u32[]{:S(2)}, u32[]{:S(2)}) collective-permute-start(f32[80,128]{1,0:T(8,128)S(1)} %shard_map.90.own), channel_id=1, source_target_pairs={{0,1},{1,0},{2,3},{3,2},{4,5},{5,4},{6,7},{7,6},{8,9},{9,8},{10,11... | collective-permute-start | bytes 122888 | tf_op jit(solution)/shard_map/ppermute | solution.py:372
  87.4 3.8 %collective-permute-start.2 = (f32[80,128]{1,0:T(8,128)S(1)}, f32[80,128]{1,0:T(8,128)S(1)}, u32[]{:S(2)}, u32[]{:S(2)}) collective-permute-start(f32[80,128]{1,0:T(8,128)S(1)} %shard_map.93.own), channel_id=1, source_target_pairs={{0,1},{1,0},{2,3},{3,2},{4,5},{5,4},{6,7},{7,6},{8,9},{9,8},{10,11... | collective-permute-start | bytes 122888 | tf_op jit(solution)/shard_map/ppermute | solution.py:372

commit v7 on v6

--- a/solution.py
+++ b/solution.py
@@ -76,7 +76,7 @@
     values = jnp.where(keep, pixels[...].astype(F32), 0.0)
     n_pix, n_col = jac.shape[1:]
     acc = jnp.zeros((n_blk, n_col), F32)
-    cut = n_blk * 3 // 4
+    cut = n_blk - 1
     for first, last in ((0, cut), (cut, n_blk)):
         signals = [jnp.where(row == b, values, 0.0).astype(BF16) for b in range(first, last)]
         for copy in copies[first:last]:
@@ -173,7 +173,7 @@
         sums[0] += damping[:, cols] * new_dir * new_dir
         sums[1] += new_res * precon
 
-    acc = block_pass(picks, aux, jac, 5, update)
+    acc = block_pass(picks, aux, jac, 4, update)
     scalars = (jnp.sum(picks * acc), jnp.sum(sums[0]), jnp.sum(sums[1]))
     pack_return(acc, aux[0:n_blk, :], scalars, stage, out)
 
@@ -240,18 +240,51 @@
 def projected(proj, field, h, table):
     cols = slice(h * LANES, (h + 1) * LANES)
     for k in range(proj.shape[0]):
-        table[k : k + 1, cols] = jnp.sum(
+        table[k * 8 + h : k * 8 + h + 1, :] = jnp.sum(
             proj[k, :, cols].astype(F32) * field, axis=0, keepdims=True
         )
 
 
+def pairs(n_proj):
+    return [(k, m) for k in range(n_proj) for m in range(k, n_proj)]
+
+
+def form_kernel(after, proj, precond, out):
+    del after
+    n_proj = proj.shape[0]
+    for h in range(precond.shape[1] // LANES):
+        cols = slice(h * LANES, (h + 1) * LANES)
+        tiles = [proj[k, :, cols].astype(F32) for k in range(n_proj)]
+        scaled = [tile * precond[:, cols] for tile in tiles]
+        for i, (k, m) in enumerate(pairs(n_proj)):
+            out[i * 8 + h : i * 8 + h + 1, :] = jnp.sum(
+                scaled[k] * tiles[m], axis=0, keepdims=True
+            )
+
+
+def blended(matrix, weights):
+    n_proj = 9
+    sums = [None] * n_proj
+
+    def add(k, tile, m):
+        term = tile * weights[m * 8 : m * 8 + 8, :]
+        sums[k] = term if sums[k] is None else sums[k] + term
+
+    for i, (k, m) in enumerate(pairs(n_proj)):
+        tile = matrix[i * 8 : i * 8 + 8, :]
+        add(k, tile, m)
+        if k != m:
+            add(m, tile, k)
+    return sums
+
+
 def lane_pick(table, low):
     return jnp.take_along_axis(table, low, axis=1, mode="promise_in_bounds")
 
 
 def send_picks(table, ids, scalars, stage, out):
     n_blk = ids.shape[0]
-    n_chunk = table.shape[1] // LANES
+    n_chunk = 8
     stage[...] = jnp.zeros_like(stage)
     index = ids[...]
     low = index & 127
@@ -261,50 +294,62 @@
         high_b = jnp.broadcast_to(high[b : b + 1, :], (8, LANES))
         got = jnp.zeros((8, LANES), F32)
         for h in range(n_chunk):
-            piece = lane_pick(table[0:8, h * LANES : (h + 1) * LANES], low_b)
+            piece = lane_pick(table[pl.ds(h, 8, stride=8), :], low_b)
             got = jnp.where(high_b == h, piece, got)
         stage[b * ROWS : b * ROWS + 8, :] = got
     got = jnp.zeros((n_blk, LANES), F32)
     for h in range(n_chunk):
-        line = jnp.broadcast_to(table[8:9, h * LANES : (h + 1) * LANES], (n_blk, LANES))
+        line = jnp.broadcast_to(table[64 + h : 65 + h, :], (n_blk, LANES))
         got = jnp.where(high == h, lane_pick(line, low), got)
     stage[pl.ds(8, n_blk, stride=ROWS), :] = got
     for i, value in enumerate(scalars):
-        stage[10 + i : 11 + i, :] = jnp.full((1, LANES), value, F32)
+        stage[10 + i : 11 + i, :] = jnp.broadcast_to(value, (1, LANES))
     out[...] = stage[...].T.reshape(out.shape)
 
 
-def start_kernel(own, partner, proj, precond, ids, out, res_out, dir_out, weights, table, stage):
+def start_kernel(own, partner, matrix, ids, out, weights, table, stage):
+    weights[...] = own[...] + partner[...]
+    for k, tile in enumerate(blended(matrix, weights)):
+        table[k * 8 : k * 8 + 8, :] = -tile
+    send_picks(table, ids, (), stage, out)
+
+
+def state_kernel(
+    after, own, partner, proj, precond, damping, res_out, dir_out, cross, rz_out, weights
+):
+    del after
     weights[...] = own[...] + partner[...]
     n_par, width = precond.shape
+    rz = jnp.zeros((n_par, LANES), F32)
     for h in range(width // LANES):
         cols = slice(h * LANES, (h + 1) * LANES)
         res = -lifted(proj, weights, h)
         dirn = precond[:, cols] * res
         res_out[:, cols] = res
         dir_out[:, cols] = dirn
-        projected(proj, dirn, h, table)
-    send_picks(table, ids, (), stage, out)
+        rz += res * dirn
+        projected(proj, precond[:, cols] * damping[:, cols] * dirn, h, cross)
+    rz_out[...] = jnp.full(rz_out.shape, jnp.sum(rz), F32)
 
 
 def step_kernel(
-    own, partner, proj, precond, damping, ids, res, dirn, out, image_out, weights, table, stage
+    own, partner, proj, precond, damping, matrix, cross, rz_in, ids, dirn,
+    out, image_out, weights, table, stage,
 ):
     weights[...] = own[...] + partner[...]
     n_par, width = precond.shape
-    rz = jnp.zeros((n_par, LANES), F32)
+    for k, tile in enumerate(blended(matrix, weights)):
+        table[k * 8 : k * 8 + 8, :] = tile + cross[k * 8 : k * 8 + 8, :]
     curve = jnp.zeros((n_par, LANES), F32)
     square = jnp.zeros((n_par, LANES), F32)
     for h in range(width // LANES):
         cols = slice(h * LANES, (h + 1) * LANES)
         image = lifted(proj, weights, h) + damping[:, cols] * dirn[:, cols]
         image_out[:, cols] = image
-        scaled = precond[:, cols] * image
-        projected(proj, scaled, h, table)
-        rz += res[:, cols] * dirn[:, cols]
         curve += dirn[:, cols] * image
-        square += scaled * image
-    send_picks(table, ids, (jnp.sum(rz), jnp.sum(curve), jnp.sum(square)), stage, out)
+        square += precond[:, cols] * image * image
+    scalars = (rz_in[0:1, :], jnp.sum(curve), jnp.sum(square))
+    send_picks(table, ids, scalars, stage, out)
 
 
 def last_kernel(
@@ -350,7 +395,7 @@
     square = pltpu.VMEM((LANES, LANES), F32)
     whole = jax.ShapeDtypeStruct
     weights = pltpu.VMEM((80, LANES), F32)
-    table = pltpu.VMEM((16, g_dev), F32)
+    table = pltpu.VMEM((72, LANES), F32)
 
     def to_owners(message, right):
         flat = message.reshape(n_scene * n_x, per, LANES)
@@ -389,9 +434,13 @@
         ],
     )(*map(in_hbm, (live_blocks.reshape(1, -1), jacobian, pix_residual, splat_ids)))
     own, partner, index, right = to_owners(message, None)
-    message, res, first_dir = call(
-        start_kernel, (msg, state, state), [VMEM] * 5, [weights, table, square]
-    )(own, partner, proj_jac, precond, index)
+    matrix = call(form_kernel, (f32(45 * 8, LANES),), [VMEM] * 3, (), 1 << 31)(
+        own, proj_jac, precond
+    )[0]
+    message = call(start_kernel, (msg,), [VMEM] * 4, [weights, table, square])(
+        own, partner, matrix, index
+    )[0]
+    first_own, first_partner = own, partner
     arrived = to_blocks(message)
     message, picks = call(
         first_kernel,
@@ -400,8 +449,11 @@
         [square, square],
     )(jac, aux, arrived)
     own, partner = to_owners(message, right)
-    message, image = call(step_kernel, (msg, state), [VMEM] * 8, [weights, table, square])(
-        own, partner, proj_jac, precond, damping, index, res, first_dir
+    res, first_dir, cross, rz = call(
+        state_kernel, (state, state, f32(72, LANES), f32(8, LANES)), [VMEM] * 6, [weights], 1 << 31
+    )(own, first_own, first_partner, proj_jac, precond, damping)
+    message, image = call(step_kernel, (msg, state), [VMEM] * 10, [weights, table, square])(
+        own, partner, proj_jac, precond, damping, matrix, cross, rz, index, first_dir
     )
     arrived = to_blocks(message)
     message, res, second_dir, alpha = call(

time: 92.6 us -> 92 us (level)
  waiting for transfers between devices: 2.61 us -> 1 us
  Pallas kernels: 12.1 us -> 13.4 us
    ppermute x3, waiting for transfers between devices: 2.61 us -> 1 us  [to_owners(): partner = lax.ppermute(own, 'core', [(0, 1), (1, 0)])]
    pallas_call x2 -> x4, Pallas kernels: 1.74 us -> 2.79 us  [the longest x1 1.22 us: local(): call(form_kernel, (f32(45 * 8, LANES),), [VMEM] * 3, (), 1 << 31)]
  transfers between devices with their start and end apart: 3 -> 3, of which waited for: 3 -> 2; matrix products, arithmetic and copies ran while one was open for 0% -> 0% of each run, Pallas kernels for 0% -> 2%
where the time goes in v7:
time: 92 us; the launch traced here: 91.7 us
  blocking collectives  68.8 us (75%)
  Pallas kernels  13.4 us (15%)
  starting transfers between devices  7.72 us (8%)
  waiting for transfers between devices  1 us (1%)
    all_to_all x3, blocking collectives, to_owners(): got = lax.all_to_all(flat, ('scene', 'x'), 0, 0, tiled=True)  50.2 us
    all_to_all x2, blocking collectives, to_blocks(): return lax.all_to_all(message, 'scene', 0, 0, tiled=True)  18.6 us
    ppermute x3, starting transfers between devices, to_owners(): partner = lax.ppermute(own, 'core', [(0, 1), (1, 0)])  7.72 us
    pallas_call x1, Pallas kernels, local(): call(rhs_kernel, (wide, whole(jacobian.shape, BF16), whole((2 * n_blk, LA...  3.38 us
    pallas_call x3, Pallas kernels, to_owners(): call(functools.partial(sum_kernel, first), (sums,) + (extra if first else...  2.35 us
    pallas_call x1, Pallas kernels, local(): call(second_kernel, (wide, state, state, f32(8, LANES)), [VMEM] * 9, [squ...  2.11 us
  transfers between devices with their start and end apart: 3, of which 2 were waited for; matrix products, arithmetic and copies ran while one was open for 0% of the time, Pallas kernels for 2%

profile of v7, /device:TPU:1, one launch (start us, length us, event | category | flops | bytes accessed | tf_op | source)
XLA Modules:
  0.0 91.7 jit_solution(744469781254835296)
XLA Ops:
  0.6 3.4 %shard_map.86 = (f32[16,4,8,128]{3,2,1,0:T(8,128)S(1)}, bf16[8,256,1152]{2,1,0:T(8,128)(2,1)S(1)}, s32[16,128]{1,0:T(8,128)S(1)}) custom-call(s32[1,128]{1,0:T(1,128)} %bitcast.13, bf16[8,256,1152]{2,1,0:T(8,128)(2,1)} %jac.1, bf16[8,256]{1,0:T(8,128)(2,1)} %pix.1, s32[8,128]{1,0:T(8,128)} %ids.1), custom_call_target="tpu_custom_call" | custom-call | flops 1048576 | bytes 1048576 | tf_op jit(solution)/shard_map/pallas_call | solution.py:423
  4.0 0.0 copy-start
  4.0 0.0 copy-start.2
  4.0 21.4 %all_to_all.25 = f32[64,8,128]{2,1,0:T(8,128)S(1)} all-to-all(f32[64,8,128]{2,1,0:T(8,128)S(1)} %bitcast.9), channel_id=1, replica_groups=mesh['scene'=16,'x'=4,'core'=2] {'scene','x'}, dimensions={0} | all-to-all | bytes 524288 | tf_op jit(solution)/shard_map/all_to_all | solution.py:402
  25.4 1.0 %shard_map.87 = (f32[80,128]{1,0:T(8,128)S(1)}, s32[8,128]{1,0:T(8,128)S(1)}, bf16[128,4096]{1,0:T(8,128)(2,1)S(1)}) custom-call(f32[16,4,8,128]{3,2,1,0:T(8,128)S(1)} %bitcast.8), custom_call_target="tpu_custom_call" | custom-call | flops 2147483648 | bytes 1048576 | tf_op jit(solution)/shard_map/pallas_call | solution.py:406
  26.4 2.1 %collective-permute-start = (f32[80,128]{1,0:T(8,128)S(1)}, f32[80,128]{1,0:T(8,128)S(1)}, u32[]{:S(2)}, u32[]{:S(2)}) collective-permute-start(f32[80,128]{1,0:T(8,128)S(1)} %get-tuple-element.23.after.own), channel_id=1, source_target_pairs={{0,1},{1,0},{2,3},{3,2},{4,5},{5,4},{6,7},{7,6},{8,9},{9,8},{10,11... | collective-permute-start | bytes 122888 | tf_op jit(solution)/shard_map/ppermute | solution.py:417
  28.6 1.2 %shard_map.88.matrix = f32[360,128]{1,0:T(8,128)S(1)} custom-call(f32[80,128]{1,0:T(8,128)S(1)} %get-tuple-element.23.after.own, bf16[9,59,1024]{2,1,0:T(8,128)(2,1)S(1)} %copy-done, f32[59,1024]{1,0:T(8,128)S(1)} %copy-done.2), custom_call_target="tpu_custom_call" | custom-call | flops 2147483648 | bytes 1048576 | tf_op jit(solution)/shard_map/pallas_call | solution.py:437
  29.8 0.3 shard_map.89
  30.1 9.3 %all_to_all.26.recv = f32[16,8,128]{2,1,0:T(8,128)S(1)} all-to-all(f32[16,8,128]{2,1,0:T(8,128)S(1)} %shard_map.89), channel_id=1, replica_groups=mesh['scene'=16,'x'=4,'core'=2] {'scene'}, dimensions={0} | all-to-all | bytes 131072 | tf_op jit(solution)/shard_map/all_to_all | solution.py:421
  39.4 1.7 %shard_map.90 = (f32[16,4,8,128]{3,2,1,0:T(8,128)S(1)}, f32[8,1152]{1,0:T(8,128)S(1)}) custom-call(bf16[8,256,1152]{2,1,0:T(8,128)(2,1)S(1)} %get-tuple-element.20.jac, s32[16,128]{1,0:T(8,128)S(1)} %get-tuple-element.21.aux, f32[16,8,128]{2,1,0:T(8,128)S(1)} %all_to_all.26.recv), custom_call_target="tpu_custom_call" | custom-call | flops 1048576 | bytes 1048576 | tf_op jit(solution)/shard_map/pallas_call | solution.py:445
  41.1 0.0 copy-start.1
  41.1 14.5 %all_to_all.27 = f32[64,8,128]{2,1,0:T(8,128)S(1)} all-to-all(f32[64,8,128]{2,1,0:T(8,128)S(1)} %bitcast.10), channel_id=1, replica_groups=mesh['scene'=16,'x'=4,'core'=2] {'scene','x'}, dimensions={0} | all-to-all | bytes 524288 | tf_op jit(solution)/shard_map/all_to_all | solution.py:402
  55.6 0.7 shard_map.91.after.own
  56.2 2.6 %collective-permute-start.1 = (f32[80,128]{1,0:T(8,128)S(1)}, f32[80,128]{1,0:T(8,128)S(1)}, u32[]{:S(2)}, u32[]{:S(2)}) collective-permute-start(f32[80,128]{1,0:T(8,128)S(1)} %shard_map.91.after.own), channel_id=1, source_target_pairs={{0,1},{1,0},{2,3},{3,2},{4,5},{5,4},{6,7},{7,6},{8,9},{9,8},{10,11... | collective-permute-start | bytes 122888 | tf_op jit(solution)/shard_map/ppermute | solution.py:417
  58.9 0.7 shard_map.92
  59.6 0.1 collective-permute-done.1.partner
  59.7 0.6 shard_map.93
  60.3 9.3 %all_to_all.28.recv = f32[16,8,128]{2,1,0:T(8,128)S(1)} all-to-all(f32[16,8,128]{2,1,0:T(8,128)S(1)} %get-tuple-element.30), channel_id=1, replica_groups=mesh['scene'=16,'x'=4,'core'=2] {'scene'}, dimensions={0} | all-to-all | bytes 131072 | tf_op jit(solution)/shard_map/all_to_all | solution.py:421
  69.6 2.1 %shard_map.94 = (f32[16,4,8,128]{3,2,1,0:T(8,128)S(1)}, f32[59,1024]{1,0:T(8,128)S(1)}, f32[59,1024]{1,0:T(8,128)S(1)}, f32[8,128]{1,0:T(8,128)S(1)}) custom-call(bf16[8,256,1152]{2,1,0:T(8,128)(2,1)S(1)} %get-tuple-element.20.jac, s32[16,128]{1,0:T(8,128)S(1)} %get-tuple-element.21.aux, f32[16,8,128]{2,1,0:T(8,128)S(1)} %all_to_all.28.recv, ...), custom_call_target="tpu_custom_call" | custom-call | flops 1048576 | bytes 1048576 | tf_op jit(solution)/shard_map/pallas_call | solution.py:459
  71.7 14.4 %all_to_all.29 = f32[64,8,128]{2,1,0:T(8,128)S(1)} all-to-all(f32[64,8,128]{2,1,0:T(8,128)S(1)} %bitcast.7), channel_id=1, replica_groups=mesh['scene'=16,'x'=4,'core'=2] {'scene','x'}, dimensions={0} | all-to-all | bytes 524288 | tf_op jit(solution)/shard_map/all_to_all | solution.py:402
  86.1 0.7 shard_map.95.own
  86.8 2.9 %collective-permute-start.2 = (f32[80,128]{1,0:T(8,128)S(1)}, f32[80,128]{1,0:T(8,128)S(1)}, u32[]{:S(2)}, u32[]{:S(2)}) collective-permute-start(f32[80,128]{1,0:T(8,128)S(1)} %shard_map.95.own), channel_id=1, source_target_pairs={{0,1},{1,0},{2,3},{3,2},{4,5},{5,4},{6,7},{7,6},{8,9},{9,8},{10,11... | collective-permute-start | bytes 122888 | tf_op jit(solution)/shard_map/ppermute | solution.py:417
  89.7 0.9 collective-permute-done.2.partner
  90.6 1.1 %shard_map.96 = (f32[59,1024]{1,0:T(8,128)}, f32[59,1024]{1,0:T(8,128)}) custom-call(f32[80,128]{1,0:T(8,128)S(1)} %shard_map.95.own, f32[80,128]{1,0:T(8,128)S(1)} %collective-permute-done.2.partner, bf16[9,59,1024]{2,1,0:T(8,128)(2,1)S(1)} %copy-done, f32[59,1024]{1,0:T(8,128)S(1)} %copy-done.1, f32[8,128]{1,0:T(8,128)S(1)} %get-tuple-element.35.alpha_in, ...), custom_call_target="tpu_custom_call" | custom-call | flops 1048576 | bytes 1048576 | tf_op jit(solution)/shard_map/pallas_call | solution.py:467
  (4 shorter events, 0.0 us)
Async XLA Ops:
  4.0 24.6 %copy-start = (bf16[9,59,1024]{2,1,0:T(8,128)(2,1)S(1)}, bf16[9,59,1024]{2,1,0:T(8,128)(2,1)}, u32[]{:S(2)}) copy-start(bf16[9,59,1024]{2,1,0:T(8,128)(2,1)} %proj.7) | copy-start | bytes 3262468
  4.0 24.6 %copy-start.2 = (f32[59,1024]{1,0:T(8,128)S(1)}, f32[59,1024]{1,0:T(8,128)}, u32[]{:S(2)}) copy-start(f32[59,1024]{1,0:T(8,128)} %precond.7) | copy-start | bytes 724996
  26.4 3.4 %collective-permute-start = (f32[80,128]{1,0:T(8,128)S(1)}, f32[80,128]{1,0:T(8,128)S(1)}, u32[]{:S(2)}, u32[]{:S(2)}) collective-permute-start(f32[80,128]{1,0:T(8,128)S(1)} %get-tuple-element.23.after.own), channel_id=1, source_target_pairs={{0,1},{1,0},{2,3},{3,2},{4,5},{5,4},{6,7},{7,6},{8,9},{9,8},{10,11... | collective-permute-start | bytes 122888 | tf_op jit(solution)/shard_map/ppermute | solution.py:417
  41.1 17.8 %copy-start.1 = (f32[59,1024]{1,0:T(8,128)S(1)}, f32[59,1024]{1,0:T(8,128)}, u32[]{:S(2)}) copy-start(f32[59,1024]{1,0:T(8,128)} %damping.7) | copy-start | bytes 724996
  56.2 3.5 %collective-permute-start.1 = (f32[80,128]{1,0:T(8,128)S(1)}, f32[80,128]{1,0:T(8,128)S(1)}, u32[]{:S(2)}, u32[]{:S(2)}) collective-permute-start(f32[80,128]{1,0:T(8,128)S(1)} %shard_map.91.after.own), channel_id=1, source_target_pairs={{0,1},{1,0},{2,3},{3,2},{4,5},{5,4},{6,7},{7,6},{8,9},{9,8},{10,11... | collective-permute-start | bytes 122888 | tf_op jit(solution)/shard_map/ppermute | solution.py:417
  86.8 3.8 %collective-permute-start.2 = (f32[80,128]{1,0:T(8,128)S(1)}, f32[80,128]{1,0:T(8,128)S(1)}, u32[]{:S(2)}, u32[]{:S(2)}) collective-permute-start(f32[80,128]{1,0:T(8,128)S(1)} %shard_map.95.own), channel_id=1, source_target_pairs={{0,1},{1,0},{2,3},{3,2},{4,5},{5,4},{6,7},{7,6},{8,9},{9,8},{10,11... | collective-permute-start | bytes 122888 | tf_op jit(solution)/shard_map/ppermute | solution.py:417

commit v8 on v7

--- a/solution.py
+++ b/solution.py
@@ -76,7 +76,7 @@
     values = jnp.where(keep, pixels[...].astype(F32), 0.0)
     n_pix, n_col = jac.shape[1:]
     acc = jnp.zeros((n_blk, n_col), F32)
-    cut = n_blk - 1
+    cut = n_blk * 3 // 4
     for first, last in ((0, cut), (cut, n_blk)):
         signals = [jnp.where(row == b, values, 0.0).astype(BF16) for b in range(first, last)]
         for copy in copies[first:last]:
@@ -100,7 +100,7 @@
     )
 
 
-def block_pass(picks, aux, jac, by_lanes, beside=None):
+def block_pass(picks, aux, jac, by_lanes):
     n_blk, n_pix = jac.shape[:2]
     row = lax.broadcasted_iota(jnp.int32, (n_blk, n_pix), 0)
     live = row < aux[n_blk : n_blk + 1, 0:1]
@@ -113,8 +113,6 @@
             image = lane_image(jac, b, rounded[b : b + 1, :], ones)
         else:
             image = lax.dot_general(chosen, jac[b], NT, preferred_element_type=F32)
-        if beside is not None:
-            beside(b)
         signals.append(jnp.where((row == b) & live, image, 0.0).astype(BF16))
     stacked = jac[...].reshape(n_blk * n_pix, jac.shape[2])
     return jnp.dot(jnp.concatenate(signals, axis=1), stacked, preferred_element_type=F32)
@@ -140,42 +138,43 @@
     pack_return(acc, aux[0:n_blk, :], (), stage, out)
 
 
-def second_kernel(
-    jac, aux, recv, picks_in, res, dirn, image, precond, damping,
-    out, res_out, dir_out, alpha_out, turned, stage,
-):
+def second_kernel(jac, aux, recv, picks_in, out, steps_out, turned, stage):
     n_blk = jac.shape[0]
     n_proj = jac.shape[2] // LANES
     fresh = unpack_picks(recv, turned, n_blk, n_proj)
     per = recv.shape[1]
-    rz = total_of(turned[n_proj + 1 : n_proj + 2, :], per)
-    curve = total_of(turned[n_proj + 2 : n_proj + 3, :], per)
-    square = total_of(turned[n_proj + 3 : n_proj + 4, :], per)
-    alpha = jnp.full((1, LANES), rz, F32) / jnp.full((1, LANES), curve, F32)
+    rz, curve, square, damped, mixed, scaled = (
+        jnp.full((1, LANES), total_of(turned[n_proj + 1 + i : n_proj + 2 + i, :], per), F32)
+        for i in range(6)
+    )
+    alpha = rz / curve
     after = rz - 2.0 * alpha * curve + alpha * alpha * square
-    beta = after / jnp.full((1, LANES), rz, F32)
-    alpha_out[...] = jnp.broadcast_to(alpha, alpha_out.shape)
+    beta = after / rz
+    grown = 1.0 + beta
+    steps_out[0:1, :] = alpha
+    steps_out[1:2, :] = beta
+    steps_out[2:3, :] = after
+    steps_out[3:4, :] = (
+        grown * grown * damped - 2.0 * grown * alpha * mixed + alpha * alpha * scaled
+    )
+    steps_out[4:8, :] = jnp.zeros((4, LANES), F32)
     pieces = []
     for k in range(n_proj):
         cols = slice(k * LANES, (k + 1) * LANES)
-        pieces.append((1.0 + beta) * picks_in[:, cols] - alpha * fresh[:, cols])
+        pieces.append(grown * picks_in[:, cols] - alpha * fresh[:, cols])
     picks = jnp.concatenate(pieces, axis=1)
-    n_par, width = res.shape
-    sums = [jnp.zeros((n_par, LANES), F32)] * 2
-
-    def update(h):
+    acc = block_pass(picks, aux, jac, 5)
+    pack_return(acc, aux[0:n_blk, :], (jnp.sum(picks * acc),), stage, out)
+
+
+def update_kernel(after, steps, res, dirn, image, precond, res_out, dir_out):
+    del after
+    alpha, beta = steps[0:1, :], steps[1:2, :]
+    for h in range(res.shape[1] // LANES):
         cols = slice(h * LANES, (h + 1) * LANES)
         new_res = res[:, cols] - alpha * image[:, cols]
-        precon = precond[:, cols] * new_res
-        new_dir = precon + beta * dirn[:, cols]
         res_out[:, cols] = new_res
-        dir_out[:, cols] = new_dir
-        sums[0] += damping[:, cols] * new_dir * new_dir
-        sums[1] += new_res * precon
-
-    acc = block_pass(picks, aux, jac, 4, update)
-    scalars = (jnp.sum(picks * acc), jnp.sum(sums[0]), jnp.sum(sums[1]))
-    pack_return(acc, aux[0:n_blk, :], scalars, stage, out)
+        dir_out[:, cols] = precond[:, cols] * new_res + beta * dirn[:, cols]
 
 
 def sum_kernel(first, recv, *rest):
@@ -219,10 +218,7 @@
     for x in range(n_x):
         mixed += turned[x, n_proj + 1 : n_proj + 2, :]
     out[half : half + 1, :] = jnp.full((1, LANES), total_of(mixed, per), F32)
-    for i in (1, 2):
-        line = turned[0, n_proj + 1 + i : n_proj + 2 + i, :]
-        out[half + i : half + i + 1, :] = jnp.full((1, LANES), total_of(line, per), F32)
-    out[half + 3 : half + 8, :] = jnp.zeros((5, LANES), F32)
+    out[half + 1 : half + 8, :] = jnp.zeros((7, LANES), F32)
     if first:
         ids_out[...] = turned[lax.axis_index("x"), pl.ds(n_proj, n_blk, stride=ROWS), :].astype(jnp.int32)
 
@@ -340,45 +336,52 @@
     n_par, width = precond.shape
     for k, tile in enumerate(blended(matrix, weights)):
         table[k * 8 : k * 8 + 8, :] = tile + cross[k * 8 : k * 8 + 8, :]
-    curve = jnp.zeros((n_par, LANES), F32)
-    square = jnp.zeros((n_par, LANES), F32)
+    curve, square, damped, mixed, scaled = [jnp.zeros((n_par, LANES), F32)] * 5
     for h in range(width // LANES):
         cols = slice(h * LANES, (h + 1) * LANES)
-        image = lifted(proj, weights, h) + damping[:, cols] * dirn[:, cols]
+        pull = damping[:, cols] * dirn[:, cols]
+        image = lifted(proj, weights, h) + pull
         image_out[:, cols] = image
+        change = precond[:, cols] * image
         curve += dirn[:, cols] * image
-        square += precond[:, cols] * image * image
-    scalars = (rz_in[0:1, :], jnp.sum(curve), jnp.sum(square))
+        square += change * image
+        damped += pull * dirn[:, cols]
+        mixed += pull * change
+        scaled += damping[:, cols] * change * change
+    scalars = (rz_in[0:1, :],) + tuple(map(jnp.sum, (curve, square, damped, mixed, scaled)))
     send_picks(table, ids, scalars, stage, out)
 
 
 def last_kernel(
-    own, partner, proj, damping, alpha_in, first_dir, res, dirn,
+    own, partner, proj, damping, steps, first_dir, res, dirn,
     sol_hbm, res_hbm, weights, sol_out, res_out, sem,
 ):
     weights[...] = own[...] + partner[...]
     rows = proj.shape[0] * 8
-    curve = weights[rows : rows + 1, :] + own[rows + 1 : rows + 2, :]
-    alpha = own[rows + 2 : rows + 3, :] / curve
-    alpha_first = alpha_in[0:1, :]
+    curve = weights[rows : rows + 1, :] + steps[3:4, :]
+    alpha = steps[2:3, :] / curve
+    alpha_first = steps[0:1, :]
     chunks = damping.shape[1] // LANES
     copies = []
 
-    def send(end):
-        cols = pl.ds((end - 2) * LANES, 2 * LANES)
-        for here, there in ((sol_out, sol_hbm), (res_out, res_hbm)):
-            copy = pltpu.make_async_copy(here.at[:, cols], there.at[:, cols], sem.at[len(copies)])
-            copy.start()
-            copies.append(copy)
+    def send(here, there, first, last):
+        cols = pl.ds(first * LANES, (last - first) * LANES)
+        copy = pltpu.make_async_copy(here.at[:, cols], there.at[:, cols], sem.at[len(copies)])
+        copy.start()
+        copies.append(copy)
 
     for h in range(chunks):
         cols = slice(h * LANES, (h + 1) * LANES)
+        sol_out[:, cols] = alpha_first * first_dir[:, cols] + alpha * dirn[:, cols]
+    for h in range(chunks):
+        cols = slice(h * LANES, (h + 1) * LANES)
         image = lifted(proj, weights, h) + damping[:, cols] * dirn[:, cols]
-        sol_out[:, cols] = alpha_first * first_dir[:, cols] + alpha * dirn[:, cols]
         res_out[:, cols] = res[:, cols] - alpha * image
-        if h >= 2 and h % 2 == 0:
-            send(h)
-    send(chunks)
+        if h == 0:
+            send(sol_out, sol_hbm, 0, chunks)
+        elif h % 2 == 0:
+            send(res_out, res_hbm, h - 2, h)
+    send(res_out, res_hbm, chunks - 2, chunks)
     for copy in copies:
         copy.wait()
 
@@ -456,22 +459,22 @@
         own, partner, proj_jac, precond, damping, matrix, cross, rz, index, first_dir
     )
     arrived = to_blocks(message)
-    message, res, second_dir, alpha = call(
-        second_kernel,
-        (wide, state, state, f32(8, LANES)),
-        [VMEM] * 9,
-        [square, square],
-    )(jac, aux, arrived, picks, res, first_dir, image, precond, damping)
+    message, steps = call(
+        second_kernel, (wide, f32(8, LANES)), [VMEM] * 4, [square, square]
+    )(jac, aux, arrived, picks)
     own, partner = to_owners(message, right)
+    res, second_dir = call(update_kernel, (state, state), [VMEM] * 6, (), 1 << 31)(
+        own, steps, res, first_dir, image, precond
+    )
     held = pltpu.VMEM((n_par, g_dev), F32)
     return call(
         last_kernel,
         (state, state),
         [VMEM] * 8,
-        [weights, held, held, pltpu.SemaphoreType.DMA((2 * (g_dev // (2 * LANES)),))],
+        [weights, held, held, pltpu.SemaphoreType.DMA((1 + g_dev // (2 * LANES),))],
         out_space=HBM,
     )(
-        own, partner, proj_jac, damping, alpha, first_dir, res, second_dir
+        own, partner, proj_jac, damping, steps, first_dir, res, second_dir
     )
 
 

time: 92 us -> 91.6 us (level)
    pallas_call x1 -> x2, Pallas kernels: 2.11 us -> 1.95 us  [the longest x1 1.88 us: local(): call(second_kernel, (wide, f32(8, LANES)), [VMEM] * 4, [square, square])]
where the time goes in v8:
time: 91.6 us; the launch traced here: 91.3 us
  blocking collectives  68.8 us (75%)
  Pallas kernels  13.1 us (14%)
  starting transfers between devices  7.72 us (8%)
    all_to_all x3, blocking collectives, to_owners(): got = lax.all_to_all(flat, ('scene', 'x'), 0, 0, tiled=True)  50.2 us
    all_to_all x2, blocking collectives, to_blocks(): return lax.all_to_all(message, 'scene', 0, 0, tiled=True)  18.6 us
    ppermute x3, starting transfers between devices, to_owners(): partner = lax.ppermute(own, 'core', [(0, 1), (1, 0)])  7.72 us
    pallas_call x1, Pallas kernels, local(): call(rhs_kernel, (wide, whole(jacobian.shape, BF16), whole((2 * n_blk, LA...  3.27 us
    pallas_call x3, Pallas kernels, to_owners(): call(functools.partial(sum_kernel, first), (sums,) + (extra if first else...  2.29 us
    pallas_call x1, Pallas kernels, local(): call(second_kernel, (wide, f32(8, LANES)), [VMEM] * 4, [square, square])  1.88 us
  transfers between devices with their start and end apart: 3, of which 2 were waited for; matrix products, arithmetic and copies ran while one was open for 0% of the time, Pallas kernels for 2%

profile of v8, /device:TPU:1, one launch (start us, length us, event | category | flops | bytes accessed | tf_op | source)
XLA Modules:
  0.0 91.3 jit_solution(17528467503461656872)
XLA Ops:
  0.6 3.3 %shard_map.86 = (f32[16,4,8,128]{3,2,1,0:T(8,128)S(1)}, bf16[8,256,1152]{2,1,0:T(8,128)(2,1)S(1)}, s32[16,128]{1,0:T(8,128)S(1)}) custom-call(s32[1,128]{1,0:T(1,128)} %bitcast.13, bf16[8,256,1152]{2,1,0:T(8,128)(2,1)} %jac.1, bf16[8,256]{1,0:T(8,128)(2,1)} %pix.1, s32[8,128]{1,0:T(8,128)} %ids.1), custom_call_target="tpu_custom_call" | custom-call | flops 1048576 | bytes 1048576 | tf_op jit(solution)/shard_map/pallas_call | solution.py:426
  3.9 0.0 copy-start
  3.9 21.4 %all_to_all.25 = f32[64,8,128]{2,1,0:T(8,128)S(1)} all-to-all(f32[64,8,128]{2,1,0:T(8,128)S(1)} %bitcast.9), channel_id=1, replica_groups=mesh['scene'=16,'x'=4,'core'=2] {'scene','x'}, dimensions={0} | all-to-all | bytes 524288 | tf_op jit(solution)/shard_map/all_to_all | solution.py:405
  25.3 1.0 %shard_map.87 = (f32[80,128]{1,0:T(8,128)S(1)}, s32[8,128]{1,0:T(8,128)S(1)}, bf16[128,4096]{1,0:T(8,128)(2,1)S(1)}) custom-call(f32[16,4,8,128]{3,2,1,0:T(8,128)S(1)} %bitcast.8), custom_call_target="tpu_custom_call" | custom-call | flops 2147483648 | bytes 1048576 | tf_op jit(solution)/shard_map/pallas_call | solution.py:409
  26.3 2.1 %collective-permute-start = (f32[80,128]{1,0:T(8,128)S(1)}, f32[80,128]{1,0:T(8,128)S(1)}, u32[]{:S(2)}, u32[]{:S(2)}) collective-permute-start(f32[80,128]{1,0:T(8,128)S(1)} %get-tuple-element.23.after.own), channel_id=1, source_target_pairs={{0,1},{1,0},{2,3},{3,2},{4,5},{5,4},{6,7},{7,6},{8,9},{9,8},{10,11... | collective-permute-start | bytes 122888 | tf_op jit(solution)/shard_map/ppermute | solution.py:420
  28.5 1.2 %shard_map.88.matrix = f32[360,128]{1,0:T(8,128)S(1)} custom-call(f32[80,128]{1,0:T(8,128)S(1)} %get-tuple-element.23.after.own, bf16[9,59,1024]{2,1,0:T(8,128)(2,1)S(1)} %copy-done, f32[59,1024]{1,0:T(8,128)S(1)} %copy-done.2), custom_call_target="tpu_custom_call" | custom-call | flops 2147483648 | bytes 1048576 | tf_op jit(solution)/shard_map/pallas_call | solution.py:440
  29.7 0.3 shard_map.89
  30.0 9.3 %all_to_all.26.recv = f32[16,8,128]{2,1,0:T(8,128)S(1)} all-to-all(f32[16,8,128]{2,1,0:T(8,128)S(1)} %shard_map.89), channel_id=1, replica_groups=mesh['scene'=16,'x'=4,'core'=2] {'scene'}, dimensions={0} | all-to-all | bytes 131072 | tf_op jit(solution)/shard_map/all_to_all | solution.py:424
  39.3 1.7 %shard_map.90 = (f32[16,4,8,128]{3,2,1,0:T(8,128)S(1)}, f32[8,1152]{1,0:T(8,128)S(1)}) custom-call(bf16[8,256,1152]{2,1,0:T(8,128)(2,1)S(1)} %get-tuple-element.20.jac, s32[16,128]{1,0:T(8,128)S(1)} %get-tuple-element.21.aux, f32[16,8,128]{2,1,0:T(8,128)S(1)} %all_to_all.26.recv), custom_call_target="tpu_custom_call" | custom-call | flops 1048576 | bytes 1048576 | tf_op jit(solution)/shard_map/pallas_call | solution.py:448
  40.9 0.0 copy-start.1
  41.0 14.5 %all_to_all.27 = f32[64,8,128]{2,1,0:T(8,128)S(1)} all-to-all(f32[64,8,128]{2,1,0:T(8,128)S(1)} %bitcast.10), channel_id=1, replica_groups=mesh['scene'=16,'x'=4,'core'=2] {'scene','x'}, dimensions={0} | all-to-all | bytes 524288 | tf_op jit(solution)/shard_map/all_to_all | solution.py:405
  55.4 0.6 shard_map.91.after.own
  56.1 2.6 %collective-permute-start.1 = (f32[80,128]{1,0:T(8,128)S(1)}, f32[80,128]{1,0:T(8,128)S(1)}, u32[]{:S(2)}, u32[]{:S(2)}) collective-permute-start(f32[80,128]{1,0:T(8,128)S(1)} %shard_map.91.after.own), channel_id=1, source_target_pairs={{0,1},{1,0},{2,3},{3,2},{4,5},{5,4},{6,7},{7,6},{8,9},{9,8},{10,11... | collective-permute-start | bytes 122888 | tf_op jit(solution)/shard_map/ppermute | solution.py:420
  58.7 0.7 shard_map.92
  59.5 0.1 collective-permute-done.1.partner
  59.6 0.7 shard_map.93
  60.3 9.3 %all_to_all.28.recv = f32[16,8,128]{2,1,0:T(8,128)S(1)} all-to-all(f32[16,8,128]{2,1,0:T(8,128)S(1)} %get-tuple-element.30), channel_id=1, replica_groups=mesh['scene'=16,'x'=4,'core'=2] {'scene'}, dimensions={0} | all-to-all | bytes 131072 | tf_op jit(solution)/shard_map/all_to_all | solution.py:424
  69.6 1.9 %shard_map.94 = (f32[16,4,8,128]{3,2,1,0:T(8,128)S(1)}, f32[8,128]{1,0:T(8,128)S(1)}) custom-call(bf16[8,256,1152]{2,1,0:T(8,128)(2,1)S(1)} %get-tuple-element.20.jac, s32[16,128]{1,0:T(8,128)S(1)} %get-tuple-element.21.aux, f32[16,8,128]{2,1,0:T(8,128)S(1)} %all_to_all.28.recv, f32[8,1152]{1,0:T(8,128)S(1)} %get-tuple-element.31.picks_in), custom_call_target="tpu_custom_call" | custom-call | flops 1048576 | bytes 1048576 | tf_op jit(solution)/shard_map/pallas_call | solution.py:462
  71.5 14.4 %all_to_all.29 = f32[64,8,128]{2,1,0:T(8,128)S(1)} all-to-all(f32[64,8,128]{2,1,0:T(8,128)S(1)} %bitcast.7), channel_id=1, replica_groups=mesh['scene'=16,'x'=4,'core'=2] {'scene','x'}, dimensions={0} | all-to-all | bytes 524288 | tf_op jit(solution)/shard_map/all_to_all | solution.py:405
  85.8 0.6 shard_map.95.after.own
  86.5 2.9 %collective-permute-start.2 = (f32[80,128]{1,0:T(8,128)S(1)}, f32[80,128]{1,0:T(8,128)S(1)}, u32[]{:S(2)}, u32[]{:S(2)}) collective-permute-start(f32[80,128]{1,0:T(8,128)S(1)} %shard_map.95.after.own), channel_id=1, source_target_pairs={{0,1},{1,0},{2,3},{3,2},{4,5},{5,4},{6,7},{7,6},{8,9},{9,8},{10,11... | collective-permute-start | bytes 122888 | tf_op jit(solution)/shard_map/ppermute | solution.py:420
  89.4 0.1 shard_map.96
  89.5 0.8 collective-permute-done.2.partner
  90.3 1.0 %shard_map.97 = (f32[59,1024]{1,0:T(8,128)}, f32[59,1024]{1,0:T(8,128)}) custom-call(f32[80,128]{1,0:T(8,128)S(1)} %shard_map.95.after.own, f32[80,128]{1,0:T(8,128)S(1)} %collective-permute-done.2.partner, bf16[9,59,1024]{2,1,0:T(8,128)(2,1)S(1)} %copy-done, f32[59,1024]{1,0:T(8,128)S(1)} %copy-done.1, f32[8,128]{1,0:T(8,128)S(1)} %get-tuple-element.33.steps, ...), custom_call_target="tpu_custom_call" | custom-call | flops 1048576 | bytes 1048576 | tf_op jit(solution)/shard_map/pallas_call | solution.py:470
  (5 shorter events, 0.0 us)
Async XLA Ops:
  3.9 24.6 %copy-start = (bf16[9,59,1024]{2,1,0:T(8,128)(2,1)S(1)}, bf16[9,59,1024]{2,1,0:T(8,128)(2,1)}, u32[]{:S(2)}) copy-start(bf16[9,59,1024]{2,1,0:T(8,128)(2,1)} %proj.7) | copy-start | bytes 3262468
  3.9 24.6 %copy-start.2 = (f32[59,1024]{1,0:T(8,128)S(1)}, f32[59,1024]{1,0:T(8,128)}, u32[]{:S(2)}) copy-start(f32[59,1024]{1,0:T(8,128)} %precond.7) | copy-start | bytes 724996
  26.3 3.4 %collective-permute-start = (f32[80,128]{1,0:T(8,128)S(1)}, f32[80,128]{1,0:T(8,128)S(1)}, u32[]{:S(2)}, u32[]{:S(2)}) collective-permute-start(f32[80,128]{1,0:T(8,128)S(1)} %get-tuple-element.23.after.own), channel_id=1, source_target_pairs={{0,1},{1,0},{2,3},{3,2},{4,5},{5,4},{6,7},{7,6},{8,9},{9,8},{10,11... | collective-permute-start | bytes 122888 | tf_op jit(solution)/shard_map/ppermute | solution.py:420
  40.9 17.8 %copy-start.1 = (f32[59,1024]{1,0:T(8,128)S(1)}, f32[59,1024]{1,0:T(8,128)}, u32[]{:S(2)}) copy-start(f32[59,1024]{1,0:T(8,128)} %damping.5) | copy-start | bytes 724996
  56.1 3.5 %collective-permute-start.1 = (f32[80,128]{1,0:T(8,128)S(1)}, f32[80,128]{1,0:T(8,128)S(1)}, u32[]{:S(2)}, u32[]{:S(2)}) collective-permute-start(f32[80,128]{1,0:T(8,128)S(1)} %shard_map.91.after.own), channel_id=1, source_target_pairs={{0,1},{1,0},{2,3},{3,2},{4,5},{5,4},{6,7},{7,6},{8,9},{9,8},{10,11... | collective-permute-start | bytes 122888 | tf_op jit(solution)/shard_map/ppermute | solution.py:420
  86.5 3.8 %collective-permute-start.2 = (f32[80,128]{1,0:T(8,128)S(1)}, f32[80,128]{1,0:T(8,128)S(1)}, u32[]{:S(2)}, u32[]{:S(2)}) collective-permute-start(f32[80,128]{1,0:T(8,128)S(1)} %shard_map.95.after.own), channel_id=1, source_target_pairs={{0,1},{1,0},{2,3},{3,2},{4,5},{5,4},{6,7},{7,6},{8,9},{9,8},{10,11... | collective-permute-start | bytes 122888 | tf_op jit(solution)/shard_map/ppermute | solution.py:420

commit v9 on v8

--- a/solution.py
+++ b/solution.py
@@ -37,15 +37,18 @@
     return jax.ShapeDtypeStruct(shape, F32)
 
 
-def pack_return(acc, ids, scalars, stage, out):
+def clear_stage(ids, stage, n_proj):
+    stage[...] = jnp.zeros_like(stage)
+    stage[pl.ds(n_proj, ids.shape[0], stride=ROWS), :] = ids.astype(F32)
+
+
+def pack_return(acc, scalars, stage, out):
     n_blk = acc.shape[0]
     n_proj = acc.shape[1] // LANES
-    stage[...] = jnp.zeros_like(stage)
     for k in range(n_proj):
         stage[pl.ds(k, n_blk, stride=ROWS), :] = acc[:, k * LANES : (k + 1) * LANES]
-    stage[pl.ds(n_proj, n_blk, stride=ROWS), :] = ids.astype(F32)
     for i, value in enumerate(scalars):
-        stage[n_proj + 1 + i : n_proj + 2 + i, :] = jnp.full((1, LANES), value, F32)
+        stage[n_proj + 1 + i : n_proj + 2 + i, :] = value
     turned = stage[...].T.reshape(out.shape[0], *out.shape[2:])
     for x in range(out.shape[1]):
         out[:, x] = turned
@@ -71,6 +74,7 @@
     local_ids = index[...] & (LANES * 8 - 1)
     aux[0:n_blk, :] = local_ids
     aux[n_blk : 2 * n_blk, :] = jnp.broadcast_to(own, (n_blk, LANES))
+    clear_stage(local_ids, stage, jac.shape[2] // LANES)
     row = lax.broadcasted_iota(jnp.int32, pix.shape, 0)
     keep = row < jnp.broadcast_to(own, pix.shape)
     values = jnp.where(keep, pixels[...].astype(F32), 0.0)
@@ -83,7 +87,7 @@
             copy.wait()
         stacked = jbuf[first:last].reshape((last - first) * n_pix, n_col)
         acc += jnp.dot(jnp.concatenate(signals, axis=1), stacked, preferred_element_type=F32)
-    pack_return(acc, local_ids, (), stage, out)
+    pack_return(acc, (), stage, out)
 
 
 def lane_image(jac, b, line, ones):
@@ -125,8 +129,8 @@
     )
 
 
-def total_of(row, copies):
-    return jnp.sum(row) * (1.0 / copies)
+def over_lanes(rows):
+    return jnp.broadcast_to(jnp.sum(rows, axis=1, keepdims=True), rows.shape)
 
 
 def first_kernel(jac, aux, recv, out, picks_out, turned, stage):
@@ -135,7 +139,8 @@
     picks = unpack_picks(recv, turned, n_blk, n_proj)
     picks_out[...] = picks
     acc = block_pass(picks, aux, jac, 5)
-    pack_return(acc, aux[0:n_blk, :], (), stage, out)
+    clear_stage(aux[0:n_blk, :], stage, n_proj)
+    pack_return(acc, (), stage, out)
 
 
 def second_kernel(jac, aux, recv, picks_in, out, steps_out, turned, stage):
@@ -143,10 +148,8 @@
     n_proj = jac.shape[2] // LANES
     fresh = unpack_picks(recv, turned, n_blk, n_proj)
     per = recv.shape[1]
-    rz, curve, square, damped, mixed, scaled = (
-        jnp.full((1, LANES), total_of(turned[n_proj + 1 + i : n_proj + 2 + i, :], per), F32)
-        for i in range(6)
-    )
+    totals = over_lanes(turned[8:16, :]) * (1.0 / per)
+    rz, curve, square, damped, mixed, scaled = (totals[i : i + 1, :] for i in range(2, 8))
     alpha = rz / curve
     after = rz - 2.0 * alpha * curve + alpha * alpha * square
     beta = after / rz
@@ -164,7 +167,13 @@
         pieces.append(grown * picks_in[:, cols] - alpha * fresh[:, cols])
     picks = jnp.concatenate(pieces, axis=1)
     acc = block_pass(picks, aux, jac, 5)
-    pack_return(acc, aux[0:n_blk, :], (jnp.sum(picks * acc),), stage, out)
+    weighed = picks * acc
+    line = jnp.zeros((n_blk, LANES), F32)
+    for k in range(n_proj):
+        line += weighed[:, k * LANES : (k + 1) * LANES]
+    line = over_lanes(jnp.sum(line, axis=0, keepdims=True))
+    clear_stage(aux[0:n_blk, :], stage, n_proj)
+    pack_return(acc, (line,), stage, out)
 
 
 def update_kernel(after, steps, res, dirn, image, precond, res_out, dir_out):
@@ -186,7 +195,7 @@
     n_blk = LANES // ROWS
     n_proj = 9
     sub = lax.broadcasted_iota(jnp.int32, (n_blk, LANES), 0)
-    deep = lax.broadcasted_iota(jnp.int32, (LANES, LANES), 0)
+    deep = lax.broadcasted_iota(jnp.int32, (LANES, LANES), 0).astype(BF16)
     half = n_proj * 8
 
     def spread(table, x, base, high):
@@ -209,15 +218,15 @@
             left[0:half, cols] = spread(turned, x, base, high).astype(BF16)
             left[80 : 80 + half, cols] = spread(fine, x, base, high).astype(BF16)
             if first:
-                low = jnp.broadcast_to(ids & 127, (LANES, LANES)) == deep
-                right[:, cols] = jnp.where(low, 1.0, 0.0).astype(BF16)
+                low = jnp.broadcast_to((ids & 127).astype(BF16), (LANES, LANES)) == deep
+                right[:, cols] = jnp.where(low, jnp.ones_like(deep), jnp.zeros_like(deep))
     summed = lax.dot_general(left[...], right[...], NT, preferred_element_type=F32)
     out[0:half, :] = summed[0:half] + summed[80 : 80 + half]
     per = recv.shape[2]
     mixed = jnp.zeros((1, LANES), F32)
     for x in range(n_x):
         mixed += turned[x, n_proj + 1 : n_proj + 2, :]
-    out[half : half + 1, :] = jnp.full((1, LANES), total_of(mixed, per), F32)
+    out[half : half + 1, :] = over_lanes(mixed) * (1.0 / per)
     out[half + 1 : half + 8, :] = jnp.zeros((7, LANES), F32)
     if first:
         ids_out[...] = turned[lax.axis_index("x"), pl.ds(n_proj, n_blk, stride=ROWS), :].astype(jnp.int32)
@@ -298,8 +307,10 @@
         line = jnp.broadcast_to(table[64 + h : 65 + h, :], (n_blk, LANES))
         got = jnp.where(high == h, lane_pick(line, low), got)
     stage[pl.ds(8, n_blk, stride=ROWS), :] = got
-    for i, value in enumerate(scalars):
-        stage[10 + i : 11 + i, :] = jnp.broadcast_to(value, (1, LANES))
+    at = 10
+    for rows in scalars:
+        stage[at : at + rows.shape[0], :] = rows
+        at += rows.shape[0]
     out[...] = stage[...].T.reshape(out.shape)
 
 
@@ -348,8 +359,8 @@
         damped += pull * dirn[:, cols]
         mixed += pull * change
         scaled += damping[:, cols] * change * change
-    scalars = (rz_in[0:1, :],) + tuple(map(jnp.sum, (curve, square, damped, mixed, scaled)))
-    send_picks(table, ids, scalars, stage, out)
+    lines = [jnp.sum(each, axis=0, keepdims=True) for each in (curve, square, damped, mixed, scaled)]
+    send_picks(table, ids, (rz_in[0:1, :], over_lanes(jnp.concatenate(lines, axis=0))), stage, out)
 
 
 def last_kernel(

time: 91.6 us -> 91.4 us (level)
  no operation moved by 1% of the time
where the time goes in v9:
time: 91.4 us; the launch traced here: 91.1 us
  blocking collectives  68.8 us (75%)
  Pallas kernels  12.9 us (14%)
  starting transfers between devices  7.73 us (8%)
    all_to_all x3, blocking collectives, to_owners(): got = lax.all_to_all(flat, ('scene', 'x'), 0, 0, tiled=True)  50.2 us
    all_to_all x2, blocking collectives, to_blocks(): return lax.all_to_all(message, 'scene', 0, 0, tiled=True)  18.6 us
    ppermute x3, starting transfers between devices, to_owners(): partner = lax.ppermute(own, 'core', [(0, 1), (1, 0)])  7.73 us
    pallas_call x1, Pallas kernels, local(): call(rhs_kernel, (wide, whole(jacobian.shape, BF16), whole((2 * n_blk, LA...  3.27 us
    pallas_call x3, Pallas kernels, to_owners(): call(functools.partial(sum_kernel, first), (sums,) + (extra if first else...  2.16 us
  transfers between devices with their start and end apart: 3, of which 2 were waited for; matrix products, arithmetic and copies ran while one was open for 0% of the time, Pallas kernels for 2%

profile of v9, /device:TPU:1, one launch (start us, length us, event | category | flops | bytes accessed | tf_op | source)
XLA Modules:
  0.0 91.1 jit_solution(2061401587601113975)
XLA Ops:
  0.6 3.3 %shard_map.86 = (f32[16,4,8,128]{3,2,1,0:T(8,128)S(1)}, bf16[8,256,1152]{2,1,0:T(8,128)(2,1)S(1)}, s32[16,128]{1,0:T(8,128)S(1)}) custom-call(s32[1,128]{1,0:T(1,128)} %bitcast.13, bf16[8,256,1152]{2,1,0:T(8,128)(2,1)} %jac.1, bf16[8,256]{1,0:T(8,128)(2,1)} %pix.1, s32[8,128]{1,0:T(8,128)} %ids.1), custom_call_target="tpu_custom_call" | custom-call | flops 1048576 | bytes 1048576 | tf_op jit(solution)/shard_map/pallas_call | solution.py:437
  3.9 0.0 copy-start
  3.9 0.0 copy-start.2
  3.9 21.4 %all_to_all.25 = f32[64,8,128]{2,1,0:T(8,128)S(1)} all-to-all(f32[64,8,128]{2,1,0:T(8,128)S(1)} %bitcast.9), channel_id=1, replica_groups=mesh['scene'=16,'x'=4,'core'=2] {'scene','x'}, dimensions={0} | all-to-all | bytes 524288 | tf_op jit(solution)/shard_map/all_to_all | solution.py:416
  25.3 0.9 shard_map.87
  26.2 2.1 %collective-permute-start = (f32[80,128]{1,0:T(8,128)S(1)}, f32[80,128]{1,0:T(8,128)S(1)}, u32[]{:S(2)}, u32[]{:S(2)}) collective-permute-start(f32[80,128]{1,0:T(8,128)S(1)} %get-tuple-element.23.after.own), channel_id=1, source_target_pairs={{0,1},{1,0},{2,3},{3,2},{4,5},{5,4},{6,7},{7,6},{8,9},{9,8},{10,11... | collective-permute-start | bytes 122888 | tf_op jit(solution)/shard_map/ppermute | solution.py:431
  28.4 1.2 %shard_map.88.matrix = f32[360,128]{1,0:T(8,128)S(1)} custom-call(f32[80,128]{1,0:T(8,128)S(1)} %get-tuple-element.23.after.own, bf16[9,59,1024]{2,1,0:T(8,128)(2,1)S(1)} %copy-done, f32[59,1024]{1,0:T(8,128)S(1)} %copy-done.2), custom_call_target="tpu_custom_call" | custom-call | flops 2147483648 | bytes 1048576 | tf_op jit(solution)/shard_map/pallas_call | solution.py:451
  29.6 0.3 shard_map.89
  29.9 9.3 %all_to_all.26.recv = f32[16,8,128]{2,1,0:T(8,128)S(1)} all-to-all(f32[16,8,128]{2,1,0:T(8,128)S(1)} %shard_map.89), channel_id=1, replica_groups=mesh['scene'=16,'x'=4,'core'=2] {'scene'}, dimensions={0} | all-to-all | bytes 131072 | tf_op jit(solution)/shard_map/all_to_all | solution.py:435
  39.2 1.7 %shard_map.90 = (f32[16,4,8,128]{3,2,1,0:T(8,128)S(1)}, f32[8,1152]{1,0:T(8,128)S(1)}) custom-call(bf16[8,256,1152]{2,1,0:T(8,128)(2,1)S(1)} %get-tuple-element.20.jac, s32[16,128]{1,0:T(8,128)S(1)} %get-tuple-element.21.aux, f32[16,8,128]{2,1,0:T(8,128)S(1)} %all_to_all.26.recv), custom_call_target="tpu_custom_call" | custom-call | flops 1048576 | bytes 1048576 | tf_op jit(solution)/shard_map/pallas_call | solution.py:459
  40.8 14.5 %all_to_all.27 = f32[64,8,128]{2,1,0:T(8,128)S(1)} all-to-all(f32[64,8,128]{2,1,0:T(8,128)S(1)} %bitcast.10), channel_id=1, replica_groups=mesh['scene'=16,'x'=4,'core'=2] {'scene','x'}, dimensions={0} | all-to-all | bytes 524288 | tf_op jit(solution)/shard_map/all_to_all | solution.py:416
  55.3 0.6 shard_map.91.after.own
  56.0 2.6 %collective-permute-start.1 = (f32[80,128]{1,0:T(8,128)S(1)}, f32[80,128]{1,0:T(8,128)S(1)}, u32[]{:S(2)}, u32[]{:S(2)}) collective-permute-start(f32[80,128]{1,0:T(8,128)S(1)} %shard_map.91.after.own), channel_id=1, source_target_pairs={{0,1},{1,0},{2,3},{3,2},{4,5},{5,4},{6,7},{7,6},{8,9},{9,8},{10,11... | collective-permute-start | bytes 122888 | tf_op jit(solution)/shard_map/ppermute | solution.py:431
  58.6 0.7 shard_map.92
  59.3 0.1 collective-permute-done.1.partner
  59.5 0.7 shard_map.93
  60.1 9.3 %all_to_all.28.recv = f32[16,8,128]{2,1,0:T(8,128)S(1)} all-to-all(f32[16,8,128]{2,1,0:T(8,128)S(1)} %get-tuple-element.30), channel_id=1, replica_groups=mesh['scene'=16,'x'=4,'core'=2] {'scene'}, dimensions={0} | all-to-all | bytes 131072 | tf_op jit(solution)/shard_map/all_to_all | solution.py:435
  69.4 1.8 %shard_map.94 = (f32[16,4,8,128]{3,2,1,0:T(8,128)S(1)}, f32[8,128]{1,0:T(8,128)S(1)}) custom-call(bf16[8,256,1152]{2,1,0:T(8,128)(2,1)S(1)} %get-tuple-element.20.jac, s32[16,128]{1,0:T(8,128)S(1)} %get-tuple-element.21.aux, f32[16,8,128]{2,1,0:T(8,128)S(1)} %all_to_all.28.recv, f32[8,1152]{1,0:T(8,128)S(1)} %get-tuple-element.31.picks_in), custom_call_target="tpu_custom_call" | custom-call | flops 1048576 | bytes 1048576 | tf_op jit(solution)/shard_map/pallas_call | solution.py:473
  71.2 14.4 %all_to_all.29 = f32[64,8,128]{2,1,0:T(8,128)S(1)} all-to-all(f32[64,8,128]{2,1,0:T(8,128)S(1)} %bitcast.7), channel_id=1, replica_groups=mesh['scene'=16,'x'=4,'core'=2] {'scene','x'}, dimensions={0} | all-to-all | bytes 524288 | tf_op jit(solution)/shard_map/all_to_all | solution.py:416
  85.6 0.6 shard_map.95.after.own
  86.2 2.9 %collective-permute-start.2 = (f32[80,128]{1,0:T(8,128)S(1)}, f32[80,128]{1,0:T(8,128)S(1)}, u32[]{:S(2)}, u32[]{:S(2)}) collective-permute-start(f32[80,128]{1,0:T(8,128)S(1)} %shard_map.95.after.own), channel_id=1, source_target_pairs={{0,1},{1,0},{2,3},{3,2},{4,5},{5,4},{6,7},{7,6},{8,9},{9,8},{10,11... | collective-permute-start | bytes 122888 | tf_op jit(solution)/shard_map/ppermute | solution.py:431
  89.2 0.1 shard_map.96
  89.2 0.8 collective-permute-done.2.partner
  90.0 1.0 %shard_map.97 = (f32[59,1024]{1,0:T(8,128)}, f32[59,1024]{1,0:T(8,128)}) custom-call(f32[80,128]{1,0:T(8,128)S(1)} %shard_map.95.after.own, f32[80,128]{1,0:T(8,128)S(1)} %collective-permute-done.2.partner, bf16[9,59,1024]{2,1,0:T(8,128)(2,1)S(1)} %copy-done, f32[59,1024]{1,0:T(8,128)S(1)} %copy-done.1, f32[8,128]{1,0:T(8,128)S(1)} %get-tuple-element.33.steps, ...), custom_call_target="tpu_custom_call" | custom-call | flops 1048576 | bytes 1048576 | tf_op jit(solution)/shard_map/pallas_call | solution.py:481
  (5 shorter events, 0.0 us)
Async XLA Ops:
  3.9 24.5 %copy-start = (bf16[9,59,1024]{2,1,0:T(8,128)(2,1)S(1)}, bf16[9,59,1024]{2,1,0:T(8,128)(2,1)}, u32[]{:S(2)}) copy-start(bf16[9,59,1024]{2,1,0:T(8,128)(2,1)} %proj.7) | copy-start | bytes 3262468
  3.9 24.4 %copy-start.2 = (f32[59,1024]{1,0:T(8,128)S(1)}, f32[59,1024]{1,0:T(8,128)}, u32[]{:S(2)}) copy-start(f32[59,1024]{1,0:T(8,128)} %precond.7) | copy-start | bytes 724996
  26.2 3.4 %collective-permute-start = (f32[80,128]{1,0:T(8,128)S(1)}, f32[80,128]{1,0:T(8,128)S(1)}, u32[]{:S(2)}, u32[]{:S(2)}) collective-permute-start(f32[80,128]{1,0:T(8,128)S(1)} %get-tuple-element.23.after.own), channel_id=1, source_target_pairs={{0,1},{1,0},{2,3},{3,2},{4,5},{5,4},{6,7},{7,6},{8,9},{9,8},{10,11... | collective-permute-start | bytes 122888 | tf_op jit(solution)/shard_map/ppermute | solution.py:431
  40.8 17.8 %copy-start.1 = (f32[59,1024]{1,0:T(8,128)S(1)}, f32[59,1024]{1,0:T(8,128)}, u32[]{:S(2)}) copy-start(f32[59,1024]{1,0:T(8,128)} %damping.5) | copy-start | bytes 724996
  56.0 3.5 %collective-permute-start.1 = (f32[80,128]{1,0:T(8,128)S(1)}, f32[80,128]{1,0:T(8,128)S(1)}, u32[]{:S(2)}, u32[]{:S(2)}) collective-permute-start(f32[80,128]{1,0:T(8,128)S(1)} %shard_map.91.after.own), channel_id=1, source_target_pairs={{0,1},{1,0},{2,3},{3,2},{4,5},{5,4},{6,7},{7,6},{8,9},{9,8},{10,11... | collective-permute-start | bytes 122888 | tf_op jit(solution)/shard_map/ppermute | solution.py:431
  86.2 3.8 %collective-permute-start.2 = (f32[80,128]{1,0:T(8,128)S(1)}, f32[80,128]{1,0:T(8,128)S(1)}, u32[]{:S(2)}, u32[]{:S(2)}) collective-permute-start(f32[80,128]{1,0:T(8,128)S(1)} %shard_map.95.after.own), channel_id=1, source_target_pairs={{0,1},{1,0},{2,3},{3,2},{4,5},{5,4},{6,7},{7,6},{8,9},{9,8},{10,11... | collective-permute-start | bytes 122888 | tf_op jit(solution)/shard_map/ppermute | solution.py:431

commit v10 on v9

--- a/solution.py
+++ b/solution.py
@@ -42,6 +42,12 @@
     stage[pl.ds(n_proj, ids.shape[0], stride=ROWS), :] = ids.astype(F32)
 
 
+def send_return(stage, out):
+    turned = stage[...].T.reshape(out.shape[0], *out.shape[2:])
+    for x in range(out.shape[1]):
+        out[:, x] = turned
+
+
 def pack_return(acc, scalars, stage, out):
     n_blk = acc.shape[0]
     n_proj = acc.shape[1] // LANES
@@ -49,12 +55,12 @@
         stage[pl.ds(k, n_blk, stride=ROWS), :] = acc[:, k * LANES : (k + 1) * LANES]
     for i, value in enumerate(scalars):
         stage[n_proj + 1 + i : n_proj + 2 + i, :] = value
-    turned = stage[...].T.reshape(out.shape[0], *out.shape[2:])
-    for x in range(out.shape[1]):
-        out[:, x] = turned
-
-
-def rhs_kernel(live, jac, pix, ids, out, jbuf, aux, pixels, lives, index, stage, sem, small):
+    send_return(stage, out)
+
+
+def rhs_kernel(
+    live, jac, pix, ids, out, jbuf, aux, pixels, lives, index, stage, spread, sem, small
+):
     n_blk = jac.shape[0]
     minor = [
         pltpu.make_async_copy(pix, pixels, small.at[0]),
@@ -79,15 +85,24 @@
     keep = row < jnp.broadcast_to(own, pix.shape)
     values = jnp.where(keep, pixels[...].astype(F32), 0.0)
     n_pix, n_col = jac.shape[1:]
-    acc = jnp.zeros((n_blk, n_col), F32)
-    cut = n_blk * 3 // 4
-    for first, last in ((0, cut), (cut, n_blk)):
-        signals = [jnp.where(row == b, values, 0.0).astype(BF16) for b in range(first, last)]
-        for copy in copies[first:last]:
-            copy.wait()
-        stacked = jbuf[first:last].reshape((last - first) * n_pix, n_col)
-        acc += jnp.dot(jnp.concatenate(signals, axis=1), stacked, preferred_element_type=F32)
-    pack_return(acc, (), stage, out)
+    for half in range(0, n_pix, LANES):
+        turned = values[:, half : half + LANES].T
+        for b in range(n_blk):
+            spread[b, half : half + LANES, :] = jnp.broadcast_to(
+                turned[:, b : b + 1], (LANES, LANES)
+            )
+    for b, copy in enumerate(copies):
+        copy.wait()
+        sums = [jnp.zeros((16, LANES), F32)] * (n_col // LANES)
+        for top in range(0, n_pix, 16):
+            line = spread[b, top : top + 16, :]
+            for k in range(len(sums)):
+                tile = jbuf[b, top : top + 16, k * LANES : (k + 1) * LANES].astype(F32)
+                sums[k] = sums[k] + tile * line
+        for k, each in enumerate(sums):
+            at = b * ROWS + k
+            stage[at : at + 1, :] = jnp.sum(each, axis=0, keepdims=True)
+    send_return(stage, out)
 
 
 def lane_image(jac, b, line, ones):
@@ -443,6 +458,7 @@
             pltpu.VMEM((1, live_blocks.shape[0]), jnp.int32),
             pltpu.VMEM((n_blk, LANES), jnp.int32),
             square,
+            pltpu.VMEM((n_blk, n_pix, LANES), F32),
             pltpu.SemaphoreType.DMA((n_blk,)),
             pltpu.SemaphoreType.DMA((3,)),
         ],

time: 91.4 us -> 91.7 us (level)
  no operation moved by 1% of the time
where the time goes in v10:
time: 91.7 us; the launch traced here: 91.4 us
  blocking collectives  68.8 us (75%)
  Pallas kernels  13.2 us (14%)
  starting transfers between devices  7.72 us (8%)
    all_to_all x3, blocking collectives, to_owners(): got = lax.all_to_all(flat, ('scene', 'x'), 0, 0, tiled=True)  50.2 us
    all_to_all x2, blocking collectives, to_blocks(): return lax.all_to_all(message, 'scene', 0, 0, tiled=True)  18.6 us
    ppermute x3, starting transfers between devices, to_owners(): partner = lax.ppermute(own, 'core', [(0, 1), (1, 0)])  7.72 us
    pallas_call x1, Pallas kernels, local(): call(rhs_kernel, (wide, whole(jacobian.shape, BF16), whole((2 * n_blk, LA...  3.61 us
    pallas_call x3, Pallas kernels, to_owners(): call(functools.partial(sum_kernel, first), (sums,) + (extra if first else...  2.16 us
  transfers between devices with their start and end apart: 3, of which 2 were waited for; matrix products, arithmetic and copies ran while one was open for 0% of the time, Pallas kernels for 2%

profile of v10, /device:TPU:1, one launch (start us, length us, event | category | flops | bytes accessed | tf_op | source)
XLA Modules:
  0.0 91.4 jit_solution(15452254724473208661)
XLA Ops:
  0.6 3.6 %shard_map.86 = (f32[16,4,8,128]{3,2,1,0:T(8,128)S(1)}, bf16[8,256,1152]{2,1,0:T(8,128)(2,1)S(1)}, s32[16,128]{1,0:T(8,128)S(1)}) custom-call(s32[1,128]{1,0:T(1,128)} %bitcast.13, bf16[8,256,1152]{2,1,0:T(8,128)(2,1)} %jac.1, bf16[8,256]{1,0:T(8,128)(2,1)} %pix.1, s32[8,128]{1,0:T(8,128)} %ids.1), custom_call_target="tpu_custom_call" | custom-call | flops 1048576 | bytes 1048576 | tf_op jit(solution)/shard_map/pallas_call | solution.py:452
  4.3 0.0 copy-start
  4.3 21.4 %all_to_all.25 = f32[64,8,128]{2,1,0:T(8,128)S(1)} all-to-all(f32[64,8,128]{2,1,0:T(8,128)S(1)} %bitcast.9), channel_id=1, replica_groups=mesh['scene'=16,'x'=4,'core'=2] {'scene','x'}, dimensions={0} | all-to-all | bytes 524288 | tf_op jit(solution)/shard_map/all_to_all | solution.py:431
  25.7 0.9 shard_map.87
  26.6 2.1 %collective-permute-start = (f32[80,128]{1,0:T(8,128)S(1)}, f32[80,128]{1,0:T(8,128)S(1)}, u32[]{:S(2)}, u32[]{:S(2)}) collective-permute-start(f32[80,128]{1,0:T(8,128)S(1)} %get-tuple-element.23.after.own), channel_id=1, source_target_pairs={{0,1},{1,0},{2,3},{3,2},{4,5},{5,4},{6,7},{7,6},{8,9},{9,8},{10,11... | collective-permute-start | bytes 122888 | tf_op jit(solution)/shard_map/ppermute | solution.py:446
  28.7 1.2 %shard_map.88.matrix = f32[360,128]{1,0:T(8,128)S(1)} custom-call(f32[80,128]{1,0:T(8,128)S(1)} %get-tuple-element.23.after.own, bf16[9,59,1024]{2,1,0:T(8,128)(2,1)S(1)} %copy-done, f32[59,1024]{1,0:T(8,128)S(1)} %copy-done.2), custom_call_target="tpu_custom_call" | custom-call | flops 2147483648 | bytes 1048576 | tf_op jit(solution)/shard_map/pallas_call | solution.py:467
  29.9 0.3 shard_map.89
  30.2 9.3 %all_to_all.26.recv = f32[16,8,128]{2,1,0:T(8,128)S(1)} all-to-all(f32[16,8,128]{2,1,0:T(8,128)S(1)} %shard_map.89), channel_id=1, replica_groups=mesh['scene'=16,'x'=4,'core'=2] {'scene'}, dimensions={0} | all-to-all | bytes 131072 | tf_op jit(solution)/shard_map/all_to_all | solution.py:450
  39.5 1.7 %shard_map.90 = (f32[16,4,8,128]{3,2,1,0:T(8,128)S(1)}, f32[8,1152]{1,0:T(8,128)S(1)}) custom-call(bf16[8,256,1152]{2,1,0:T(8,128)(2,1)S(1)} %get-tuple-element.20.jac, s32[16,128]{1,0:T(8,128)S(1)} %get-tuple-element.21.aux, f32[16,8,128]{2,1,0:T(8,128)S(1)} %all_to_all.26.recv), custom_call_target="tpu_custom_call" | custom-call | flops 1048576 | bytes 1048576 | tf_op jit(solution)/shard_map/pallas_call | solution.py:475
  41.2 0.0 copy-start.1
  41.2 14.5 %all_to_all.27 = f32[64,8,128]{2,1,0:T(8,128)S(1)} all-to-all(f32[64,8,128]{2,1,0:T(8,128)S(1)} %bitcast.10), channel_id=1, replica_groups=mesh['scene'=16,'x'=4,'core'=2] {'scene','x'}, dimensions={0} | all-to-all | bytes 524288 | tf_op jit(solution)/shard_map/all_to_all | solution.py:431
  55.7 0.6 shard_map.91.after.own
  56.3 2.6 %collective-permute-start.1 = (f32[80,128]{1,0:T(8,128)S(1)}, f32[80,128]{1,0:T(8,128)S(1)}, u32[]{:S(2)}, u32[]{:S(2)}) collective-permute-start(f32[80,128]{1,0:T(8,128)S(1)} %shard_map.91.after.own), channel_id=1, source_target_pairs={{0,1},{1,0},{2,3},{3,2},{4,5},{5,4},{6,7},{7,6},{8,9},{9,8},{10,11... | collective-permute-start | bytes 122888 | tf_op jit(solution)/shard_map/ppermute | solution.py:446
  58.9 0.7 shard_map.92
  59.7 0.1 collective-permute-done.1.partner
  59.8 0.7 shard_map.93
  60.5 9.3 %all_to_all.28.recv = f32[16,8,128]{2,1,0:T(8,128)S(1)} all-to-all(f32[16,8,128]{2,1,0:T(8,128)S(1)} %get-tuple-element.30), channel_id=1, replica_groups=mesh['scene'=16,'x'=4,'core'=2] {'scene'}, dimensions={0} | all-to-all | bytes 131072 | tf_op jit(solution)/shard_map/all_to_all | solution.py:450
  69.8 1.8 %shard_map.94 = (f32[16,4,8,128]{3,2,1,0:T(8,128)S(1)}, f32[8,128]{1,0:T(8,128)S(1)}) custom-call(bf16[8,256,1152]{2,1,0:T(8,128)(2,1)S(1)} %get-tuple-element.20.jac, s32[16,128]{1,0:T(8,128)S(1)} %get-tuple-element.21.aux, f32[16,8,128]{2,1,0:T(8,128)S(1)} %all_to_all.28.recv, f32[8,1152]{1,0:T(8,128)S(1)} %get-tuple-element.31.picks_in), custom_call_target="tpu_custom_call" | custom-call | flops 1048576 | bytes 1048576 | tf_op jit(solution)/shard_map/pallas_call | solution.py:489
  71.6 14.4 %all_to_all.29 = f32[64,8,128]{2,1,0:T(8,128)S(1)} all-to-all(f32[64,8,128]{2,1,0:T(8,128)S(1)} %bitcast.7), channel_id=1, replica_groups=mesh['scene'=16,'x'=4,'core'=2] {'scene','x'}, dimensions={0} | all-to-all | bytes 524288 | tf_op jit(solution)/shard_map/all_to_all | solution.py:431
  85.9 0.6 shard_map.95.after.own
  86.6 2.9 %collective-permute-start.2 = (f32[80,128]{1,0:T(8,128)S(1)}, f32[80,128]{1,0:T(8,128)S(1)}, u32[]{:S(2)}, u32[]{:S(2)}) collective-permute-start(f32[80,128]{1,0:T(8,128)S(1)} %shard_map.95.after.own), channel_id=1, source_target_pairs={{0,1},{1,0},{2,3},{3,2},{4,5},{5,4},{6,7},{7,6},{8,9},{9,8},{10,11... | collective-permute-start | bytes 122888 | tf_op jit(solution)/shard_map/ppermute | solution.py:446
  89.5 0.1 shard_map.96
  89.6 0.8 collective-permute-done.2.partner
  90.4 1.0 %shard_map.97 = (f32[59,1024]{1,0:T(8,128)}, f32[59,1024]{1,0:T(8,128)}) custom-call(f32[80,128]{1,0:T(8,128)S(1)} %shard_map.95.after.own, f32[80,128]{1,0:T(8,128)S(1)} %collective-permute-done.2.partner, bf16[9,59,1024]{2,1,0:T(8,128)(2,1)S(1)} %copy-done, f32[59,1024]{1,0:T(8,128)S(1)} %copy-done.1, f32[8,128]{1,0:T(8,128)S(1)} %get-tuple-element.33.steps, ...), custom_call_target="tpu_custom_call" | custom-call | flops 1048576 | bytes 1048576 | tf_op jit(solution)/shard_map/pallas_call | solution.py:497
  (5 shorter events, 0.0 us)
Async XLA Ops:
  4.3 24.5 %copy-start = (bf16[9,59,1024]{2,1,0:T(8,128)(2,1)S(1)}, bf16[9,59,1024]{2,1,0:T(8,128)(2,1)}, u32[]{:S(2)}) copy-start(bf16[9,59,1024]{2,1,0:T(8,128)(2,1)} %proj.7) | copy-start | bytes 3262468
  4.3 24.4 %copy-start.2 = (f32[59,1024]{1,0:T(8,128)S(1)}, f32[59,1024]{1,0:T(8,128)}, u32[]{:S(2)}) copy-start(f32[59,1024]{1,0:T(8,128)} %precond.7) | copy-start | bytes 724996
  26.6 3.4 %collective-permute-start = (f32[80,128]{1,0:T(8,128)S(1)}, f32[80,128]{1,0:T(8,128)S(1)}, u32[]{:S(2)}, u32[]{:S(2)}) collective-permute-start(f32[80,128]{1,0:T(8,128)S(1)} %get-tuple-element.23.after.own), channel_id=1, source_target_pairs={{0,1},{1,0},{2,3},{3,2},{4,5},{5,4},{6,7},{7,6},{8,9},{9,8},{10,11... | collective-permute-start | bytes 122888 | tf_op jit(solution)/shard_map/ppermute | solution.py:446
  41.2 17.8 %copy-start.1 = (f32[59,1024]{1,0:T(8,128)S(1)}, f32[59,1024]{1,0:T(8,128)}, u32[]{:S(2)}) copy-start(f32[59,1024]{1,0:T(8,128)} %damping.5) | copy-start | bytes 724996
  56.3 3.5 %collective-permute-start.1 = (f32[80,128]{1,0:T(8,128)S(1)}, f32[80,128]{1,0:T(8,128)S(1)}, u32[]{:S(2)}, u32[]{:S(2)}) collective-permute-start(f32[80,128]{1,0:T(8,128)S(1)} %shard_map.91.after.own), channel_id=1, source_target_pairs={{0,1},{1,0},{2,3},{3,2},{4,5},{5,4},{6,7},{7,6},{8,9},{9,8},{10,11... | collective-permute-start | bytes 122888 | tf_op jit(solution)/shard_map/ppermute | solution.py:446
  86.6 3.8 %collective-permute-start.2 = (f32[80,128]{1,0:T(8,128)S(1)}, f32[80,128]{1,0:T(8,128)S(1)}, u32[]{:S(2)}, u32[]{:S(2)}) collective-permute-start(f32[80,128]{1,0:T(8,128)S(1)} %shard_map.95.after.own), channel_id=1, source_target_pairs={{0,1},{1,0},{2,3},{3,2},{4,5},{5,4},{6,7},{7,6},{8,9},{9,8},{10,11... | collective-permute-start | bytes 122888 | tf_op jit(solution)/shard_map/ppermute | solution.py:446

commit v11 on v9

--- a/solution.py
+++ b/solution.py
@@ -80,7 +80,7 @@
     values = jnp.where(keep, pixels[...].astype(F32), 0.0)
     n_pix, n_col = jac.shape[1:]
     acc = jnp.zeros((n_blk, n_col), F32)
-    cut = n_blk * 3 // 4
+    cut = n_blk * 5 // 8
     for first, last in ((0, cut), (cut, n_blk)):
         signals = [jnp.where(row == b, values, 0.0).astype(BF16) for b in range(first, last)]
         for copy in copies[first:last]:
@@ -390,9 +390,9 @@
         res_out[:, cols] = res[:, cols] - alpha * image
         if h == 0:
             send(sol_out, sol_hbm, 0, chunks)
-        elif h % 2 == 0:
-            send(res_out, res_hbm, h - 2, h)
-    send(res_out, res_hbm, chunks - 2, chunks)
+        else:
+            send(res_out, res_hbm, h - 1, h)
+    send(res_out, res_hbm, chunks - 1, chunks)
     for copy in copies:
         copy.wait()
 
@@ -482,7 +482,7 @@
         last_kernel,
         (state, state),
         [VMEM] * 8,
-        [weights, held, held, pltpu.SemaphoreType.DMA((1 + g_dev // (2 * LANES),))],
+        [weights, held, held, pltpu.SemaphoreType.DMA((1 + g_dev // LANES,))],
         out_space=HBM,
     )(
         own, partner, proj_jac, damping, steps, first_dir, res, second_dir

time: 91.4 us -> 91.4 us (level)
  no operation moved by 1% of the time
where the time goes in v11:
time: 91.4 us; the launch traced here: 91.1 us
  blocking collectives  68.8 us (75%)
  Pallas kernels  12.9 us (14%)
  starting transfers between devices  7.73 us (8%)
    all_to_all x3, blocking collectives, to_owners(): got = lax.all_to_all(flat, ('scene', 'x'), 0, 0, tiled=True)  50.2 us
    all_to_all x2, blocking collectives, to_blocks(): return lax.all_to_all(message, 'scene', 0, 0, tiled=True)  18.6 us
    ppermute x3, starting transfers between devices, to_owners(): partner = lax.ppermute(own, 'core', [(0, 1), (1, 0)])  7.73 us
    pallas_call x1, Pallas kernels, local(): call(rhs_kernel, (wide, whole(jacobian.shape, BF16), whole((2 * n_blk, LA...  3.27 us
    pallas_call x3, Pallas kernels, to_owners(): call(functools.partial(sum_kernel, first), (sums,) + (extra if first else...  2.16 us
  transfers between devices with their start and end apart: 3, of which 2 were waited for; matrix products, arithmetic and copies ran while one was open for 0% of the time, Pallas kernels for 2%

profile of v11, /device:TPU:1, one launch (start us, length us, event | category | flops | bytes accessed | tf_op | source)
XLA Modules:
  0.0 91.1 jit_solution(3428752432037973423)
XLA Ops:
  0.6 3.3 %shard_map.86 = (f32[16,4,8,128]{3,2,1,0:T(8,128)S(1)}, bf16[8,256,1152]{2,1,0:T(8,128)(2,1)S(1)}, s32[16,128]{1,0:T(8,128)S(1)}) custom-call(s32[1,128]{1,0:T(1,128)} %bitcast.13, bf16[8,256,1152]{2,1,0:T(8,128)(2,1)} %jac.1, bf16[8,256]{1,0:T(8,128)(2,1)} %pix.1, s32[8,128]{1,0:T(8,128)} %ids.1), custom_call_target="tpu_custom_call" | custom-call | flops 1048576 | bytes 1048576 | tf_op jit(solution)/shard_map/pallas_call | solution.py:437
  3.9 0.0 copy-start
  3.9 0.0 copy-start.2
  3.9 21.4 %all_to_all.25 = f32[64,8,128]{2,1,0:T(8,128)S(1)} all-to-all(f32[64,8,128]{2,1,0:T(8,128)S(1)} %bitcast.9), channel_id=1, replica_groups=mesh['scene'=16,'x'=4,'core'=2] {'scene','x'}, dimensions={0} | all-to-all | bytes 524288 | tf_op jit(solution)/shard_map/all_to_all | solution.py:416
  25.3 0.9 shard_map.87
  26.2 2.1 %collective-permute-start = (f32[80,128]{1,0:T(8,128)S(1)}, f32[80,128]{1,0:T(8,128)S(1)}, u32[]{:S(2)}, u32[]{:S(2)}) collective-permute-start(f32[80,128]{1,0:T(8,128)S(1)} %get-tuple-element.23.after.own), channel_id=1, source_target_pairs={{0,1},{1,0},{2,3},{3,2},{4,5},{5,4},{6,7},{7,6},{8,9},{9,8},{10,11... | collective-permute-start | bytes 122888 | tf_op jit(solution)/shard_map/ppermute | solution.py:431
  28.4 1.2 %shard_map.88.matrix = f32[360,128]{1,0:T(8,128)S(1)} custom-call(f32[80,128]{1,0:T(8,128)S(1)} %get-tuple-element.23.after.own, bf16[9,59,1024]{2,1,0:T(8,128)(2,1)S(1)} %copy-done, f32[59,1024]{1,0:T(8,128)S(1)} %copy-done.2), custom_call_target="tpu_custom_call" | custom-call | flops 2147483648 | bytes 1048576 | tf_op jit(solution)/shard_map/pallas_call | solution.py:451
  29.6 0.3 shard_map.89
  29.9 9.3 %all_to_all.26.recv = f32[16,8,128]{2,1,0:T(8,128)S(1)} all-to-all(f32[16,8,128]{2,1,0:T(8,128)S(1)} %shard_map.89), channel_id=1, replica_groups=mesh['scene'=16,'x'=4,'core'=2] {'scene'}, dimensions={0} | all-to-all | bytes 131072 | tf_op jit(solution)/shard_map/all_to_all | solution.py:435
  39.2 1.7 %shard_map.90 = (f32[16,4,8,128]{3,2,1,0:T(8,128)S(1)}, f32[8,1152]{1,0:T(8,128)S(1)}) custom-call(bf16[8,256,1152]{2,1,0:T(8,128)(2,1)S(1)} %get-tuple-element.20.jac, s32[16,128]{1,0:T(8,128)S(1)} %get-tuple-element.21.aux, f32[16,8,128]{2,1,0:T(8,128)S(1)} %all_to_all.26.recv), custom_call_target="tpu_custom_call" | custom-call | flops 1048576 | bytes 1048576 | tf_op jit(solution)/shard_map/pallas_call | solution.py:459
  40.8 14.5 %all_to_all.27 = f32[64,8,128]{2,1,0:T(8,128)S(1)} all-to-all(f32[64,8,128]{2,1,0:T(8,128)S(1)} %bitcast.10), channel_id=1, replica_groups=mesh['scene'=16,'x'=4,'core'=2] {'scene','x'}, dimensions={0} | all-to-all | bytes 524288 | tf_op jit(solution)/shard_map/all_to_all | solution.py:416
  55.3 0.6 shard_map.91.after.own
  56.0 2.6 %collective-permute-start.1 = (f32[80,128]{1,0:T(8,128)S(1)}, f32[80,128]{1,0:T(8,128)S(1)}, u32[]{:S(2)}, u32[]{:S(2)}) collective-permute-start(f32[80,128]{1,0:T(8,128)S(1)} %shard_map.91.after.own), channel_id=1, source_target_pairs={{0,1},{1,0},{2,3},{3,2},{4,5},{5,4},{6,7},{7,6},{8,9},{9,8},{10,11... | collective-permute-start | bytes 122888 | tf_op jit(solution)/shard_map/ppermute | solution.py:431
  58.6 0.7 shard_map.92
  59.3 0.1 collective-permute-done.1.partner
  59.5 0.7 shard_map.93
  60.1 9.3 %all_to_all.28.recv = f32[16,8,128]{2,1,0:T(8,128)S(1)} all-to-all(f32[16,8,128]{2,1,0:T(8,128)S(1)} %get-tuple-element.30), channel_id=1, replica_groups=mesh['scene'=16,'x'=4,'core'=2] {'scene'}, dimensions={0} | all-to-all | bytes 131072 | tf_op jit(solution)/shard_map/all_to_all | solution.py:435
  69.4 1.8 %shard_map.94 = (f32[16,4,8,128]{3,2,1,0:T(8,128)S(1)}, f32[8,128]{1,0:T(8,128)S(1)}) custom-call(bf16[8,256,1152]{2,1,0:T(8,128)(2,1)S(1)} %get-tuple-element.20.jac, s32[16,128]{1,0:T(8,128)S(1)} %get-tuple-element.21.aux, f32[16,8,128]{2,1,0:T(8,128)S(1)} %all_to_all.28.recv, f32[8,1152]{1,0:T(8,128)S(1)} %get-tuple-element.31.picks_in), custom_call_target="tpu_custom_call" | custom-call | flops 1048576 | bytes 1048576 | tf_op jit(solution)/shard_map/pallas_call | solution.py:473
  71.2 14.4 %all_to_all.29 = f32[64,8,128]{2,1,0:T(8,128)S(1)} all-to-all(f32[64,8,128]{2,1,0:T(8,128)S(1)} %bitcast.7), channel_id=1, replica_groups=mesh['scene'=16,'x'=4,'core'=2] {'scene','x'}, dimensions={0} | all-to-all | bytes 524288 | tf_op jit(solution)/shard_map/all_to_all | solution.py:416
  85.6 0.6 shard_map.95.after.own
  86.2 2.9 %collective-permute-start.2 = (f32[80,128]{1,0:T(8,128)S(1)}, f32[80,128]{1,0:T(8,128)S(1)}, u32[]{:S(2)}, u32[]{:S(2)}) collective-permute-start(f32[80,128]{1,0:T(8,128)S(1)} %shard_map.95.after.own), channel_id=1, source_target_pairs={{0,1},{1,0},{2,3},{3,2},{4,5},{5,4},{6,7},{7,6},{8,9},{9,8},{10,11... | collective-permute-start | bytes 122888 | tf_op jit(solution)/shard_map/ppermute | solution.py:431
  89.2 0.1 shard_map.96
  89.2 0.8 collective-permute-done.2.partner
  90.0 1.1 %shard_map.97 = (f32[59,1024]{1,0:T(8,128)}, f32[59,1024]{1,0:T(8,128)}) custom-call(f32[80,128]{1,0:T(8,128)S(1)} %shard_map.95.after.own, f32[80,128]{1,0:T(8,128)S(1)} %collective-permute-done.2.partner, bf16[9,59,1024]{2,1,0:T(8,128)(2,1)S(1)} %copy-done, f32[59,1024]{1,0:T(8,128)S(1)} %copy-done.1, f32[8,128]{1,0:T(8,128)S(1)} %get-tuple-element.33.steps, ...), custom_call_target="tpu_custom_call" | custom-call | flops 1048576 | bytes 1048576 | tf_op jit(solution)/shard_map/pallas_call | solution.py:481
  (5 shorter events, 0.0 us)
Async XLA Ops:
  3.9 24.5 %copy-start = (bf16[9,59,1024]{2,1,0:T(8,128)(2,1)S(1)}, bf16[9,59,1024]{2,1,0:T(8,128)(2,1)}, u32[]{:S(2)}) copy-start(bf16[9,59,1024]{2,1,0:T(8,128)(2,1)} %proj.7) | copy-start | bytes 3262468
  3.9 24.4 %copy-start.2 = (f32[59,1024]{1,0:T(8,128)S(1)}, f32[59,1024]{1,0:T(8,128)}, u32[]{:S(2)}) copy-start(f32[59,1024]{1,0:T(8,128)} %precond.7) | copy-start | bytes 724996
  26.2 3.4 %collective-permute-start = (f32[80,128]{1,0:T(8,128)S(1)}, f32[80,128]{1,0:T(8,128)S(1)}, u32[]{:S(2)}, u32[]{:S(2)}) collective-permute-start(f32[80,128]{1,0:T(8,128)S(1)} %get-tuple-element.23.after.own), channel_id=1, source_target_pairs={{0,1},{1,0},{2,3},{3,2},{4,5},{5,4},{6,7},{7,6},{8,9},{9,8},{10,11... | collective-permute-start | bytes 122888 | tf_op jit(solution)/shard_map/ppermute | solution.py:431
  40.8 17.8 %copy-start.1 = (f32[59,1024]{1,0:T(8,128)S(1)}, f32[59,1024]{1,0:T(8,128)}, u32[]{:S(2)}) copy-start(f32[59,1024]{1,0:T(8,128)} %damping.5) | copy-start | bytes 724996
  56.0 3.5 %collective-permute-start.1 = (f32[80,128]{1,0:T(8,128)S(1)}, f32[80,128]{1,0:T(8,128)S(1)}, u32[]{:S(2)}, u32[]{:S(2)}) collective-permute-start(f32[80,128]{1,0:T(8,128)S(1)} %shard_map.91.after.own), channel_id=1, source_target_pairs={{0,1},{1,0},{2,3},{3,2},{4,5},{5,4},{6,7},{7,6},{8,9},{9,8},{10,11... | collective-permute-start | bytes 122888 | tf_op jit(solution)/shard_map/ppermute | solution.py:431
  86.2 3.8 %collective-permute-start.2 = (f32[80,128]{1,0:T(8,128)S(1)}, f32[80,128]{1,0:T(8,128)S(1)}, u32[]{:S(2)}, u32[]{:S(2)}) collective-permute-start(f32[80,128]{1,0:T(8,128)S(1)} %shard_map.95.after.own), channel_id=1, source_target_pairs={{0,1},{1,0},{2,3},{3,2},{4,5},{5,4},{6,7},{7,6},{8,9},{9,8},{10,11... | collective-permute-start | bytes 122888 | tf_op jit(solution)/shard_map/ppermute | solution.py:431

commit v12 on v9

--- a/solution.py
+++ b/solution.py
@@ -149,7 +149,7 @@
     fresh = unpack_picks(recv, turned, n_blk, n_proj)
     per = recv.shape[1]
     totals = over_lanes(turned[8:16, :]) * (1.0 / per)
-    rz, curve, square, damped, mixed, scaled = (totals[i : i + 1, :] for i in range(2, 8))
+    rz, damped, curve, square, mixed, scaled = (totals[i : i + 1, :] for i in range(2, 8))
     alpha = rz / curve
     after = rz - 2.0 * alpha * curve + alpha * alpha * square
     beta = after / rz
@@ -322,21 +322,27 @@
 
 
 def state_kernel(
-    after, own, partner, proj, precond, damping, res_out, dir_out, cross, rz_out, weights
+    after, own, partner, proj, precond, damping,
+    res_out, dir_out, cross, rz_out, wide_proj, weights,
 ):
     del after
     weights[...] = own[...] + partner[...]
     n_par, width = precond.shape
-    rz = jnp.zeros((n_par, LANES), F32)
+    rz, damped = jnp.zeros((n_par, LANES), F32), jnp.zeros((n_par, LANES), F32)
     for h in range(width // LANES):
         cols = slice(h * LANES, (h + 1) * LANES)
+        for k in range(proj.shape[0]):
+            wide_proj[k, :, cols] = proj[k, :, cols].astype(F32)
         res = -lifted(proj, weights, h)
         dirn = precond[:, cols] * res
         res_out[:, cols] = res
         dir_out[:, cols] = dirn
         rz += res * dirn
-        projected(proj, precond[:, cols] * damping[:, cols] * dirn, h, cross)
-    rz_out[...] = jnp.full(rz_out.shape, jnp.sum(rz), F32)
+        pull = damping[:, cols] * dirn
+        damped += pull * dirn
+        projected(proj, precond[:, cols] * pull, h, cross)
+    rz_out[0:4, :] = jnp.full((4, LANES), jnp.sum(rz), F32)
+    rz_out[4:8, :] = jnp.full((4, LANES), jnp.sum(damped), F32)
 
 
 def step_kernel(
@@ -347,7 +353,7 @@
     n_par, width = precond.shape
     for k, tile in enumerate(blended(matrix, weights)):
         table[k * 8 : k * 8 + 8, :] = tile + cross[k * 8 : k * 8 + 8, :]
-    curve, square, damped, mixed, scaled = [jnp.zeros((n_par, LANES), F32)] * 5
+    curve, square, mixed, scaled = [jnp.zeros((n_par, LANES), F32)] * 4
     for h in range(width // LANES):
         cols = slice(h * LANES, (h + 1) * LANES)
         pull = damping[:, cols] * dirn[:, cols]
@@ -356,11 +362,11 @@
         change = precond[:, cols] * image
         curve += dirn[:, cols] * image
         square += change * image
-        damped += pull * dirn[:, cols]
         mixed += pull * change
         scaled += damping[:, cols] * change * change
-    lines = [jnp.sum(each, axis=0, keepdims=True) for each in (curve, square, damped, mixed, scaled)]
-    send_picks(table, ids, (rz_in[0:1, :], over_lanes(jnp.concatenate(lines, axis=0))), stage, out)
+    lines = [jnp.sum(each, axis=0, keepdims=True) for each in (curve, square, mixed, scaled)]
+    totals = over_lanes(jnp.concatenate(lines, axis=0))
+    send_picks(table, ids, (rz_in[0:1, :], rz_in[4:5, :], totals), stage, out)
 
 
 def last_kernel(
@@ -463,11 +469,15 @@
         [square, square],
     )(jac, aux, arrived)
     own, partner = to_owners(message, right)
-    res, first_dir, cross, rz = call(
-        state_kernel, (state, state, f32(72, LANES), f32(8, LANES)), [VMEM] * 6, [weights], 1 << 31
+    res, first_dir, cross, rz, wide_proj = call(
+        state_kernel,
+        (state, state, f32(72, LANES), f32(8, LANES), f32(*proj_jac.shape)),
+        [VMEM] * 6,
+        [weights],
+        1 << 31,
     )(own, first_own, first_partner, proj_jac, precond, damping)
     message, image = call(step_kernel, (msg, state), [VMEM] * 10, [weights, table, square])(
-        own, partner, proj_jac, precond, damping, matrix, cross, rz, index, first_dir
+        own, partner, wide_proj, precond, damping, matrix, cross, rz, index, first_dir
     )
     arrived = to_blocks(message)
     message, steps = call(
@@ -485,7 +495,7 @@
         [weights, held, held, pltpu.SemaphoreType.DMA((1 + g_dev // (2 * LANES),))],
         out_space=HBM,
     )(
-        own, partner, proj_jac, damping, steps, first_dir, res, second_dir
+        own, partner, wide_proj, damping, steps, first_dir, res, second_dir
     )
 
 

time: 91.4 us -> 91.4 us (level)
  transfers between devices with their start and end apart: 3 -> 3, of which waited for: 2 -> 1; matrix products, arithmetic and copies ran while one was open for 0% -> 0% of each run, Pallas kernels for 2% -> 3%
where the time goes in v12:
time: 91.4 us; the launch traced here: 91.1 us
  blocking collectives  68.8 us (75%)
  Pallas kernels  13.2 us (14%)
  starting transfers between devices  7.57 us (8%)
    all_to_all x3, blocking collectives, to_owners(): got = lax.all_to_all(flat, ('scene', 'x'), 0, 0, tiled=True)  50.2 us
    all_to_all x2, blocking collectives, to_blocks(): return lax.all_to_all(message, 'scene', 0, 0, tiled=True)  18.6 us
    ppermute x3, starting transfers between devices, to_owners(): partner = lax.ppermute(own, 'core', [(0, 1), (1, 0)])  7.57 us
    pallas_call x1, Pallas kernels, local(): call(rhs_kernel, (wide, whole(jacobian.shape, BF16), whole((2 * n_blk, LA...  3.27 us
    pallas_call x3, Pallas kernels, to_owners(): call(functools.partial(sum_kernel, first), (sums,) + (extra if first else...  2.15 us
  transfers between devices with their start and end apart: 3, of which 1 were waited for; matrix products, arithmetic and copies ran while one was open for 0% of the time, Pallas kernels for 3%

profile of v12, /device:TPU:1, one launch (start us, length us, event | category | flops | bytes accessed | tf_op | source)
XLA Modules:
  0.0 91.1 jit_solution(4090182324535630021)
XLA Ops:
  0.6 3.3 %shard_map.86 = (f32[16,4,8,128]{3,2,1,0:T(8,128)S(1)}, bf16[8,256,1152]{2,1,0:T(8,128)(2,1)S(1)}, s32[16,128]{1,0:T(8,128)S(1)}) custom-call(s32[1,128]{1,0:T(1,128)} %bitcast.13, bf16[8,256,1152]{2,1,0:T(8,128)(2,1)} %jac.1, bf16[8,256]{1,0:T(8,128)(2,1)} %pix.1, s32[8,128]{1,0:T(8,128)} %ids.1), custom_call_target="tpu_custom_call" | custom-call | flops 1048576 | bytes 1048576 | tf_op jit(solution)/shard_map/pallas_call | solution.py:443
  3.9 0.0 copy-start.1
  3.9 0.0 copy-start.2
  3.9 21.4 %all_to_all.25 = f32[64,8,128]{2,1,0:T(8,128)S(1)} all-to-all(f32[64,8,128]{2,1,0:T(8,128)S(1)} %bitcast.9), channel_id=1, replica_groups=mesh['scene'=16,'x'=4,'core'=2] {'scene','x'}, dimensions={0} | all-to-all | bytes 524288 | tf_op jit(solution)/shard_map/all_to_all | solution.py:422
  25.3 0.9 shard_map.87
  26.2 2.1 %collective-permute-start = (f32[80,128]{1,0:T(8,128)S(1)}, f32[80,128]{1,0:T(8,128)S(1)}, u32[]{:S(2)}, u32[]{:S(2)}) collective-permute-start(f32[80,128]{1,0:T(8,128)S(1)} %get-tuple-element.24.after.own), channel_id=1, source_target_pairs={{0,1},{1,0},{2,3},{3,2},{4,5},{5,4},{6,7},{7,6},{8,9},{9,8},{10,11... | collective-permute-start | bytes 122888 | tf_op jit(solution)/shard_map/ppermute | solution.py:437
  28.4 1.2 %shard_map.88.matrix = f32[360,128]{1,0:T(8,128)S(1)} custom-call(f32[80,128]{1,0:T(8,128)S(1)} %get-tuple-element.24.after.own, bf16[9,59,1024]{2,1,0:T(8,128)(2,1)S(1)} %copy-done.2, f32[59,1024]{1,0:T(8,128)S(1)} %copy-done.1), custom_call_target="tpu_custom_call" | custom-call | flops 2147483648 | bytes 1048576 | tf_op jit(solution)/shard_map/pallas_call | solution.py:457
  29.6 0.3 shard_map.89
  29.9 9.3 %all_to_all.26.recv = f32[16,8,128]{2,1,0:T(8,128)S(1)} all-to-all(f32[16,8,128]{2,1,0:T(8,128)S(1)} %shard_map.89), channel_id=1, replica_groups=mesh['scene'=16,'x'=4,'core'=2] {'scene'}, dimensions={0} | all-to-all | bytes 131072 | tf_op jit(solution)/shard_map/all_to_all | solution.py:441
  39.2 1.7 %shard_map.90 = (f32[16,4,8,128]{3,2,1,0:T(8,128)S(1)}, f32[8,1152]{1,0:T(8,128)S(1)}) custom-call(bf16[8,256,1152]{2,1,0:T(8,128)(2,1)S(1)} %get-tuple-element.21.jac, s32[16,128]{1,0:T(8,128)S(1)} %get-tuple-element.22.aux, f32[16,8,128]{2,1,0:T(8,128)S(1)} %all_to_all.26.recv), custom_call_target="tpu_custom_call" | custom-call | flops 1048576 | bytes 1048576 | tf_op jit(solution)/shard_map/pallas_call | solution.py:465
  40.8 0.0 copy-start
  40.8 14.5 %all_to_all.27 = f32[64,8,128]{2,1,0:T(8,128)S(1)} all-to-all(f32[64,8,128]{2,1,0:T(8,128)S(1)} %bitcast.10), channel_id=1, replica_groups=mesh['scene'=16,'x'=4,'core'=2] {'scene','x'}, dimensions={0} | all-to-all | bytes 524288 | tf_op jit(solution)/shard_map/all_to_all | solution.py:422
  55.3 0.6 shard_map.91.after.own
  56.0 2.6 %collective-permute-start.1 = (f32[80,128]{1,0:T(8,128)S(1)}, f32[80,128]{1,0:T(8,128)S(1)}, u32[]{:S(2)}, u32[]{:S(2)}) collective-permute-start(f32[80,128]{1,0:T(8,128)S(1)} %shard_map.91.after.own), channel_id=1, source_target_pairs={{0,1},{1,0},{2,3},{3,2},{4,5},{5,4},{6,7},{7,6},{8,9},{9,8},{10,11... | collective-permute-start | bytes 122888 | tf_op jit(solution)/shard_map/ppermute | solution.py:437
  58.6 1.0 %shard_map.92 = (f32[59,1024]{1,0:T(8,128)S(1)}, f32[59,1024]{1,0:T(8,128)S(1)}, f32[72,128]{1,0:T(8,128)S(1)}, f32[8,128]{1,0:T(8,128)S(1)}, f32[9,59,1024]{2,1,0:T(8,128)S(1)}) custom-call(f32[80,128]{1,0:T(8,128)S(1)} %shard_map.91.after.own, f32[80,128]{1,0:T(8,128)S(1)} %get-tuple-element.24.after.own, f32[80,128]{1,0:T(8,128)S(1)} %collective-permute-done.partner, ...), custom_call_target="tpu_custom_call" | custom-call | flops 2147483648 | bytes 1048576 | tf_op jit(solution)/shard_map/pallas_call | solution.py:472
  59.6 0.7 shard_map.93
  60.3 9.3 %all_to_all.28.recv = f32[16,8,128]{2,1,0:T(8,128)S(1)} all-to-all(f32[16,8,128]{2,1,0:T(8,128)S(1)} %get-tuple-element.32), channel_id=1, replica_groups=mesh['scene'=16,'x'=4,'core'=2] {'scene'}, dimensions={0} | all-to-all | bytes 131072 | tf_op jit(solution)/shard_map/all_to_all | solution.py:441
  69.6 1.8 %shard_map.94 = (f32[16,4,8,128]{3,2,1,0:T(8,128)S(1)}, f32[8,128]{1,0:T(8,128)S(1)}) custom-call(bf16[8,256,1152]{2,1,0:T(8,128)(2,1)S(1)} %get-tuple-element.21.jac, s32[16,128]{1,0:T(8,128)S(1)} %get-tuple-element.22.aux, f32[16,8,128]{2,1,0:T(8,128)S(1)} %all_to_all.28.recv, f32[8,1152]{1,0:T(8,128)S(1)} %get-tuple-element.33.picks_in), custom_call_target="tpu_custom_call" | custom-call | flops 1048576 | bytes 1048576 | tf_op jit(solution)/shard_map/pallas_call | solution.py:483
  71.4 14.3 %all_to_all.29 = f32[64,8,128]{2,1,0:T(8,128)S(1)} all-to-all(f32[64,8,128]{2,1,0:T(8,128)S(1)} %bitcast.7), channel_id=1, replica_groups=mesh['scene'=16,'x'=4,'core'=2] {'scene','x'}, dimensions={0} | all-to-all | bytes 524288 | tf_op jit(solution)/shard_map/all_to_all | solution.py:422
  85.8 0.6 shard_map.95.after.own
  86.4 2.8 %collective-permute-start.2 = (f32[80,128]{1,0:T(8,128)S(1)}, f32[80,128]{1,0:T(8,128)S(1)}, u32[]{:S(2)}, u32[]{:S(2)}) collective-permute-start(f32[80,128]{1,0:T(8,128)S(1)} %shard_map.95.after.own), channel_id=1, source_target_pairs={{0,1},{1,0},{2,3},{3,2},{4,5},{5,4},{6,7},{7,6},{8,9},{9,8},{10,11... | collective-permute-start | bytes 122888 | tf_op jit(solution)/shard_map/ppermute | solution.py:437
  89.2 0.1 shard_map.96
  89.3 0.8 collective-permute-done.2.partner
  90.1 1.1 %shard_map.97 = (f32[59,1024]{1,0:T(8,128)}, f32[59,1024]{1,0:T(8,128)}) custom-call(f32[80,128]{1,0:T(8,128)S(1)} %shard_map.95.after.own, f32[80,128]{1,0:T(8,128)S(1)} %collective-permute-done.2.partner, f32[9,59,1024]{2,1,0:T(8,128)S(1)} %get-tuple-element.28.proj, f32[59,1024]{1,0:T(8,128)S(1)} %copy-done, f32[8,128]{1,0:T(8,128)S(1)} %get-tuple-element.35.steps, ...), custom_call_target="tpu_custom_call" | custom-call | flops 1048576 | bytes 1048576 | tf_op jit(solution)/shard_map/pallas_call | solution.py:491
  (5 shorter events, 0.0 us)
Async XLA Ops:
  3.9 24.5 %copy-start.1 = (f32[59,1024]{1,0:T(8,128)S(1)}, f32[59,1024]{1,0:T(8,128)}, u32[]{:S(2)}) copy-start(f32[59,1024]{1,0:T(8,128)} %precond.7) | copy-start | bytes 724996
  3.9 24.4 %copy-start.2 = (bf16[9,59,1024]{2,1,0:T(8,128)(2,1)S(1)}, bf16[9,59,1024]{2,1,0:T(8,128)(2,1)}, u32[]{:S(2)}) copy-start(bf16[9,59,1024]{2,1,0:T(8,128)(2,1)} %proj.3) | copy-start | bytes 3262468
  26.2 3.4 %collective-permute-start = (f32[80,128]{1,0:T(8,128)S(1)}, f32[80,128]{1,0:T(8,128)S(1)}, u32[]{:S(2)}, u32[]{:S(2)}) collective-permute-start(f32[80,128]{1,0:T(8,128)S(1)} %get-tuple-element.24.after.own), channel_id=1, source_target_pairs={{0,1},{1,0},{2,3},{3,2},{4,5},{5,4},{6,7},{7,6},{8,9},{9,8},{10,11... | collective-permute-start | bytes 122888 | tf_op jit(solution)/shard_map/ppermute | solution.py:437
  40.8 17.8 %copy-start = (f32[59,1024]{1,0:T(8,128)S(1)}, f32[59,1024]{1,0:T(8,128)}, u32[]{:S(2)}) copy-start(f32[59,1024]{1,0:T(8,128)} %damping.5) | copy-start | bytes 724996
  56.0 3.7 %collective-permute-start.1 = (f32[80,128]{1,0:T(8,128)S(1)}, f32[80,128]{1,0:T(8,128)S(1)}, u32[]{:S(2)}, u32[]{:S(2)}) collective-permute-start(f32[80,128]{1,0:T(8,128)S(1)} %shard_map.91.after.own), channel_id=1, source_target_pairs={{0,1},{1,0},{2,3},{3,2},{4,5},{5,4},{6,7},{7,6},{8,9},{9,8},{10,11... | collective-permute-start | bytes 122888 | tf_op jit(solution)/shard_map/ppermute | solution.py:437
  86.4 3.7 %collective-permute-start.2 = (f32[80,128]{1,0:T(8,128)S(1)}, f32[80,128]{1,0:T(8,128)S(1)}, u32[]{:S(2)}, u32[]{:S(2)}) collective-permute-start(f32[80,128]{1,0:T(8,128)S(1)} %shard_map.95.after.own), channel_id=1, source_target_pairs={{0,1},{1,0},{2,3},{3,2},{4,5},{5,4},{6,7},{7,6},{8,9},{9,8},{10,11... | collective-permute-start | bytes 122888 | tf_op jit(solution)/shard_map/ppermute | solution.py:437

commit v13 on v9

--- a/solution.py
+++ b/solution.py
@@ -390,9 +390,9 @@
         res_out[:, cols] = res[:, cols] - alpha * image
         if h == 0:
             send(sol_out, sol_hbm, 0, chunks)
-        elif h % 2 == 0:
-            send(res_out, res_hbm, h - 2, h)
-    send(res_out, res_hbm, chunks - 2, chunks)
+        elif h == chunks // 2 + 1:
+            send(res_out, res_hbm, 0, chunks // 2)
+    send(res_out, res_hbm, chunks // 2, chunks)
     for copy in copies:
         copy.wait()
 
@@ -482,7 +482,7 @@
         last_kernel,
         (state, state),
         [VMEM] * 8,
-        [weights, held, held, pltpu.SemaphoreType.DMA((1 + g_dev // (2 * LANES),))],
+        [weights, held, held, pltpu.SemaphoreType.DMA((3,))],
         out_space=HBM,
     )(
         own, partner, proj_jac, damping, steps, first_dir, res, second_dir

time: 91.4 us -> 91.4 us (level)
  no operation moved by 1% of the time
where the time goes in v13:
time: 91.4 us; the launch traced here: 91.1 us
  blocking collectives  68.8 us (75%)
  Pallas kernels  12.9 us (14%)
  starting transfers between devices  7.73 us (8%)
    all_to_all x3, blocking collectives, to_owners(): got = lax.all_to_all(flat, ('scene', 'x'), 0, 0, tiled=True)  50.2 us
    all_to_all x2, blocking collectives, to_blocks(): return lax.all_to_all(message, 'scene', 0, 0, tiled=True)  18.6 us
    ppermute x3, starting transfers between devices, to_owners(): partner = lax.ppermute(own, 'core', [(0, 1), (1, 0)])  7.73 us
    pallas_call x1, Pallas kernels, local(): call(rhs_kernel, (wide, whole(jacobian.shape, BF16), whole((2 * n_blk, LA...  3.27 us
    pallas_call x3, Pallas kernels, to_owners(): call(functools.partial(sum_kernel, first), (sums,) + (extra if first else...  2.16 us
  transfers between devices with their start and end apart: 3, of which 2 were waited for; matrix products, arithmetic and copies ran while one was open for 0% of the time, Pallas kernels for 2%

profile of v13, /device:TPU:1, one launch (start us, length us, event | category | flops | bytes accessed | tf_op | source)
XLA Modules:
  0.0 91.1 jit_solution(327679456267505035)
XLA Ops:
  0.6 3.3 %shard_map.86 = (f32[16,4,8,128]{3,2,1,0:T(8,128)S(1)}, bf16[8,256,1152]{2,1,0:T(8,128)(2,1)S(1)}, s32[16,128]{1,0:T(8,128)S(1)}) custom-call(s32[1,128]{1,0:T(1,128)} %bitcast.13, bf16[8,256,1152]{2,1,0:T(8,128)(2,1)} %jac.1, bf16[8,256]{1,0:T(8,128)(2,1)} %pix.1, s32[8,128]{1,0:T(8,128)} %ids.1), custom_call_target="tpu_custom_call" | custom-call | flops 1048576 | bytes 1048576 | tf_op jit(solution)/shard_map/pallas_call | solution.py:437
  3.9 0.0 copy-start
  3.9 0.0 copy-start.2
  3.9 21.4 %all_to_all.25 = f32[64,8,128]{2,1,0:T(8,128)S(1)} all-to-all(f32[64,8,128]{2,1,0:T(8,128)S(1)} %bitcast.9), channel_id=1, replica_groups=mesh['scene'=16,'x'=4,'core'=2] {'scene','x'}, dimensions={0} | all-to-all | bytes 524288 | tf_op jit(solution)/shard_map/all_to_all | solution.py:416
  25.3 0.9 shard_map.87
  26.2 2.1 %collective-permute-start = (f32[80,128]{1,0:T(8,128)S(1)}, f32[80,128]{1,0:T(8,128)S(1)}, u32[]{:S(2)}, u32[]{:S(2)}) collective-permute-start(f32[80,128]{1,0:T(8,128)S(1)} %get-tuple-element.23.after.own), channel_id=1, source_target_pairs={{0,1},{1,0},{2,3},{3,2},{4,5},{5,4},{6,7},{7,6},{8,9},{9,8},{10,11... | collective-permute-start | bytes 122888 | tf_op jit(solution)/shard_map/ppermute | solution.py:431
  28.4 1.2 %shard_map.88.matrix = f32[360,128]{1,0:T(8,128)S(1)} custom-call(f32[80,128]{1,0:T(8,128)S(1)} %get-tuple-element.23.after.own, bf16[9,59,1024]{2,1,0:T(8,128)(2,1)S(1)} %copy-done, f32[59,1024]{1,0:T(8,128)S(1)} %copy-done.2), custom_call_target="tpu_custom_call" | custom-call | flops 2147483648 | bytes 1048576 | tf_op jit(solution)/shard_map/pallas_call | solution.py:451
  29.6 0.3 shard_map.89
  29.9 9.3 %all_to_all.26.recv = f32[16,8,128]{2,1,0:T(8,128)S(1)} all-to-all(f32[16,8,128]{2,1,0:T(8,128)S(1)} %shard_map.89), channel_id=1, replica_groups=mesh['scene'=16,'x'=4,'core'=2] {'scene'}, dimensions={0} | all-to-all | bytes 131072 | tf_op jit(solution)/shard_map/all_to_all | solution.py:435
  39.2 1.7 %shard_map.90 = (f32[16,4,8,128]{3,2,1,0:T(8,128)S(1)}, f32[8,1152]{1,0:T(8,128)S(1)}) custom-call(bf16[8,256,1152]{2,1,0:T(8,128)(2,1)S(1)} %get-tuple-element.20.jac, s32[16,128]{1,0:T(8,128)S(1)} %get-tuple-element.21.aux, f32[16,8,128]{2,1,0:T(8,128)S(1)} %all_to_all.26.recv), custom_call_target="tpu_custom_call" | custom-call | flops 1048576 | bytes 1048576 | tf_op jit(solution)/shard_map/pallas_call | solution.py:459
  40.8 14.5 %all_to_all.27 = f32[64,8,128]{2,1,0:T(8,128)S(1)} all-to-all(f32[64,8,128]{2,1,0:T(8,128)S(1)} %bitcast.10), channel_id=1, replica_groups=mesh['scene'=16,'x'=4,'core'=2] {'scene','x'}, dimensions={0} | all-to-all | bytes 524288 | tf_op jit(solution)/shard_map/all_to_all | solution.py:416
  55.3 0.6 shard_map.91.after.own
  56.0 2.6 %collective-permute-start.1 = (f32[80,128]{1,0:T(8,128)S(1)}, f32[80,128]{1,0:T(8,128)S(1)}, u32[]{:S(2)}, u32[]{:S(2)}) collective-permute-start(f32[80,128]{1,0:T(8,128)S(1)} %shard_map.91.after.own), channel_id=1, source_target_pairs={{0,1},{1,0},{2,3},{3,2},{4,5},{5,4},{6,7},{7,6},{8,9},{9,8},{10,11... | collective-permute-start | bytes 122888 | tf_op jit(solution)/shard_map/ppermute | solution.py:431
  58.6 0.7 shard_map.92
  59.3 0.1 collective-permute-done.1.partner
  59.5 0.7 shard_map.93
  60.1 9.3 %all_to_all.28.recv = f32[16,8,128]{2,1,0:T(8,128)S(1)} all-to-all(f32[16,8,128]{2,1,0:T(8,128)S(1)} %get-tuple-element.30), channel_id=1, replica_groups=mesh['scene'=16,'x'=4,'core'=2] {'scene'}, dimensions={0} | all-to-all | bytes 131072 | tf_op jit(solution)/shard_map/all_to_all | solution.py:435
  69.4 1.8 %shard_map.94 = (f32[16,4,8,128]{3,2,1,0:T(8,128)S(1)}, f32[8,128]{1,0:T(8,128)S(1)}) custom-call(bf16[8,256,1152]{2,1,0:T(8,128)(2,1)S(1)} %get-tuple-element.20.jac, s32[16,128]{1,0:T(8,128)S(1)} %get-tuple-element.21.aux, f32[16,8,128]{2,1,0:T(8,128)S(1)} %all_to_all.28.recv, f32[8,1152]{1,0:T(8,128)S(1)} %get-tuple-element.31.picks_in), custom_call_target="tpu_custom_call" | custom-call | flops 1048576 | bytes 1048576 | tf_op jit(solution)/shard_map/pallas_call | solution.py:473
  71.2 14.4 %all_to_all.29 = f32[64,8,128]{2,1,0:T(8,128)S(1)} all-to-all(f32[64,8,128]{2,1,0:T(8,128)S(1)} %bitcast.7), channel_id=1, replica_groups=mesh['scene'=16,'x'=4,'core'=2] {'scene','x'}, dimensions={0} | all-to-all | bytes 524288 | tf_op jit(solution)/shard_map/all_to_all | solution.py:416
  85.6 0.6 shard_map.95.after.own
  86.2 2.9 %collective-permute-start.2 = (f32[80,128]{1,0:T(8,128)S(1)}, f32[80,128]{1,0:T(8,128)S(1)}, u32[]{:S(2)}, u32[]{:S(2)}) collective-permute-start(f32[80,128]{1,0:T(8,128)S(1)} %shard_map.95.after.own), channel_id=1, source_target_pairs={{0,1},{1,0},{2,3},{3,2},{4,5},{5,4},{6,7},{7,6},{8,9},{9,8},{10,11... | collective-permute-start | bytes 122888 | tf_op jit(solution)/shard_map/ppermute | solution.py:431
  89.2 0.1 shard_map.96
  89.2 0.8 collective-permute-done.2.partner
  90.0 1.0 %shard_map.97 = (f32[59,1024]{1,0:T(8,128)}, f32[59,1024]{1,0:T(8,128)}) custom-call(f32[80,128]{1,0:T(8,128)S(1)} %shard_map.95.after.own, f32[80,128]{1,0:T(8,128)S(1)} %collective-permute-done.2.partner, bf16[9,59,1024]{2,1,0:T(8,128)(2,1)S(1)} %copy-done, f32[59,1024]{1,0:T(8,128)S(1)} %copy-done.1, f32[8,128]{1,0:T(8,128)S(1)} %get-tuple-element.33.steps, ...), custom_call_target="tpu_custom_call" | custom-call | flops 1048576 | bytes 1048576 | tf_op jit(solution)/shard_map/pallas_call | solution.py:481
  (5 shorter events, 0.0 us)
Async XLA Ops:
  3.9 24.5 %copy-start = (bf16[9,59,1024]{2,1,0:T(8,128)(2,1)S(1)}, bf16[9,59,1024]{2,1,0:T(8,128)(2,1)}, u32[]{:S(2)}) copy-start(bf16[9,59,1024]{2,1,0:T(8,128)(2,1)} %proj.7) | copy-start | bytes 3262468
  3.9 24.4 %copy-start.2 = (f32[59,1024]{1,0:T(8,128)S(1)}, f32[59,1024]{1,0:T(8,128)}, u32[]{:S(2)}) copy-start(f32[59,1024]{1,0:T(8,128)} %precond.7) | copy-start | bytes 724996
  26.2 3.4 %collective-permute-start = (f32[80,128]{1,0:T(8,128)S(1)}, f32[80,128]{1,0:T(8,128)S(1)}, u32[]{:S(2)}, u32[]{:S(2)}) collective-permute-start(f32[80,128]{1,0:T(8,128)S(1)} %get-tuple-element.23.after.own), channel_id=1, source_target_pairs={{0,1},{1,0},{2,3},{3,2},{4,5},{5,4},{6,7},{7,6},{8,9},{9,8},{10,11... | collective-permute-start | bytes 122888 | tf_op jit(solution)/shard_map/ppermute | solution.py:431
  40.8 17.8 %copy-start.1 = (f32[59,1024]{1,0:T(8,128)S(1)}, f32[59,1024]{1,0:T(8,128)}, u32[]{:S(2)}) copy-start(f32[59,1024]{1,0:T(8,128)} %damping.5) | copy-start | bytes 724996
  56.0 3.5 %collective-permute-start.1 = (f32[80,128]{1,0:T(8,128)S(1)}, f32[80,128]{1,0:T(8,128)S(1)}, u32[]{:S(2)}, u32[]{:S(2)}) collective-permute-start(f32[80,128]{1,0:T(8,128)S(1)} %shard_map.91.after.own), channel_id=1, source_target_pairs={{0,1},{1,0},{2,3},{3,2},{4,5},{5,4},{6,7},{7,6},{8,9},{9,8},{10,11... | collective-permute-start | bytes 122888 | tf_op jit(solution)/shard_map/ppermute | solution.py:431
  86.2 3.8 %collective-permute-start.2 = (f32[80,128]{1,0:T(8,128)S(1)}, f32[80,128]{1,0:T(8,128)S(1)}, u32[]{:S(2)}, u32[]{:S(2)}) collective-permute-start(f32[80,128]{1,0:T(8,128)S(1)} %shard_map.95.after.own), channel_id=1, source_target_pairs={{0,1},{1,0},{2,3},{3,2},{4,5},{5,4},{6,7},{7,6},{8,9},{9,8},{10,11... | collective-permute-start | bytes 122888 | tf_op jit(solution)/shard_map/ppermute | solution.py:431

commit v14 on v9

--- a/solution.py
+++ b/solution.py
@@ -62,8 +62,10 @@
         pltpu.make_async_copy(ids, index, small.at[2]),
     ]
     copies = [pltpu.make_async_copy(jac.at[b], jbuf.at[b], sem.at[b]) for b in range(n_blk)]
-    for copy in minor + copies:
+    for copy in minor:
         copy.start()
+    for b, copy in enumerate(copies):
+        copy.start(priority=b % 2)
     for copy in minor:
         copy.wait()
     n_x, n_core = lax.axis_size("x"), lax.axis_size("core")

time: 91.4 us -> 91.4 us (level)
  no operation moved by 1% of the time
where the time goes in v14:
time: 91.4 us; the launch traced here: 91.1 us
  blocking collectives  68.8 us (75%)
  Pallas kernels  12.9 us (14%)
  starting transfers between devices  7.73 us (8%)
    all_to_all x3, blocking collectives, to_owners(): got = lax.all_to_all(flat, ('scene', 'x'), 0, 0, tiled=True)  50.2 us
    all_to_all x2, blocking collectives, to_blocks(): return lax.all_to_all(message, 'scene', 0, 0, tiled=True)  18.6 us
    ppermute x3, starting transfers between devices, to_owners(): partner = lax.ppermute(own, 'core', [(0, 1), (1, 0)])  7.73 us
    pallas_call x1, Pallas kernels, local(): call(rhs_kernel, (wide, whole(jacobian.shape, BF16), whole((2 * n_blk, LA...  3.34 us
    pallas_call x3, Pallas kernels, to_owners(): call(functools.partial(sum_kernel, first), (sums,) + (extra if first else...  2.16 us
  transfers between devices with their start and end apart: 3, of which 2 were waited for; matrix products, arithmetic and copies ran while one was open for 0% of the time, Pallas kernels for 2%

profile of v14, /device:TPU:1, one launch (start us, length us, event | category | flops | bytes accessed | tf_op | source)
XLA Modules:
  0.0 91.1 jit_solution(15209774844068862366)
XLA Ops:
  0.6 3.3 %shard_map.86 = (f32[16,4,8,128]{3,2,1,0:T(8,128)S(1)}, bf16[8,256,1152]{2,1,0:T(8,128)(2,1)S(1)}, s32[16,128]{1,0:T(8,128)S(1)}) custom-call(s32[1,128]{1,0:T(1,128)} %bitcast.13, bf16[8,256,1152]{2,1,0:T(8,128)(2,1)} %jac.1, bf16[8,256]{1,0:T(8,128)(2,1)} %pix.1, s32[8,128]{1,0:T(8,128)} %ids.1), custom_call_target="tpu_custom_call" | custom-call | flops 1048576 | bytes 1048576 | tf_op jit(solution)/shard_map/pallas_call | solution.py:439
  4.0 0.0 copy-start
  4.0 21.4 %all_to_all.25 = f32[64,8,128]{2,1,0:T(8,128)S(1)} all-to-all(f32[64,8,128]{2,1,0:T(8,128)S(1)} %bitcast.9), channel_id=1, replica_groups=mesh['scene'=16,'x'=4,'core'=2] {'scene','x'}, dimensions={0} | all-to-all | bytes 524288 | tf_op jit(solution)/shard_map/all_to_all | solution.py:418
  25.4 0.9 shard_map.87
  26.3 2.1 %collective-permute-start = (f32[80,128]{1,0:T(8,128)S(1)}, f32[80,128]{1,0:T(8,128)S(1)}, u32[]{:S(2)}, u32[]{:S(2)}) collective-permute-start(f32[80,128]{1,0:T(8,128)S(1)} %get-tuple-element.23.after.own), channel_id=1, source_target_pairs={{0,1},{1,0},{2,3},{3,2},{4,5},{5,4},{6,7},{7,6},{8,9},{9,8},{10,11... | collective-permute-start | bytes 122888 | tf_op jit(solution)/shard_map/ppermute | solution.py:433
  28.4 1.2 %shard_map.88.matrix = f32[360,128]{1,0:T(8,128)S(1)} custom-call(f32[80,128]{1,0:T(8,128)S(1)} %get-tuple-element.23.after.own, bf16[9,59,1024]{2,1,0:T(8,128)(2,1)S(1)} %copy-done, f32[59,1024]{1,0:T(8,128)S(1)} %copy-done.2), custom_call_target="tpu_custom_call" | custom-call | flops 2147483648 | bytes 1048576 | tf_op jit(solution)/shard_map/pallas_call | solution.py:453
  29.7 0.3 shard_map.89
  29.9 9.3 %all_to_all.26.recv = f32[16,8,128]{2,1,0:T(8,128)S(1)} all-to-all(f32[16,8,128]{2,1,0:T(8,128)S(1)} %shard_map.89), channel_id=1, replica_groups=mesh['scene'=16,'x'=4,'core'=2] {'scene'}, dimensions={0} | all-to-all | bytes 131072 | tf_op jit(solution)/shard_map/all_to_all | solution.py:437
  39.2 1.7 %shard_map.90 = (f32[16,4,8,128]{3,2,1,0:T(8,128)S(1)}, f32[8,1152]{1,0:T(8,128)S(1)}) custom-call(bf16[8,256,1152]{2,1,0:T(8,128)(2,1)S(1)} %get-tuple-element.20.jac, s32[16,128]{1,0:T(8,128)S(1)} %get-tuple-element.21.aux, f32[16,8,128]{2,1,0:T(8,128)S(1)} %all_to_all.26.recv), custom_call_target="tpu_custom_call" | custom-call | flops 1048576 | bytes 1048576 | tf_op jit(solution)/shard_map/pallas_call | solution.py:461
  40.9 0.0 copy-start.1
  40.9 14.5 %all_to_all.27 = f32[64,8,128]{2,1,0:T(8,128)S(1)} all-to-all(f32[64,8,128]{2,1,0:T(8,128)S(1)} %bitcast.10), channel_id=1, replica_groups=mesh['scene'=16,'x'=4,'core'=2] {'scene','x'}, dimensions={0} | all-to-all | bytes 524288 | tf_op jit(solution)/shard_map/all_to_all | solution.py:418
  55.4 0.6 shard_map.91.after.own
  56.0 2.6 %collective-permute-start.1 = (f32[80,128]{1,0:T(8,128)S(1)}, f32[80,128]{1,0:T(8,128)S(1)}, u32[]{:S(2)}, u32[]{:S(2)}) collective-permute-start(f32[80,128]{1,0:T(8,128)S(1)} %shard_map.91.after.own), channel_id=1, source_target_pairs={{0,1},{1,0},{2,3},{3,2},{4,5},{5,4},{6,7},{7,6},{8,9},{9,8},{10,11... | collective-permute-start | bytes 122888 | tf_op jit(solution)/shard_map/ppermute | solution.py:433
  58.7 0.7 shard_map.92
  59.4 0.1 collective-permute-done.1.partner
  59.5 0.7 shard_map.93
  60.2 9.3 %all_to_all.28.recv = f32[16,8,128]{2,1,0:T(8,128)S(1)} all-to-all(f32[16,8,128]{2,1,0:T(8,128)S(1)} %get-tuple-element.30), channel_id=1, replica_groups=mesh['scene'=16,'x'=4,'core'=2] {'scene'}, dimensions={0} | all-to-all | bytes 131072 | tf_op jit(solution)/shard_map/all_to_all | solution.py:437
  69.5 1.8 %shard_map.94 = (f32[16,4,8,128]{3,2,1,0:T(8,128)S(1)}, f32[8,128]{1,0:T(8,128)S(1)}) custom-call(bf16[8,256,1152]{2,1,0:T(8,128)(2,1)S(1)} %get-tuple-element.20.jac, s32[16,128]{1,0:T(8,128)S(1)} %get-tuple-element.21.aux, f32[16,8,128]{2,1,0:T(8,128)S(1)} %all_to_all.28.recv, f32[8,1152]{1,0:T(8,128)S(1)} %get-tuple-element.31.picks_in), custom_call_target="tpu_custom_call" | custom-call | flops 1048576 | bytes 1048576 | tf_op jit(solution)/shard_map/pallas_call | solution.py:475
  71.3 14.4 %all_to_all.29 = f32[64,8,128]{2,1,0:T(8,128)S(1)} all-to-all(f32[64,8,128]{2,1,0:T(8,128)S(1)} %bitcast.7), channel_id=1, replica_groups=mesh['scene'=16,'x'=4,'core'=2] {'scene','x'}, dimensions={0} | all-to-all | bytes 524288 | tf_op jit(solution)/shard_map/all_to_all | solution.py:418
  85.6 0.6 shard_map.95.after.own
  86.3 2.9 %collective-permute-start.2 = (f32[80,128]{1,0:T(8,128)S(1)}, f32[80,128]{1,0:T(8,128)S(1)}, u32[]{:S(2)}, u32[]{:S(2)}) collective-permute-start(f32[80,128]{1,0:T(8,128)S(1)} %shard_map.95.after.own), channel_id=1, source_target_pairs={{0,1},{1,0},{2,3},{3,2},{4,5},{5,4},{6,7},{7,6},{8,9},{9,8},{10,11... | collective-permute-start | bytes 122888 | tf_op jit(solution)/shard_map/ppermute | solution.py:433
  89.2 0.1 shard_map.96
  89.3 0.8 collective-permute-done.2.partner
  90.1 1.0 %shard_map.97 = (f32[59,1024]{1,0:T(8,128)}, f32[59,1024]{1,0:T(8,128)}) custom-call(f32[80,128]{1,0:T(8,128)S(1)} %shard_map.95.after.own, f32[80,128]{1,0:T(8,128)S(1)} %collective-permute-done.2.partner, bf16[9,59,1024]{2,1,0:T(8,128)(2,1)S(1)} %copy-done, f32[59,1024]{1,0:T(8,128)S(1)} %copy-done.1, f32[8,128]{1,0:T(8,128)S(1)} %get-tuple-element.33.steps, ...), custom_call_target="tpu_custom_call" | custom-call | flops 1048576 | bytes 1048576 | tf_op jit(solution)/shard_map/pallas_call | solution.py:483
  (5 shorter events, 0.0 us)
Async XLA Ops:
  4.0 24.5 %copy-start = (bf16[9,59,1024]{2,1,0:T(8,128)(2,1)S(1)}, bf16[9,59,1024]{2,1,0:T(8,128)(2,1)}, u32[]{:S(2)}) copy-start(bf16[9,59,1024]{2,1,0:T(8,128)(2,1)} %proj.7) | copy-start | bytes 3262468
  4.0 24.4 %copy-start.2 = (f32[59,1024]{1,0:T(8,128)S(1)}, f32[59,1024]{1,0:T(8,128)}, u32[]{:S(2)}) copy-start(f32[59,1024]{1,0:T(8,128)} %precond.7) | copy-start | bytes 724996
  26.3 3.4 %collective-permute-start = (f32[80,128]{1,0:T(8,128)S(1)}, f32[80,128]{1,0:T(8,128)S(1)}, u32[]{:S(2)}, u32[]{:S(2)}) collective-permute-start(f32[80,128]{1,0:T(8,128)S(1)} %get-tuple-element.23.after.own), channel_id=1, source_target_pairs={{0,1},{1,0},{2,3},{3,2},{4,5},{5,4},{6,7},{7,6},{8,9},{9,8},{10,11... | collective-permute-start | bytes 122888 | tf_op jit(solution)/shard_map/ppermute | solution.py:433
  40.9 17.8 %copy-start.1 = (f32[59,1024]{1,0:T(8,128)S(1)}, f32[59,1024]{1,0:T(8,128)}, u32[]{:S(2)}) copy-start(f32[59,1024]{1,0:T(8,128)} %damping.5) | copy-start | bytes 724996
  56.0 3.5 %collective-permute-start.1 = (f32[80,128]{1,0:T(8,128)S(1)}, f32[80,128]{1,0:T(8,128)S(1)}, u32[]{:S(2)}, u32[]{:S(2)}) collective-permute-start(f32[80,128]{1,0:T(8,128)S(1)} %shard_map.91.after.own), channel_id=1, source_target_pairs={{0,1},{1,0},{2,3},{3,2},{4,5},{5,4},{6,7},{7,6},{8,9},{9,8},{10,11... | collective-permute-start | bytes 122888 | tf_op jit(solution)/shard_map/ppermute | solution.py:433
  86.3 3.8 %collective-permute-start.2 = (f32[80,128]{1,0:T(8,128)S(1)}, f32[80,128]{1,0:T(8,128)S(1)}, u32[]{:S(2)}, u32[]{:S(2)}) collective-permute-start(f32[80,128]{1,0:T(8,128)S(1)} %shard_map.95.after.own), channel_id=1, source_target_pairs={{0,1},{1,0},{2,3},{3,2},{4,5},{5,4},{6,7},{7,6},{8,9},{9,8},{10,11... | collective-permute-start | bytes 122888 | tf_op jit(solution)/shard_map/ppermute | solution.py:433
